TPU v7x, 256 devices: a whole 4x4x8 slice. The times are simulated.
256 devices in a mesh: gz: 8 (over z), gx: 4 (over x), gy: 8 (over y, core).
Axes of the slice: x: 4, y: 4, z: 8, core: 2. Of those that a mesh axis runs over, the one named last changes fastest.
Arguments:
- density: float32 [256, 1024, 1024], P('gz', 'gy', 'gx'), may hold values from 0 to 1
- mask: int32 [32, 128, 128], P('gz', 'gy', 'gx'), may hold values from 0 to 3
Outputs:
- filtered: float32 [256, 1024, 1024], P(('gz', 'gx'), 'gy')
- projected: float32 [256, 1024, 1024], P(('gz', 'gx'), 'gy')
Inputs may be any that keep to these rules, and one draw needn't show every extreme that they name: `mask`: code 0 marks a void block, 1 a solid block, 2 and 3 design blocks.
All inputs are finite; a program needn't handle non-finite values.
Results may differ from a plain program's by a relative error of at most 0.0003.
Values sent between devices are 32-bit elements; how exact they have to be, the bound alone decides.
No kernel may reach another device: no remote copies, remote signals or barrier semaphores. Data moves between devices by JAX's collectives and lax.ppermute only.
A program may use at most 128 MiB of HBM per device.

v0:
```python
import jax
import jax.numpy as jnp
from jax import lax
from jax.sharding import PartitionSpec as P

RADIUS = 6
CELLS = 8


sharpness = 8.0
threshold = 0.5
highest = lax.Precision.HIGHEST


def with_halo(x, sides, width):
    for axis, dim in sides:
        peers, length = (lax.axis_size(axis), x.shape[dim])
        up = [(i, (i + 1) % peers) for i in range(peers - 1)]
        down = [(j, i) for i, j in up]
        last = lax.slice_in_dim(x, length - width, length, axis=dim)
        leading = lax.slice_in_dim(x, 0, width, axis=dim)
        before = lax.ppermute(last, axis, up)
        after = lax.ppermute(leading, axis, down)
        x = jnp.concatenate([before, x, after], axis=dim)
    return x


def passed_along(block, axis, distance):
    devices = range(lax.axis_size(axis))
    route = [(i - distance, i) for i in devices if i - distance in devices]
    return lax.ppermute(block, axis, route)


def band(outputs, inputs, shift):
    out_index = lax.broadcasted_iota(jnp.int32, (outputs, inputs), 0)
    in_index = lax.broadcasted_iota(jnp.int32, (outputs, inputs), 1)
    distance = jnp.abs(in_index + shift - out_index)
    return jnp.where(distance <= RADIUS, (RADIUS + 1 - distance).astype(jnp.float32), 0.0)


def along_first(extended, count):
    kernel = band(count, count + 2 * RADIUS, -RADIUS)
    flat = extended.reshape(count + 2 * RADIUS, -1)
    result = jnp.dot(kernel, flat, precision=highest, preferred_element_type=jnp.float32)
    return result.reshape((count,) + extended.shape[1:])


def filter_last(values):
    leading = values.shape[:-1]
    extent = values.shape[-1]
    blocks = extent // 128
    widths = [(0, 0)] * (values.ndim - 1) + [(RADIUS, 128 - RADIUS)]
    padded = jnp.pad(values, widths)
    lower_part = padded[..., :extent].reshape(leading + (blocks, 128))
    upper_part = padded[..., 128 : extent + 128].reshape(leading + (blocks, 128))[..., : 2 * RADIUS]
    lower_kernel = band(128, 128, -RADIUS).T
    upper_kernel = band(128, 2 * RADIUS, 128 - RADIUS).T
    result = jnp.einsum(
        "abcd,de->abce",
        lower_part,
        lower_kernel,
        precision=highest,
        preferred_element_type=jnp.float32,
    )
    result = result + jnp.einsum(
        "abcd,de->abce",
        upper_part,
        upper_kernel,
        precision=highest,
        preferred_element_type=jnp.float32,
    )
    return result.reshape(leading + (extent,))


def one_side(reach):
    return reach * (RADIUS + 1) - reach * (reach + 1) // 2


def edge_sums(start, length, length_all):
    position = start + lax.iota(jnp.int32, length)
    reach_left = jnp.minimum(position, RADIUS)
    reach_right = jnp.minimum(length_all - 1 - position, RADIUS)
    return (RADIUS + 1 + one_side(reach_left) + one_side(reach_right)).astype(jnp.float32)


def body(density, mask):
    planes, row_count, columns = density.shape
    design_code = jnp.repeat(jnp.repeat(jnp.repeat(mask, CELLS, 0), CELLS, 1), CELLS, 2)
    physical = jnp.where(design_code == 0, 0.0, jnp.where(design_code == 1, 1.0, density))
    extended = with_halo(physical, (("gz", 0),), RADIUS)
    physical = along_first(extended, planes)
    groups = lax.axis_size("gx")
    layers = planes // groups
    smoothed = filter_last(lax.all_to_all(physical, "gx", split_axis=0, concat_axis=2, tiled=True))
    row_kernel = band(row_count + 2 * RADIUS, row_count, RADIUS)
    partial_value = jnp.einsum(
        "wy,zyx->zwx", row_kernel, smoothed, precision=highest, preferred_element_type=jnp.float32
    )
    from_previous = passed_along(partial_value[:, row_count + RADIUS :], "gy", 1)
    from_next = passed_along(partial_value[:, :RADIUS], "gy", -1)
    summed = partial_value[:, RADIUS : row_count + RADIUS]
    summed = summed.at[:, :RADIUS].add(from_previous)
    summed = summed.at[:, row_count - RADIUS :].add(from_next)
    width_all = summed.shape[2]
    count_x = edge_sums(0, width_all, width_all)
    count_y = edge_sums(
        lax.axis_index("gy") * row_count, row_count, row_count * lax.axis_size("gy")
    )
    count_z = edge_sums(lax.axis_index(("gz", "gx")) * layers, layers, planes * lax.axis_size("gz"))
    counts = count_z[:, None, None] * count_y[None, :, None] * count_x[None, None, :]
    filtered = summed / counts
    top = jnp.tanh(sharpness * threshold)
    projected = (top + jnp.tanh(sharpness * (filtered - threshold))) / (
        top + jnp.tanh(sharpness * (1.0 - threshold))
    )
    return (filtered, projected)


def solution(mesh):
    placed = (P("gz", "gy", "gx"), P("gz", "gy", "gx"))
    return jax.shard_map(
        body,
        mesh=mesh,
        in_specs=placed,
        out_specs=(P(("gz", "gx"), "gy", None), P(("gz", "gx"), "gy", None)),
        check_vma=False,
    )
```

profile of v0, /device:TPU:105, one launch (start us, length us, event | category | flops | bytes accessed | tf_op | source)
XLA Modules:
  0.0 161.5 jit_solution(7597884732722517777)
XLA Ops:
  0.6 0.8 broadcast_compare_fusion.1
  1.4 0.3 broadcast_bitcast_fusion.1
  1.7 0.6 copy.28
  2.4 0.3 broadcast_bitcast_fusion
  2.7 0.6 copy.29
  3.4 5.6 %copy.30 = f32[32,128,256]{1,2,0:T(8,128)} copy(f32[32,128,256]{2,1,0:T(8,128)} %param.6) | data formatting | bytes 8388608 | tf_op args[0]
  8.9 3.2 %select_select_fusion = f32[32,128,256]{1,2,0:T(8,128)S(1)} fusion(f32[32,128,256]{1,2,0:T(8,128)} %copy.30, pred[32,128,32]{1,2,0:T(8,128)(4,1)S(1)} %copy.29, pred[32,128,32]{1,2,0:T(8,128)(4,1)S(1)} %copy.28), kind=kLoop, calls=%fused_computation.8 | loop fusion | flops 2097152 | bytes 8650752 | tf_op jit(solution)/shard_map/jit(_where)/select_n | solution.py:89
  12.2 0.1 fusion.79
  12.3 4.8 %collective-permute-start = (f32[6,128,256]{1,2,0:T(8,128)S(1)}, f32[6,128,256]{1,2,0:T(8,128)S(1)}, u32[]{:S(2)}, u32[]{:S(2)}) collective-permute-start(f32[6,128,256]{1,2,0:T(8,128)S(1)} %get-tuple-element.32), channel_id=1, source_target_pairs={{0,32},{32,64},{64,96},{96,128},{128,160},{160,192},{192,224},{1,3... | collective-permute-start | bytes 2359304 | tf_op jit(solution)/shard_map/ppermute | solution.py:22
  17.1 2.1 %collective-permute-start.1 = (f32[6,128,256]{1,2,0:T(8,128)S(1)}, f32[6,128,256]{1,2,0:T(8,128)S(1)}, u32[]{:S(2)}, u32[]{:S(2)}) collective-permute-start(f32[6,128,256]{1,2,0:T(8,128)S(1)} %get-tuple-element.33), channel_id=1, source_target_pairs={{32,0},{64,32},{96,64},{128,96},{160,128},{192,160},{224,192},{33,... | collective-permute-start | bytes 2359304 | tf_op jit(solution)/shard_map/ppermute | solution.py:23
  19.2 14.1 %collective-permute-done = f32[6,128,256]{1,2,0:T(8,128)S(1)} collective-permute-done((f32[6,128,256]{1,2,0:T(8,128)S(1)}, f32[6,128,256]{1,2,0:T(8,128)S(1)}, u32[]{:S(2)}, u32[]{:S(2)}) %collective-permute-start) | collective-permute-done | bytes 786464 | tf_op jit(solution)/shard_map/ppermute | solution.py:22
  33.3 5.0 %collective-permute-done.1 = f32[6,128,256]{1,2,0:T(8,128)S(1)} collective-permute-done((f32[6,128,256]{1,2,0:T(8,128)S(1)}, f32[6,128,256]{1,2,0:T(8,128)S(1)}, u32[]{:S(2)}, u32[]{:S(2)}) %collective-permute-start.1) | collective-permute-done | bytes 786464 | tf_op jit(solution)/shard_map/ppermute | solution.py:23
  38.3 2.9 %pad_maximum_fusion = f32[44,128,256]{1,2,0:T(8,128)} fusion(f32[6,128,256]{1,2,0:T(8,128)S(1)} %collective-permute-done.1, f32[32,128,256]{1,2,0:T(8,128)S(1)} %select_select_fusion, f32[6,128,256]{1,2,0:T(8,128)S(1)} %collective-permute-done), kind=kLoop, calls=%fused_computation.3 | loop fusion | flops 2883584 | bytes 11534336 | tf_op jit(solution)/shard_map/concatenate | solution.py:24
  41.2 6.3 %copy.31 = f32[44,128,256]{2,1,0:T(8,128)} copy(f32[44,128,256]{1,2,0:T(8,128)} %pad_maximum_fusion) | data formatting | bytes 11534336 | tf_op jit(solution)/shard_map/concatenate | solution.py:24
  47.5 3.3 %slice_bitcast_fusion = f32[128,256,44]{1,0,2:T(8,128)S(1)} fusion(f32[44,128,256]{2,1,0:T(8,128)} %copy.31), kind=kLoop, calls=%fused_computation.2 | loop fusion | bytes 11534336 | tf_op jit(solution)/shard_map/dot_general | solution.py:44
  50.8 7.3 %fusion = f32[32,128,256]{2,0,1:T(8,128)S(1)} fusion(f32[128,256,44]{1,0,2:T(8,128)S(1)} %slice_bitcast_fusion, s32[44]{0:T(128)S(1)} %iota_add_fusion.3), kind=kOutput, calls=%fused_computation | convolution fusion | flops 553656576 | bytes 9961648 | tf_op jit(solution)/shard_map/dot_general | solution.py:44
  58.1 4.4 %copy.33 = f32[32,128,256]{2,1,0:T(8,128)} copy(f32[32,128,256]{2,0,1:T(8,128)S(1)} %fusion) | data formatting | bytes 8388608 | tf_op jit(solution)/shard_map/dot_general | solution.py:44
  62.6 4.8 %all-to-all-start = ((f32[32,128,256]{2,1,0:T(8,128)}), f32[32,128,256]{2,1,0:T(8,128)}, u32[]{:S(2)}, u32[]{:S(2)}) async-start(f32[32,128,256]{2,1,0:T(8,128)} %copy.33), calls=%async_computation | async-start | bytes 8388608 | tf_op jit(solution)/shard_map/all_to_all | solution.py:94
  67.5 47.0 %all-to-all-done = f32[32,128,256]{2,1,0:T(8,128)} async-done(((f32[32,128,256]{2,1,0:T(8,128)}), f32[32,128,256]{2,1,0:T(8,128)}, u32[]{:S(2)}, u32[]{:S(2)}) %all-to-all-start) | async-done | bytes 4194336 | tf_op jit(solution)/shard_map/all_to_all | solution.py:94
  114.6 5.3 %copy.34 = f32[8,128,4,256]{1,3,2,0:T(8,128)} copy(f32[8,128,4,256]{3,1,0,2:T(8,128)} %bitcast.9) | data formatting | bytes 8388608 | tf_op jit(solution)/shard_map/all_to_all | solution.py:94
  119.9 4.2 %pad_slice_fusion.1 = (f32[8,128,1024]{1,2,0:T(8,128)S(1)}, f32[8,128,1024]{1,2,0:T(8,128)S(1)}) fusion(f32[8,128,1024]{1,2,0:T(8,128)} %bitcast.50), kind=kLoop, calls=%fused_computation.5 | loop fusion | bytes 12582912 | tf_op jit(solution)/shard_map/slice | solution.py:54
  124.0 3.5 %fusion.2 = f32[8,128,8,128]{1,3,2,0:T(8,128)S(1)} fusion(f32[8,128,8,128]{1,3,2,0:T(8,128)S(1)} %bitcast.52, s32[12]{0:T(128)S(1)} %iota_add_fusion.1), kind=kOutput, calls=%fused_computation.13 | convolution fusion | flops 151004160 | bytes 4719104 | tf_op jit(solution)/shard_map/abcd,de->abce/dot_general | solution.py:65
  127.6 3.9 %convolution_add_fusion = f32[8,128,8,128]{1,3,2,0:T(8,128)S(1)} fusion(f32[8,128,8,128]{1,3,2,0:T(8,128)S(1)} %fusion.2, f32[8,128,8,128]{1,3,2,0:T(8,128)S(1)} %bitcast.49, s32[128]{0:T(128)S(1)} %iota_add_fusion.2), kind=kOutput, calls=%fused_computation.10 | convolution fusion | flops 1611759616 | bytes 12583424 | tf_op jit(solution)/shard_map/abcd,de->abce/dot_general | solution.py:58
  131.5 4.4 %convolution_bitcast_fusion = f32[8,140,1024]{2,1,0:T(8,128)S(1)} fusion(f32[8,128,1024]{1,2,0:T(8,128)S(1)} %bitcast.51, s32[128]{0:T(128)S(1)} %iota_add_fusion), kind=kOutput, calls=%fused_computation.9 | convolution fusion | flops 1761715200 | bytes 8782336 | tf_op jit(solution)/shard_map/wy,zyx->zwx/dot_general | solution.py:96
  135.9 5.8 %collective-permute-start.2 = (f32[8,6,1024]{2,1,0:T(8,128)S(1)}, f32[8,6,1024]{2,1,0:T(8,128)S(1)}, u32[]{:S(2)}, u32[]{:S(2)}) collective-permute-start(f32[8,6,1024]{2,1,0:T(8,128)S(1)} %get-tuple-element.29), channel_id=1, source_target_pairs={{0,1},{1,2},{2,3},{3,4},{4,5},{5,6},{6,7},{8,9},{9,10},{10,11},{11... | collective-permute-start | bytes 589832 | tf_op jit(solution)/shard_map/ppermute | solution.py:31
  141.8 2.5 %slice.86 = f32[8,128,1024]{2,1,0:T(8,128)} slice(f32[8,140,1024]{2,1,0:T(8,128)S(1)} %convolution_bitcast_fusion), slice={[0:8], [6:134], [0:1024]} | slice | bytes 8388608 | tf_op jit(solution)/shard_map/slice | solution.py:101
  144.3 1.9 %collective-permute-start.3 = (f32[8,6,1024]{2,1,0:T(8,128)S(1)}, f32[8,6,1024]{2,1,0:T(8,128)S(1)}, u32[]{:S(2)}, u32[]{:S(2)}) collective-permute-start(f32[8,6,1024]{2,1,0:T(8,128)S(1)} %get-tuple-element.28), channel_id=1, source_target_pairs={{1,0},{2,1},{3,2},{4,3},{5,4},{6,5},{7,6},{9,8},{10,9},{11,10},{12... | collective-permute-start | bytes 589832 | tf_op jit(solution)/shard_map/ppermute | solution.py:31
  146.3 1.8 %scatter-add.6 = f32[8,128,1024]{2,1,0:T(8,128)} dynamic-update-slice(f32[8,128,1024]{2,1,0:T(8,128)} %slice.86, f32[8,6,1024]{2,1,0:T(8,128)S(1)} %slice_add_fusion.1, s32[]{:T(128)} %constant.154.clone.1, s32[]{:T(128)} %constant.154.clone.1, s32[]{:T(128)} %constant.154.clone.1) | dynamic-update-slice | bytes 393220 | tf_op jit(solution)/shard_map/scatter-add | solution.py:102
  148.1 3.9 %collective-permute-done.3 = f32[8,6,1024]{2,1,0:T(8,128)S(1)} collective-permute-done((f32[8,6,1024]{2,1,0:T(8,128)S(1)}, f32[8,6,1024]{2,1,0:T(8,128)S(1)}, u32[]{:S(2)}, u32[]{:S(2)}) %collective-permute-start.3) | collective-permute-done | bytes 196640 | tf_op jit(solution)/shard_map/ppermute | solution.py:31
  152.0 1.0 slice_add_fusion
  153.0 1.7 %scatter-add.9 = f32[8,128,1024]{2,1,0:T(8,128)} dynamic-update-slice(f32[8,128,1024]{2,1,0:T(8,128)} %scatter-add.6, f32[8,6,1024]{2,1,0:T(8,128)S(1)} %slice_add_fusion, s32[]{:T(128)} %constant.154.clone.1, s32[]{:T(128)} %constant.157.clone.1, s32[]{:T(128)} %constant.154.clone.1) | dynamic-update-slice | bytes 393220 | tf_op jit(solution)/shard_map/scatter-add | solution.py:103
  154.7 6.8 %add_multiply_fusion = (f32[8,128,1024]{2,1,0:T(8,128)}, f32[8,128,1024]{2,1,0:T(8,128)}) fusion(f32[8,128,1024]{2,1,0:T(8,128)} %scatter-add.9, f32[1024]{0:T(1024)S(1)} %fusion.49, f32[8,128]{1,0:T(8,128)S(1)} %broadcast_multiply_fusion), kind=kLoop, calls=%fused_computation.6 | loop fusion | flops 6291456 | bytes 12591104 | tf_op jit(solution)/shard_map/div | solution.py:113
  (13 shorter events, 0.3 us)
Async XLA Ops:
  12.3 21.0 %collective-permute-start = (f32[6,128,256]{1,2,0:T(8,128)S(1)}, f32[6,128,256]{1,2,0:T(8,128)S(1)}, u32[]{:S(2)}, u32[]{:S(2)}) collective-permute-start(f32[6,128,256]{1,2,0:T(8,128)S(1)} %get-tuple-element.32), channel_id=1, source_target_pairs={{0,32},{32,64},{64,96},{96,128},{128,160},{160,192},{192,224},{1,3... | collective-permute-start | bytes 2359304 | tf_op jit(solution)/shard_map/ppermute | solution.py:22
  17.1 21.3 %collective-permute-start.1 = (f32[6,128,256]{1,2,0:T(8,128)S(1)}, f32[6,128,256]{1,2,0:T(8,128)S(1)}, u32[]{:S(2)}, u32[]{:S(2)}) collective-permute-start(f32[6,128,256]{1,2,0:T(8,128)S(1)} %get-tuple-element.33), channel_id=1, source_target_pairs={{32,0},{64,32},{96,64},{128,96},{160,128},{192,160},{224,192},{33,... | collective-permute-start | bytes 2359304 | tf_op jit(solution)/shard_map/ppermute | solution.py:23
  62.6 52.0 %all-to-all-start = ((f32[32,128,256]{2,1,0:T(8,128)}), f32[32,128,256]{2,1,0:T(8,128)}, u32[]{:S(2)}, u32[]{:S(2)}) async-start(f32[32,128,256]{2,1,0:T(8,128)} %copy.33), calls=%async_computation | async-start | bytes 8388608 | tf_op jit(solution)/shard_map/all_to_all | solution.py:94
  135.9 10.3 %collective-permute-start.2 = (f32[8,6,1024]{2,1,0:T(8,128)S(1)}, f32[8,6,1024]{2,1,0:T(8,128)S(1)}, u32[]{:S(2)}, u32[]{:S(2)}) collective-permute-start(f32[8,6,1024]{2,1,0:T(8,128)S(1)} %get-tuple-element.29), channel_id=1, source_target_pairs={{0,1},{1,2},{2,3},{3,4},{4,5},{5,6},{6,7},{8,9},{9,10},{10,11},{11... | collective-permute-start | bytes 589832 | tf_op jit(solution)/shard_map/ppermute | solution.py:31
  144.3 7.7 %collective-permute-start.3 = (f32[8,6,1024]{2,1,0:T(8,128)S(1)}, f32[8,6,1024]{2,1,0:T(8,128)S(1)}, u32[]{:S(2)}, u32[]{:S(2)}) collective-permute-start(f32[8,6,1024]{2,1,0:T(8,128)S(1)} %get-tuple-element.28), channel_id=1, source_target_pairs={{1,0},{2,1},{3,2},{4,3},{5,4},{6,5},{7,6},{9,8},{10,9},{11,10},{12... | collective-permute-start | bytes 589832 | tf_op jit(solution)/shard_map/ppermute | solution.py:31
where the time goes:
time: 162 us; the launch traced here: 161 us
  waiting for transfers between devices  70.1 us (43%)
  local copies, waits for them, and re-layouts  37.2 us (23%)
  starting transfers between devices  19.4 us (12%)
  matrix products  19.1 us (12%)
  other arithmetic  14.8 us (9%)
    all_to_all x1, waiting for transfers between devices, body(): lax.all_to_all(physical, 'gx', split_axis=0, concat_axis=2, tiled=True)  47 us
    ppermute x1, waiting for transfers between devices, with_halo(): before = lax.ppermute(last, axis, up)  14.1 us
    dot_general x2, local copies, waits for them, and re-layouts, along_first(): jnp.dot(kernel, flat, precision=highest, preferred_element_type=jnp.float32)  7.74 us
    ppermute x2, starting transfers between devices, passed_along(): return lax.ppermute(block, axis, route)  7.67 us
    dot_general x1, matrix products, along_first(): jnp.dot(kernel, flat, precision=highest, preferred_element_type=jnp.float32)  7.32 us
    div x1, other arithmetic, body(): (top + jnp.tanh(sharpness * (filtered - threshold))) / (top + jnp.tanh(sh...  6.76 us
    concatenate x1, local copies, waits for them, and re-layouts, with_halo(): x = jnp.concatenate([before, x, after], axis=dim)  6.28 us
    unnamed x1, local copies, waits for them, and re-layouts  5.57 us
  transfers between devices with their start and end apart: 5, of which 4 were waited for; matrix products, arithmetic and copies ran while one was open for 3% of the time, Pallas kernels for 0%

commit v1 on v0

v1 whole, which is shorter than its diff:
```python
import functools

import jax
import jax.numpy as jnp
from jax import lax
from jax.experimental import pallas as pl
from jax.experimental.pallas import tpu as pltpu
from jax.sharding import PartitionSpec as P


RADIUS = 6
CELLS = 8
EDGE = 8
BOX = RADIUS + 1

sharpness = 8.0
threshold = 0.5


STAGES = (2, 2, 4)


def first_of(stage):
    return sum(STAGES[:stage])


def plane_offset(stage, quarter):
    ascending = first_of(stage)
    descending = sum(STAGES) - ascending - STAGES[stage]
    return jnp.where(quarter == 0, descending, ascending)


def hat(shape, shift):
    out_index = lax.broadcasted_iota(jnp.int32, shape, 0)
    in_index = lax.broadcasted_iota(jnp.int32, shape, 1)
    distance = jnp.abs(in_index + shift - out_index)
    return jnp.maximum(BOX - distance, 0)


def two_parts(values):
    high = values.astype(jnp.bfloat16)
    low = (values - high.astype(jnp.float32)).astype(jnp.bfloat16)
    return high, low


def along_rows(kernel, values):
    high, low = two_parts(values)
    return jnp.dot(kernel, high, preferred_element_type=jnp.float32) + jnp.dot(
        kernel, low, preferred_element_type=jnp.float32
    )


def vmem(count):
    return [pl.BlockSpec(memory_space=pltpu.VMEM)] * count


def params(mib):
    return pltpu.CompilerParams(vmem_limit_bytes=mib * 1024 * 1024)


def cost(flops):
    return pl.CostEstimate(flops=flops, bytes_accessed=8 * 1024 * 1024, transcendentals=0)


def section_kernel(density, mask, conv, first_rows, last_rows, *rest):
    sends, codes = rest[:4], rest[4]
    planes, rows, columns = density.shape
    blocks = rows // CELLS
    table = mask[...].reshape(planes // CELLS * blocks, columns // CELLS)
    spread = (
        lax.broadcasted_iota(jnp.int32, (columns // CELLS, columns), 1) // CELLS
        == lax.broadcasted_iota(jnp.int32, (columns // CELLS, columns), 0)
    )
    codes[...] = jnp.dot(
        table.astype(jnp.float32).astype(jnp.bfloat16),
        spread.astype(jnp.float32).astype(jnp.bfloat16),
        preferred_element_type=jnp.float32,
    )

    def tile(i, carry):
        row = pl.ds(pl.multiple_of(i * CELLS, CELLS), CELLS)
        values, boxes = [], []
        box = total = None
        for z in range(planes + 2 * RADIUS):
            if z < planes:
                if z % CELLS == 0:
                    code = jnp.broadcast_to(
                        codes[pl.ds(z // CELLS * blocks + i, 1), :], (CELLS, columns)
                    )
                    void, solid = code < 0.5, code < 1.5
                value = jnp.where(void, 0.0, jnp.where(solid, 1.0, density[z, row, :]))
                values.append(value)
                box = value if box is None else box + value
            if z < planes + RADIUS:
                if z >= BOX:
                    box = box - values[z - BOX]
                boxes.append(box)
                total = box if total is None else total + box
            if z >= BOX:
                total = total - boxes[z - BOX]
            conv[z, row, :] = total
        return carry

    lax.fori_loop(0, blocks, tile, 0)
    first_rows[...] = conv[:, :EDGE, :]
    last_rows[...] = conv[:, rows - EDGE :, :]
    kernel = hat((rows - 2 * EDGE, rows), -EDGE).astype(jnp.float32).astype(jnp.bfloat16)
    me = lax.axis_index("gx")
    for distance in range(4):
        quarter = lax.rem(me + distance, 4)
        base = RADIUS + 8 * quarter + plane_offset(0, quarter)
        for j in range(STAGES[0]):
            sends[distance][j] = along_rows(kernel, conv[base + j])


def section(density, mask):
    planes, rows, columns = density.shape
    span = planes + 2 * RADIUS
    f32 = functools.partial(jax.ShapeDtypeStruct, dtype=jnp.float32)
    return pl.pallas_call(
        section_kernel,
        out_shape=[
            f32((span, rows, columns)),
            f32((span, EDGE, columns)),
            f32((span, EDGE, columns)),
        ]
        + [f32((STAGES[0], rows - 2 * EDGE, columns))] * 4,
        in_specs=vmem(2),
        out_specs=vmem(7),
        scratch_shapes=[pltpu.VMEM((planes // CELLS * rows // CELLS, columns), jnp.float32)],
        compiler_params=params(24),
        cost_estimate=cost(40_000_000),
        name="section",
    )(density, mask)


def edges_kernel(conv, before, after, *outs):
    planes = conv.shape[0] - 2 * RADIUS
    rows = conv.shape[1]
    up = planes + RADIUS
    starts = []
    for stage in range(1, len(STAGES)):
        first = first_of(stage) - STAGES[0]
        starts.append((up + RADIUS - first - STAGES[stage], first))
    for k, (higher, lower) in enumerate(starts):
        for out, start in ((outs[2 * k], higher), (outs[2 * k + 1], lower)):
            count = out.shape[0]
            out[:, :EDGE, :] = before[start : start + count]
            out[:, EDGE : EDGE + rows, :] = conv[start : start + count]
            out[:, EDGE + rows :, :] = after[start : start + count]


def edges(conv, before, after):
    rows, columns = conv.shape[1:]
    shapes = []
    for stage in range(1, len(STAGES)):
        shapes += [
            jax.ShapeDtypeStruct((STAGES[stage], rows + 2 * EDGE, columns), jnp.float32)
        ] * 2
    return pl.pallas_call(
        edges_kernel,
        out_shape=shapes,
        in_specs=vmem(3),
        out_specs=vmem(len(shapes)),
        compiler_params=params(16),
        cost_estimate=cost(5_000_000),
        name="edges",
    )(conv, before, after)


def stage_kernel(stage, conv, before, after, lower, upper, *sends):
    rows = conv.shape[1]
    count = STAGES[stage]
    kernel = hat((rows, rows + 2 * EDGE), -EDGE).astype(jnp.float32).astype(jnp.bfloat16)
    side = 3 * EDGE
    out_row = lax.broadcasted_iota(jnp.int32, (2 * EDGE, 2 * side), 0)
    in_row = lax.broadcasted_iota(jnp.int32, (2 * EDGE, 2 * side), 1)
    out_last, in_last = out_row >= EDGE, in_row >= side
    distance = jnp.abs(
        (in_row - jnp.where(in_last, side + EDGE, 0))
        - (out_row - jnp.where(out_last, EDGE, 0))
        - jnp.where(in_last, 0, EDGE)
    )
    corner = jnp.where(out_last == in_last, jnp.maximum(BOX - distance, 0), 0)
    corner = corner.astype(jnp.float32).astype(jnp.bfloat16)
    me = lax.axis_index("gx")
    for d in range(4):
        quarter = lax.rem(me + d, 4)
        take_lower = (quarter == 0).astype(jnp.float32)
        take_upper = (quarter == 3).astype(jnp.float32)
        base = RADIUS + 8 * quarter + plane_offset(stage, quarter)
        for j in range(count):
            plane = jnp.concatenate([before[base + j], conv[base + j], after[base + j]], axis=0)
            plane = plane + take_lower * lower[j] + take_upper * upper[j]
            sends[d][j * rows : (j + 1) * rows, :] = along_rows(kernel, plane)
        if stage == 1:
            base = RADIUS + 8 * quarter + plane_offset(0, quarter)
            for j in range(STAGES[0]):
                part = jnp.concatenate(
                    [
                        before[base + j],
                        conv[base + j, : 2 * EDGE, :],
                        conv[base + j, rows - 2 * EDGE :, :],
                        after[base + j],
                    ],
                    axis=0,
                )
                at = count * rows + j * 2 * EDGE
                sends[d][at : at + 2 * EDGE, :] = along_rows(corner, part)


def stage_sends(stage, conv, before, after, lower, upper):
    rows, columns = conv.shape[1:]
    total = STAGES[stage] * rows + (STAGES[0] * 2 * EDGE if stage == 1 else 0)
    return pl.pallas_call(
        functools.partial(stage_kernel, stage),
        out_shape=[jax.ShapeDtypeStruct((total, columns), jnp.float32)] * 4,
        in_specs=vmem(5),
        out_specs=vmem(4),
        compiler_params=params(20),
        cost_estimate=cost(40_000_000),
    )(conv, before, after, lower, upper)


def finish_kernel(stage, *refs):
    aliased = 0 if stage == 0 else 2
    scale, plane_scale, own, up, across, down = refs[:6]
    filtered, projected = refs[6 + aliased : 8 + aliased]
    smooth, sharp, sem = refs[8 + aliased :]
    columns = own.shape[-1]
    half = columns // 2
    me = lax.axis_index("gx")
    center = hat((columns, columns), 0)
    row = lax.broadcasted_iota(jnp.int32, (columns, columns), 0)
    column = lax.broadcasted_iota(jnp.int32, (columns, columns), 1)
    place = jnp.where(row < half, row - half, row + half)
    outer = jnp.maximum(BOX - jnp.abs(place - column), 0)
    weights = jnp.concatenate([center, center, outer, outer], axis=0)
    weights = weights.astype(jnp.float32).astype(jnp.bfloat16)
    top = jnp.tanh(jnp.float32(sharpness * threshold))
    inverse = 1.0 / (top + jnp.tanh(jnp.float32(sharpness * (1.0 - threshold))))

    sources = [up, own, down, across]

    def rows_of(take, put_rows, scale_rows, plane_factor):
        values = [take(source) for source in sources]
        for r in range(4):
            block = lax.rem(me + 3 + r, 4)
            has_before = (block != 0).astype(jnp.float32)
            has_after = (block != 3).astype(jnp.float32)
            outer_values = jnp.concatenate(
                [
                    values[(r + 3) % 4][:, half:] * has_before,
                    values[(r + 1) % 4][:, :half] * has_after,
                ],
                axis=1,
            )
            parts = two_parts(values[r]) + two_parts(outer_values)
            summed = jnp.dot(
                jnp.concatenate(parts, axis=1), weights, preferred_element_type=jnp.float32
            )
            lanes = pl.ds(pl.multiple_of(block * columns, columns), columns)
            smoothed = summed * (scale[scale_rows, lanes] * plane_factor)
            smooth[put_rows, lanes] = smoothed
            sharp[put_rows, lanes] = (
                top + jnp.tanh(sharpness * (smoothed - threshold))
            ) * inverse

    copies = []

    def send(buffer_rows, plane, rows):
        for source, target in ((smooth, filtered), (sharp, projected)):
            copy = pltpu.make_async_copy(
                source.at[buffer_rows, :], target.at[plane, rows, :], sem.at[len(copies)]
            )
            copy.start()
            copies.append(copy)

    offset = plane_offset(stage, me)
    rows = scale.shape[0]
    if stage == 0:
        inner = rows - 2 * EDGE
        for j in range(STAGES[0]):
            here = slice(j * inner, (j + 1) * inner)
            rows_of(lambda s: s[j], here, slice(EDGE, rows - EDGE), plane_scale[offset + j])
            send(pl.ds(j * inner, inner), offset + j, pl.ds(EDGE, inner))
    else:
        for j in range(STAGES[stage]):
            here = slice(j * rows, (j + 1) * rows)
            rows_of(lambda s: s[here, :], here, slice(0, rows), plane_scale[offset + j])
            send(pl.ds(j * rows, rows), offset + j, pl.ds(0, rows))
    if stage == 1:
        first = plane_offset(0, me)
        at = STAGES[stage] * rows
        for j in range(STAGES[0]):
            for put in (0, rows - EDGE):
                here = slice(at, at + EDGE)
                rows_of(
                    lambda s: s[here, :], here, slice(put, put + EDGE), plane_scale[first + j]
                )
                send(pl.ds(at, EDGE), first + j, pl.ds(put, EDGE))
                at += EDGE
    for copy in copies:
        copy.wait()


def finish(stage, scale, plane_scale, received, results):
    rows, width = scale.shape
    whole = jax.ShapeDtypeStruct((plane_scale.shape[0], rows, width), jnp.float32)
    count = received[0].size // received[0].shape[-1]
    copies = 2 * STAGES[stage] + (4 * STAGES[0] if stage == 1 else 0)
    return pl.pallas_call(
        functools.partial(finish_kernel, stage),
        out_shape=[whole, whole],
        in_specs=[
            pl.BlockSpec(memory_space=pltpu.VMEM),
            pl.BlockSpec(memory_space=pltpu.SMEM),
        ]
        + vmem(4)
        + [pl.BlockSpec(memory_space=pl.ANY)] * len(results),
        out_specs=[pl.BlockSpec(memory_space=pl.ANY)] * 2,
        scratch_shapes=[
            pltpu.VMEM((count, width), jnp.float32),
            pltpu.VMEM((count, width), jnp.float32),
            pltpu.SemaphoreType.DMA((copies,)),
        ],
        input_output_aliases={6: 0, 7: 1} if results else {},
        compiler_params=params(20),
        cost_estimate=cost(40_000_000),
    )(scale, plane_scale, *received, *results)


def one_side(reach):
    return reach * (RADIUS + 1) - reach * (reach + 1) // 2


def edge_sums(start, length, length_all):
    position = start + lax.iota(jnp.int32, length)
    reach_left = jnp.minimum(position, RADIUS)
    reach_right = jnp.minimum(length_all - 1 - position, RADIUS)
    return (RADIUS + 1 + one_side(reach_left) + one_side(reach_right)).astype(jnp.float32)


def shifted(block, axis, distance):
    peers = lax.axis_size(axis)
    route = [(i, i + distance) for i in range(peers) if 0 <= i + distance < peers]
    return lax.ppermute(block, axis, route)


def turned(block, distance):
    peers = lax.axis_size("gx")
    return lax.ppermute(block, "gx", [(i, (i + distance) % peers) for i in range(peers)])


def around(sends):
    return [sends[0]] + [turned(sends[d], d) for d in (1, 2, 3)]


def program(density, mask):
    planes, row_count, columns = density.shape
    groups = lax.axis_size("gx")
    layers = planes // groups
    width = columns * groups
    count_x = edge_sums(0, width, width)
    count_y = edge_sums(
        lax.axis_index("gy") * row_count, row_count, row_count * lax.axis_size("gy")
    )
    count_z = edge_sums(
        lax.axis_index(("gz", "gx")) * layers, layers, planes * lax.axis_size("gz")
    )
    scale = 1.0 / (count_y[:, None] * count_x[None, :])
    plane_scale = 1.0 / count_z

    conv, first_rows, last_rows, *sends = section(density, mask)
    received = [around(sends)]
    before = shifted(last_rows, "gy", 1)
    after = shifted(first_rows, "gy", -1)
    outgoing = edges(conv, before, after)
    halos = []
    for k in range(len(STAGES) - 1):
        halos.append((shifted(outgoing[2 * k], "gz", 1), shifted(outgoing[2 * k + 1], "gz", -1)))
    for stage in range(1, len(STAGES)):
        sends = stage_sends(stage, conv, before, after, *halos[stage - 1])
        received.append(around(sends))
    results = []
    for stage in range(len(STAGES)):
        results = finish(stage, scale, plane_scale, received[stage], results)
    return tuple(results)


def solution(mesh):
    placed = (P("gz", "gy", "gx"), P("gz", "gy", "gx"))
    return jax.shard_map(
        program,
        mesh=mesh,
        in_specs=placed,
        out_specs=(P(("gz", "gx"), "gy", None), P(("gz", "gx"), "gy", None)),
        check_vma=False,
    )
```

time: 162 us -> 106 us (0.65)
  local copies, waits for them, and re-layouts: 37.2 us -> 6.99 us
  waiting for transfers between devices: 70.1 us -> 48.2 us
  matrix products: 19.1 us -> 0 us
  Pallas kernels: 0 us -> 16.1 us
  other arithmetic: 14.8 us -> 0.2 us
  starting transfers between devices: 19.4 us -> 31.9 us
    all_to_all x1 -> x0, waiting for transfers between devices: 47 us -> none  [body(): lax.all_to_all(physical, 'gx', split_axis=0, concat_axis=2, tiled=True)]
    ppermute x4 -> x15, waiting for transfers between devices: 23 us -> 48.2 us  [the longest x9 29.4 us: turned(): lax.ppermute(block, 'gx', [(i, (i + distance) % peers) for i in range(pee...]
    dot_general x4 -> x0, matrix products: 19.1 us -> none  [the longest x1 7.32 us: along_first(): jnp.dot(kernel, flat, precision=highest, preferred_element_type=jnp.float32)]
    ppermute x4 -> x15, starting transfers between devices: 14.5 us -> 31.9 us  [the longest x6 18.8 us: shifted(): return lax.ppermute(block, axis, route)]
    pallas_call x0 -> x7, Pallas kernels: none -> 16.1 us  [the longest x3 9.44 us: finish(): pl.pallas_call(functools.partial(finish_kernel, stage), out_shape=[whole,...]
    dot_general x2 -> x0, local copies, waits for them, and re-layouts: 7.74 us -> none  [along_first(): jnp.dot(kernel, flat, precision=highest, preferred_element_type=jnp.float32)]
    slice x4 -> x0, local copies, waits for them, and re-layouts: 6.87 us -> none  [the longest x1 4.16 us: filter_last(): lower_part = padded[..., :extent].reshape(leading + (blocks, 128))]
    div x1 -> x2, other arithmetic: 6.76 us -> 0.17 us  [the longest x1 0.15 us: program(): scale = 1.0 / (count_y[:, None] * count_x[None, :])]
  transfers between devices with their start and end apart: 5 -> 15, of which waited for: 4 -> 6; matrix products, arithmetic and copies ran while one was open for 3% -> 0% of each run, Pallas kernels for 0% -> 9%
where the time goes in v1:
time: 106 us; the launch traced here: 104 us
  waiting for transfers between devices  48.2 us (45%)
  starting transfers between devices  31.9 us (30%)
  Pallas kernels  16.1 us (15%)
  local copies, waits for them, and re-layouts  6.99 us (7%)
    ppermute x9, waiting for transfers between devices, turned(): lax.ppermute(block, 'gx', [(i, (i + distance) % peers) for i in range(pee...  29.4 us
    ppermute x6, waiting for transfers between devices, shifted(): return lax.ppermute(block, axis, route)  18.8 us
    ppermute x6, starting transfers between devices, shifted(): return lax.ppermute(block, axis, route)  18.8 us
    ppermute x9, starting transfers between devices, turned(): lax.ppermute(block, 'gx', [(i, (i + distance) % peers) for i in range(pee...  13.1 us
    pallas_call x3, Pallas kernels, finish(): pl.pallas_call(functools.partial(finish_kernel, stage), out_shape=[whole,...  9.44 us
    unnamed x12, local copies, waits for them, and re-layouts  6.99 us
    pallas_call x2, Pallas kernels, stage_sends(): pl.pallas_call(functools.partial(stage_kernel, stage), out_shape=[jax.Sha...  3 us
    pallas_call x1, Pallas kernels, section(): pl.pallas_call(section_kernel, out_shape=[f32((span, rows, columns)), f32...  2.73 us
  transfers between devices with their start and end apart: 15, of which 6 were waited for; matrix products, arithmetic and copies ran while one was open for 0% of the time, Pallas kernels for 9%

profile of v1, /device:TPU:105, one launch (start us, length us, event | category | flops | bytes accessed | tf_op | source)
XLA Modules:
  0.0 104.4 jit_solution(17021227801346442720)
XLA Ops:
  0.6 2.2 %copy-done.2 = f32[32,128,256]{2,1,0:T(8,128)S(1)} copy-done((f32[32,128,256]{2,1,0:T(8,128)S(1)}, f32[32,128,256]{2,1,0:T(8,128)}, u32[]{:S(2)}) %copy-start.2) | copy-done | bytes 4194328
  2.8 0.8 copy-done.3
  3.6 2.7 %section.1 = (f32[44,128,256]{2,1,0:T(8,128)S(1)}, f32[44,8,256]{2,1,0:T(8,128)S(1)}, f32[44,8,256]{2,1,0:T(8,128)S(1)}, f32[2,112,256]{2,1,0:T(8,128)S(1)}, f32...) custom-call(f32[32,128,256]{2,1,0:T(8,128)S(1)} %copy-done.2, s32[4,16,32]{2,1,0:T(8,128)S(1)} %copy-done.3), custom_call_target="tpu_custom_call" | custom-call | flops 40000000 | bytes 8388608 | tf_op jit(solution)/shard_map/section/pallas_call | solution.py:120
  6.3 3.8 %collective-permute-start = (f32[44,8,256]{2,1,0:T(8,128)S(1)}, f32[44,8,256]{2,1,0:T(8,128)S(1)}, u32[]{:S(2)}, u32[]{:S(2)}) collective-permute-start(f32[44,8,256]{2,1,0:T(8,128)S(1)} %get-tuple-element.26), channel_id=1, source_target_pairs={{0,1},{1,2},{2,3},{3,4},{4,5},{5,6},{6,7},{8,9},{9,10},{10,11},{11... | collective-permute-start | bytes 1081352 | tf_op jit(solution)/shard_map/ppermute | solution.py:347
  10.1 1.9 %collective-permute-start.1 = (f32[44,8,256]{2,1,0:T(8,128)S(1)}, f32[44,8,256]{2,1,0:T(8,128)S(1)}, u32[]{:S(2)}, u32[]{:S(2)}) collective-permute-start(f32[44,8,256]{2,1,0:T(8,128)S(1)} %get-tuple-element.27), channel_id=1, source_target_pairs={{1,0},{2,1},{3,2},{4,3},{5,4},{6,5},{7,6},{9,8},{10,9},{11,10},{12... | collective-permute-start | bytes 1081352 | tf_op jit(solution)/shard_map/ppermute | solution.py:347
  12.0 2.4 %collective-permute-done.before = f32[44,8,256]{2,1,0:T(8,128)S(1)} collective-permute-done((f32[44,8,256]{2,1,0:T(8,128)S(1)}, f32[44,8,256]{2,1,0:T(8,128)S(1)}, u32[]{:S(2)}, u32[]{:S(2)}) %collective-permute-start) | collective-permute-done | bytes 360480 | tf_op jit(solution)/shard_map/ppermute | solution.py:347
  14.4 4.4 %collective-permute-done.1.after = f32[44,8,256]{2,1,0:T(8,128)S(1)} collective-permute-done((f32[44,8,256]{2,1,0:T(8,128)S(1)}, f32[44,8,256]{2,1,0:T(8,128)S(1)}, u32[]{:S(2)}, u32[]{:S(2)}) %collective-permute-start.1) | collective-permute-done | bytes 360480 | tf_op jit(solution)/shard_map/ppermute | solution.py:347
  18.8 0.9 edges.1
  19.7 4.7 %collective-permute-start.2 = (f32[4,144,256]{2,1,0:T(8,128)S(1)}, f32[4,144,256]{2,1,0:T(8,128)S(1)}, u32[]{:S(2)}, u32[]{:S(2)}) collective-permute-start(f32[4,144,256]{2,1,0:T(8,128)S(1)} %get-tuple-element.28), channel_id=1, source_target_pairs={{0,32},{32,64},{64,96},{96,128},{128,160},{160,192},{192,224},{1,3... | collective-permute-start | bytes 1769480 | tf_op jit(solution)/shard_map/ppermute | solution.py:347
  24.5 1.9 %collective-permute-start.3 = (f32[4,144,256]{2,1,0:T(8,128)}, f32[4,144,256]{2,1,0:T(8,128)S(1)}, u32[]{:S(2)}, u32[]{:S(2)}) collective-permute-start(f32[4,144,256]{2,1,0:T(8,128)} %get-tuple-element.29), channel_id=1, source_target_pairs={{32,0},{64,32},{96,64},{128,96},{160,128},{192,160},{224,192},{33,... | collective-permute-start | bytes 1769480 | tf_op jit(solution)/shard_map/ppermute | solution.py:347
  26.4 4.6 %collective-permute-start.7 = (f32[2,144,256]{2,1,0:T(8,128)S(1)}, f32[2,144,256]{2,1,0:T(8,128)S(1)}, u32[]{:S(2)}, u32[]{:S(2)}) collective-permute-start(f32[2,144,256]{2,1,0:T(8,128)S(1)} %get-tuple-element.34), channel_id=1, source_target_pairs={{0,32},{32,64},{64,96},{96,128},{128,160},{160,192},{192,224},{1,3... | collective-permute-start | bytes 884744 | tf_op jit(solution)/shard_map/ppermute | solution.py:347
  31.0 1.9 %collective-permute-start.8 = (f32[2,144,256]{2,1,0:T(8,128)S(1)}, f32[2,144,256]{2,1,0:T(8,128)S(1)}, u32[]{:S(2)}, u32[]{:S(2)}) collective-permute-start(f32[2,144,256]{2,1,0:T(8,128)S(1)} %get-tuple-element.35), channel_id=1, source_target_pairs={{32,0},{64,32},{96,64},{128,96},{160,128},{192,160},{224,192},{33,... | collective-permute-start | bytes 884744 | tf_op jit(solution)/shard_map/ppermute | solution.py:347
  32.9 1.3 %collective-permute-start.12 = (f32[2,112,256]{2,1,0:T(8,128)}, f32[2,112,256]{2,1,0:T(8,128)S(1)}, u32[]{:S(2)}, u32[]{:S(2)}) collective-permute-start(f32[2,112,256]{2,1,0:T(8,128)} %get-tuple-element.41), channel_id=1, source_target_pairs={{0,8},{8,16},{16,24},{24,0},{1,9},{9,17},{17,25},{25,1},{2,10},{10... | collective-permute-start | bytes 688136 | tf_op jit(solution)/shard_map/ppermute | solution.py:352
  34.2 8.8 %collective-permute-done.7.lower = f32[2,144,256]{2,1,0:T(8,128)S(1)} collective-permute-done((f32[2,144,256]{2,1,0:T(8,128)S(1)}, f32[2,144,256]{2,1,0:T(8,128)S(1)}, u32[]{:S(2)}, u32[]{:S(2)}) %collective-permute-start.7) | collective-permute-done | bytes 294944 | tf_op jit(solution)/shard_map/ppermute | solution.py:347
  43.1 2.7 %collective-permute-start.13 = (f32[2,112,256]{2,1,0:T(8,128)}, f32[2,112,256]{2,1,0:T(8,128)}, u32[]{:S(2)}, u32[]{:S(2)}) collective-permute-start(f32[2,112,256]{2,1,0:T(8,128)} %get-tuple-element.42), channel_id=1, source_target_pairs={{0,16},{8,24},{16,0},{24,8},{1,17},{9,25},{17,1},{25,9},{2,18},{10... | collective-permute-start | bytes 688136 | tf_op jit(solution)/shard_map/ppermute | solution.py:352
  45.8 3.2 %collective-permute-done.8.upper = f32[2,144,256]{2,1,0:T(8,128)S(1)} collective-permute-done((f32[2,144,256]{2,1,0:T(8,128)S(1)}, f32[2,144,256]{2,1,0:T(8,128)S(1)}, u32[]{:S(2)}, u32[]{:S(2)}) %collective-permute-start.8) | collective-permute-done | bytes 294944 | tf_op jit(solution)/shard_map/ppermute | solution.py:347
  49.0 1.2 %shard_map.42 = (f32[288,256]{1,0:T(8,128)S(1)}, f32[288,256]{1,0:T(8,128)}, f32[288,256]{1,0:T(8,128)S(1)}, f32[288,256]{1,0:T(8,128)S(1)}) custom-call(f32[44,128,256]{2,1,0:T(8,128)S(1)} %get-tuple-element.25.conv, f32[44,8,256]{2,1,0:T(8,128)S(1)} %collective-permute-done.before, f32[44,8,256]{2,1,0:T(8,128)S(1)} %collective-permute-done.1.after, ...), custom_call_target="tpu_custom_call" | custom-call | flops 40000000 | bytes 8388608 | tf_op jit(solution)/shard_map/pallas_call | solution.py:215
  50.2 0.7 copy-done.4
  50.9 0.7 copy-done.5
  51.6 1.1 %collective-permute-start.9 = (f32[288,256]{1,0:T(8,128)}, f32[288,256]{1,0:T(8,128)S(1)}, u32[]{:S(2)}, u32[]{:S(2)}) collective-permute-start(f32[288,256]{1,0:T(8,128)} %get-tuple-element.37), channel_id=1, source_target_pairs={{0,8},{8,16},{16,24},{24,0},{1,9},{9,17},{17,25},{25,1},{2,10},{10... | collective-permute-start | bytes 884744 | tf_op jit(solution)/shard_map/ppermute | solution.py:352
  52.6 1.6 %collective-permute-start.14 = (f32[2,112,256]{2,1,0:T(8,128)}, f32[2,112,256]{2,1,0:T(8,128)}, u32[]{:S(2)}, u32[]{:S(2)}) collective-permute-start(f32[2,112,256]{2,1,0:T(8,128)} %get-tuple-element.43), channel_id=1, source_target_pairs={{0,24},{8,0},{16,8},{24,16},{1,25},{9,1},{17,9},{25,17},{2,26},{10... | collective-permute-start | bytes 688136 | tf_op jit(solution)/shard_map/ppermute | solution.py:352
  54.3 2.6 %copy-done.1 = f32[44,128,256]{2,1,0:T(8,128)S(1)} copy-done((f32[44,128,256]{2,1,0:T(8,128)S(1)}, f32[44,128,256]{2,1,0:T(8,128)}, u32[]{:S(2)}) %copy-start.1) | copy-done | bytes 5767192
  56.9 1.8 %shard_map.41 = (f32[512,256]{1,0:T(8,128)S(1)}, f32[512,256]{1,0:T(8,128)}, f32[512,256]{1,0:T(8,128)}, f32[512,256]{1,0:T(8,128)}) custom-call(f32[44,128,256]{2,1,0:T(8,128)S(1)} %copy-done.1, f32[44,8,256]{2,1,0:T(8,128)S(1)} %collective-permute-done.before, f32[44,8,256]{2,1,0:T(8,128)S(1)} %collective-permute-done.1.after, ...), custom_call_target="tpu_custom_call" | custom-call | flops 40000000 | bytes 8388608 | tf_op jit(solution)/shard_map/pallas_call | solution.py:215
  58.7 2.4 %collective-permute-start.5 = (f32[512,256]{1,0:T(8,128)}, f32[512,256]{1,0:T(8,128)S(1)}, u32[]{:S(2)}, u32[]{:S(2)}) collective-permute-start(f32[512,256]{1,0:T(8,128)} %get-tuple-element.32), channel_id=1, source_target_pairs={{0,16},{8,24},{16,0},{24,8},{1,17},{9,25},{17,1},{25,9},{2,18},{10... | collective-permute-start | bytes 1572872 | tf_op jit(solution)/shard_map/ppermute | solution.py:352
  61.2 1.0 collective-permute-start.6
  62.2 1.7 %collective-permute-start.10 = (f32[288,256]{1,0:T(8,128)}, f32[288,256]{1,0:T(8,128)S(1)}, u32[]{:S(2)}, u32[]{:S(2)}) collective-permute-start(f32[288,256]{1,0:T(8,128)} %copy-done.5), channel_id=1, source_target_pairs={{0,16},{8,24},{16,0},{24,8},{1,17},{9,25},{17,1},{25,9},{2,18},{10... | collective-permute-start | bytes 884744 | tf_op jit(solution)/shard_map/ppermute | solution.py:352
  63.9 1.3 %collective-permute-start.11 = (f32[288,256]{1,0:T(8,128)}, f32[288,256]{1,0:T(8,128)S(1)}, u32[]{:S(2)}, u32[]{:S(2)}) collective-permute-start(f32[288,256]{1,0:T(8,128)} %copy-done.4), channel_id=1, source_target_pairs={{0,24},{8,0},{16,8},{24,16},{1,25},{9,1},{17,9},{25,17},{2,26},{10... | collective-permute-start | bytes 884744 | tf_op jit(solution)/shard_map/ppermute | solution.py:352
  65.4 2.9 %shard_map.43 = (f32[8,128,1024]{2,1,0:T(8,128)}, f32[8,128,1024]{2,1,0:T(8,128)}) custom-call(f32[128,1024]{1,0:T(8,128)S(1)} %multiply_divide_fusion.refs_0_, f32[8]{0:T(128)S(1)} %convert_divide_fusion.refs_1_, f32[2,112,256]{2,1,0:T(8,128)S(1)} %get-tuple-element.40.refs_2_, f32[2,112,256]{2,1,0:T(8,128)S(1)} %collective-permute-done.12.refs_3_, ...), custom_call_target="tpu_custom_call" | custom-call | flops 40000000 | bytes 8388608 | tf_op jit(solution)/shard_map/pallas_call | solution.py:312
  68.3 23.2 %collective-permute-done.10.refs_4_ = f32[288,256]{1,0:T(8,128)S(1)} collective-permute-done((f32[288,256]{1,0:T(8,128)}, f32[288,256]{1,0:T(8,128)S(1)}, u32[]{:S(2)}, u32[]{:S(2)}) %collective-permute-start.10) | collective-permute-done | bytes 294944 | tf_op jit(solution)/shard_map/ppermute | solution.py:352
  91.5 6.2 %collective-permute-done.11.refs_5_ = f32[288,256]{1,0:T(8,128)S(1)} collective-permute-done((f32[288,256]{1,0:T(8,128)}, f32[288,256]{1,0:T(8,128)S(1)}, u32[]{:S(2)}, u32[]{:S(2)}) %collective-permute-start.11) | collective-permute-done | bytes 294944 | tf_op jit(solution)/shard_map/ppermute | solution.py:352
  97.6 3.3 %shard_map.44 = (f32[8,128,1024]{2,1,0:T(8,128)}, f32[8,128,1024]{2,1,0:T(8,128)}) custom-call(f32[128,1024]{1,0:T(8,128)S(1)} %multiply_divide_fusion.refs_0_, f32[8]{0:T(128)S(1)} %convert_divide_fusion.refs_1_, f32[288,256]{1,0:T(8,128)S(1)} %get-tuple-element.36.refs_2_, ...), custom_call_target="tpu_custom_call", output_to_operand_aliasing={{0}: (6, {}), {1}: (7, {})} | custom-call | flops 40000000 | bytes 8388608 | tf_op jit(solution)/shard_map/pallas_call | solution.py:312
  100.9 3.3 %shard_map.45 = (f32[8,128,1024]{2,1,0:T(8,128)}, f32[8,128,1024]{2,1,0:T(8,128)}) custom-call(f32[128,1024]{1,0:T(8,128)S(1)} %multiply_divide_fusion.refs_0_, f32[8]{0:T(128)S(1)} %convert_divide_fusion.refs_1_, f32[512,256]{1,0:T(8,128)S(1)} %get-tuple-element.30.refs_2_, ...), custom_call_target="tpu_custom_call", output_to_operand_aliasing={{0}: (6, {}), {1}: (7, {})} | custom-call | flops 40000000 | bytes 8388608 | tf_op jit(solution)/shard_map/pallas_call | solution.py:312
  (21 shorter events, 0.2 us)
Async XLA Ops:
  0.6 2.2 %copy-start.2 = (f32[32,128,256]{2,1,0:T(8,128)S(1)}, f32[32,128,256]{2,1,0:T(8,128)}, u32[]{:S(2)}) copy-start(f32[32,128,256]{2,1,0:T(8,128)} %density.1) | copy-start | bytes 12582916
  2.8 0.8 copy-start.3
  6.3 43.8 %copy-start = (f32[44,128,256]{2,1,0:T(8,128)}, f32[44,128,256]{2,1,0:T(8,128)S(1)}, u32[]{:S(2)}) copy-start(f32[44,128,256]{2,1,0:T(8,128)S(1)} %get-tuple-element.25.conv) | copy-start | bytes 17301508
  6.3 8.1 %collective-permute-start = (f32[44,8,256]{2,1,0:T(8,128)S(1)}, f32[44,8,256]{2,1,0:T(8,128)S(1)}, u32[]{:S(2)}, u32[]{:S(2)}) collective-permute-start(f32[44,8,256]{2,1,0:T(8,128)S(1)} %get-tuple-element.26), channel_id=1, source_target_pairs={{0,1},{1,2},{2,3},{3,4},{4,5},{5,6},{6,7},{8,9},{9,10},{10,11},{11... | collective-permute-start | bytes 1081352 | tf_op jit(solution)/shard_map/ppermute | solution.py:347
  10.1 8.7 %collective-permute-start.1 = (f32[44,8,256]{2,1,0:T(8,128)S(1)}, f32[44,8,256]{2,1,0:T(8,128)S(1)}, u32[]{:S(2)}, u32[]{:S(2)}) collective-permute-start(f32[44,8,256]{2,1,0:T(8,128)S(1)} %get-tuple-element.27), channel_id=1, source_target_pairs={{1,0},{2,1},{3,2},{4,3},{5,4},{6,5},{7,6},{9,8},{10,9},{11,10},{12... | collective-permute-start | bytes 1081352 | tf_op jit(solution)/shard_map/ppermute | solution.py:347
  19.7 32.9 %collective-permute-start.2 = (f32[4,144,256]{2,1,0:T(8,128)S(1)}, f32[4,144,256]{2,1,0:T(8,128)S(1)}, u32[]{:S(2)}, u32[]{:S(2)}) collective-permute-start(f32[4,144,256]{2,1,0:T(8,128)S(1)} %get-tuple-element.28), channel_id=1, source_target_pairs={{0,32},{32,64},{64,96},{96,128},{128,160},{160,192},{192,224},{1,3... | collective-permute-start | bytes 1769480 | tf_op jit(solution)/shard_map/ppermute | solution.py:347
  24.5 29.8 %collective-permute-start.3 = (f32[4,144,256]{2,1,0:T(8,128)}, f32[4,144,256]{2,1,0:T(8,128)S(1)}, u32[]{:S(2)}, u32[]{:S(2)}) collective-permute-start(f32[4,144,256]{2,1,0:T(8,128)} %get-tuple-element.29), channel_id=1, source_target_pairs={{32,0},{64,32},{96,64},{128,96},{160,128},{192,160},{224,192},{33,... | collective-permute-start | bytes 1769480 | tf_op jit(solution)/shard_map/ppermute | solution.py:347
  26.4 16.6 %collective-permute-start.7 = (f32[2,144,256]{2,1,0:T(8,128)S(1)}, f32[2,144,256]{2,1,0:T(8,128)S(1)}, u32[]{:S(2)}, u32[]{:S(2)}) collective-permute-start(f32[2,144,256]{2,1,0:T(8,128)S(1)} %get-tuple-element.34), channel_id=1, source_target_pairs={{0,32},{32,64},{64,96},{96,128},{128,160},{160,192},{192,224},{1,3... | collective-permute-start | bytes 884744 | tf_op jit(solution)/shard_map/ppermute | solution.py:347
  31.0 18.0 %collective-permute-start.8 = (f32[2,144,256]{2,1,0:T(8,128)S(1)}, f32[2,144,256]{2,1,0:T(8,128)S(1)}, u32[]{:S(2)}, u32[]{:S(2)}) collective-permute-start(f32[2,144,256]{2,1,0:T(8,128)S(1)} %get-tuple-element.35), channel_id=1, source_target_pairs={{32,0},{64,32},{96,64},{128,96},{160,128},{192,160},{224,192},{33,... | collective-permute-start | bytes 884744 | tf_op jit(solution)/shard_map/ppermute | solution.py:347
  32.9 25.8 %collective-permute-start.12 = (f32[2,112,256]{2,1,0:T(8,128)}, f32[2,112,256]{2,1,0:T(8,128)S(1)}, u32[]{:S(2)}, u32[]{:S(2)}) collective-permute-start(f32[2,112,256]{2,1,0:T(8,128)} %get-tuple-element.41), channel_id=1, source_target_pairs={{0,8},{8,16},{16,24},{24,0},{1,9},{9,17},{17,25},{25,1},{2,10},{10... | collective-permute-start | bytes 688136 | tf_op jit(solution)/shard_map/ppermute | solution.py:352
  43.1 18.1 %collective-permute-start.13 = (f32[2,112,256]{2,1,0:T(8,128)}, f32[2,112,256]{2,1,0:T(8,128)}, u32[]{:S(2)}, u32[]{:S(2)}) collective-permute-start(f32[2,112,256]{2,1,0:T(8,128)} %get-tuple-element.42), channel_id=1, source_target_pairs={{0,16},{8,24},{16,0},{24,8},{1,17},{9,25},{17,1},{25,9},{2,18},{10... | collective-permute-start | bytes 688136 | tf_op jit(solution)/shard_map/ppermute | solution.py:352
  50.2 0.7 copy-start.4
  50.9 0.7 copy-start.5
  51.6 12.3 %collective-permute-start.9 = (f32[288,256]{1,0:T(8,128)}, f32[288,256]{1,0:T(8,128)S(1)}, u32[]{:S(2)}, u32[]{:S(2)}) collective-permute-start(f32[288,256]{1,0:T(8,128)} %get-tuple-element.37), channel_id=1, source_target_pairs={{0,8},{8,16},{16,24},{24,0},{1,9},{9,17},{17,25},{25,1},{2,10},{10... | collective-permute-start | bytes 884744 | tf_op jit(solution)/shard_map/ppermute | solution.py:352
  52.6 9.6 %collective-permute-start.14 = (f32[2,112,256]{2,1,0:T(8,128)}, f32[2,112,256]{2,1,0:T(8,128)}, u32[]{:S(2)}, u32[]{:S(2)}) collective-permute-start(f32[2,112,256]{2,1,0:T(8,128)} %get-tuple-element.43), channel_id=1, source_target_pairs={{0,24},{8,0},{16,8},{24,16},{1,25},{9,1},{17,9},{25,17},{2,26},{10... | collective-permute-start | bytes 688136 | tf_op jit(solution)/shard_map/ppermute | solution.py:352
  54.3 2.6 %copy-start.1 = (f32[44,128,256]{2,1,0:T(8,128)S(1)}, f32[44,128,256]{2,1,0:T(8,128)}, u32[]{:S(2)}) copy-start(f32[44,128,256]{2,1,0:T(8,128)} %copy-done) | copy-start | bytes 17301508
  58.7 42.2 %collective-permute-start.4 = (f32[512,256]{1,0:T(8,128)}, f32[512,256]{1,0:T(8,128)S(1)}, u32[]{:S(2)}, u32[]{:S(2)}) collective-permute-start(f32[512,256]{1,0:T(8,128)} %get-tuple-element.31), channel_id=1, source_target_pairs={{0,8},{8,16},{16,24},{24,0},{1,9},{9,17},{17,25},{25,1},{2,10},{10... | collective-permute-start | bytes 1572872 | tf_op jit(solution)/shard_map/ppermute | solution.py:352
  58.7 42.2 %collective-permute-start.5 = (f32[512,256]{1,0:T(8,128)}, f32[512,256]{1,0:T(8,128)S(1)}, u32[]{:S(2)}, u32[]{:S(2)}) collective-permute-start(f32[512,256]{1,0:T(8,128)} %get-tuple-element.32), channel_id=1, source_target_pairs={{0,16},{8,24},{16,0},{24,8},{1,17},{9,25},{17,1},{25,9},{2,18},{10... | collective-permute-start | bytes 1572872 | tf_op jit(solution)/shard_map/ppermute | solution.py:352
  61.2 39.8 %collective-permute-start.6 = (f32[512,256]{1,0:T(8,128)}, f32[512,256]{1,0:T(8,128)S(1)}, u32[]{:S(2)}, u32[]{:S(2)}) collective-permute-start(f32[512,256]{1,0:T(8,128)} %get-tuple-element.33), channel_id=1, source_target_pairs={{0,24},{8,0},{16,8},{24,16},{1,25},{9,1},{17,9},{25,17},{2,26},{10... | collective-permute-start | bytes 1572872 | tf_op jit(solution)/shard_map/ppermute | solution.py:352
  62.2 29.2 %collective-permute-start.10 = (f32[288,256]{1,0:T(8,128)}, f32[288,256]{1,0:T(8,128)S(1)}, u32[]{:S(2)}, u32[]{:S(2)}) collective-permute-start(f32[288,256]{1,0:T(8,128)} %copy-done.5), channel_id=1, source_target_pairs={{0,16},{8,24},{16,0},{24,8},{1,17},{9,25},{17,1},{25,9},{2,18},{10... | collective-permute-start | bytes 884744 | tf_op jit(solution)/shard_map/ppermute | solution.py:352
  63.9 33.7 %collective-permute-start.11 = (f32[288,256]{1,0:T(8,128)}, f32[288,256]{1,0:T(8,128)S(1)}, u32[]{:S(2)}, u32[]{:S(2)}) collective-permute-start(f32[288,256]{1,0:T(8,128)} %copy-done.4), channel_id=1, source_target_pairs={{0,24},{8,0},{16,8},{24,16},{1,25},{9,1},{17,9},{25,17},{2,26},{10... | collective-permute-start | bytes 884744 | tf_op jit(solution)/shard_map/ppermute | solution.py:352

commit v2 on v1

--- a/solution.py
+++ b/solution.py
@@ -18,6 +18,7 @@
 
 
 STAGES = (2, 2, 4)
+CHUNKS = 4
 
 
 def first_of(stage):
@@ -62,17 +63,30 @@
     return pl.CostEstimate(flops=flops, bytes_accessed=8 * 1024 * 1024, transcendentals=0)
 
 
-def section_kernel(density, mask, conv, first_rows, last_rows, *rest):
-    sends, codes = rest[:4], rest[4]
+def section_kernel(density, mask, conv, *rest):
+    near_edges, far_edges, sends = rest[:2], rest[2:4], rest[4:8]
+    held, table, codes, sems = rest[8:]
     planes, rows, columns = density.shape
     blocks = rows // CELLS
-    table = mask[...].reshape(planes // CELLS * blocks, columns // CELLS)
+    copy_mask = pltpu.make_async_copy(mask, table, sems.at[CHUNKS])
+    copy_mask.start()
+    copies = []
+    for c in range(CHUNKS):
+        part = pl.ds(c * (rows // CHUNKS), rows // CHUNKS)
+        copies.append(
+            pltpu.make_async_copy(density.at[:, part, :], held.at[:, part, :], sems.at[c])
+        )
+        copies[-1].start()
     spread = (
         lax.broadcasted_iota(jnp.int32, (columns // CELLS, columns), 1) // CELLS
         == lax.broadcasted_iota(jnp.int32, (columns // CELLS, columns), 0)
     )
+    copy_mask.wait()
     codes[...] = jnp.dot(
-        table.astype(jnp.float32).astype(jnp.bfloat16),
+        table[...]
+        .reshape(planes // CELLS * blocks, columns // CELLS)
+        .astype(jnp.float32)
+        .astype(jnp.bfloat16),
         spread.astype(jnp.float32).astype(jnp.bfloat16),
         preferred_element_type=jnp.float32,
     )
@@ -88,7 +102,7 @@
                         codes[pl.ds(z // CELLS * blocks + i, 1), :], (CELLS, columns)
                     )
                     void, solid = code < 0.5, code < 1.5
-                value = jnp.where(void, 0.0, jnp.where(solid, 1.0, density[z, row, :]))
+                value = jnp.where(void, 0.0, jnp.where(solid, 1.0, held[z, row, :]))
                 values.append(value)
                 box = value if box is None else box + value
             if z < planes + RADIUS:
@@ -101,9 +115,13 @@
             conv[z, row, :] = total
         return carry
 
-    lax.fori_loop(0, blocks, tile, 0)
-    first_rows[...] = conv[:, :EDGE, :]
-    last_rows[...] = conv[:, rows - EDGE :, :]
+    for c in range(CHUNKS):
+        copies[c].wait()
+        lax.fori_loop(c * blocks // CHUNKS, (c + 1) * blocks // CHUNKS, tile, 0)
+    for k, part in enumerate((slice(0, EDGE), slice(rows - EDGE, rows))):
+        near_edges[k][:RADIUS] = conv[:RADIUS, part, :]
+        near_edges[k][RADIUS:] = conv[planes + RADIUS :, part, :]
+        far_edges[k][...] = conv[RADIUS : planes + RADIUS, part, :]
     kernel = hat((rows - 2 * EDGE, rows), -EDGE).astype(jnp.float32).astype(jnp.bfloat16)
     me = lax.axis_index("gx")
     for distance in range(4):
@@ -119,35 +137,46 @@
     f32 = functools.partial(jax.ShapeDtypeStruct, dtype=jnp.float32)
     return pl.pallas_call(
         section_kernel,
-        out_shape=[
-            f32((span, rows, columns)),
-            f32((span, EDGE, columns)),
-            f32((span, EDGE, columns)),
-        ]
+        out_shape=[f32((span, rows, columns))]
+        + [f32((2 * RADIUS, EDGE, columns))] * 2
+        + [f32((planes, EDGE, columns))] * 2
         + [f32((STAGES[0], rows - 2 * EDGE, columns))] * 4,
-        in_specs=vmem(2),
-        out_specs=vmem(7),
-        scratch_shapes=[pltpu.VMEM((planes // CELLS * rows // CELLS, columns), jnp.float32)],
+        in_specs=[pl.BlockSpec(memory_space=pltpu.HBM)] * 2,
+        out_specs=vmem(9),
+        scratch_shapes=[
+            pltpu.VMEM(density.shape, jnp.float32),
+            pltpu.VMEM(mask.shape, jnp.int32),
+            pltpu.VMEM((planes // CELLS * rows // CELLS, columns), jnp.float32),
+            pltpu.SemaphoreType.DMA((CHUNKS + 1,)),
+        ],
         compiler_params=params(24),
         cost_estimate=cost(40_000_000),
         name="section",
-    )(density, mask)
+    )(
+        pltpu.with_memory_space_constraint(density, pltpu.HBM),
+        pltpu.with_memory_space_constraint(mask, pltpu.HBM),
+    )
+
+
+def inside(axis, first):
+    place = lax.axis_index(axis)
+    edge = 0 if first else lax.axis_size(axis) - 1
+    return (place != edge).astype(jnp.float32)
 
 
 def edges_kernel(conv, before, after, *outs):
     planes = conv.shape[0] - 2 * RADIUS
     rows = conv.shape[1]
-    up = planes + RADIUS
-    starts = []
+    has_before, has_after = inside("gy", True), inside("gy", False)
     for stage in range(1, len(STAGES)):
         first = first_of(stage) - STAGES[0]
-        starts.append((up + RADIUS - first - STAGES[stage], first))
-    for k, (higher, lower) in enumerate(starts):
-        for out, start in ((outs[2 * k], higher), (outs[2 * k + 1], lower)):
-            count = out.shape[0]
-            out[:, :EDGE, :] = before[start : start + count]
-            out[:, EDGE : EDGE + rows, :] = conv[start : start + count]
-            out[:, EDGE + rows :, :] = after[start : start + count]
+        count = STAGES[stage]
+        higher, lower = outs[2 * stage - 2 : 2 * stage]
+        for out, start in ((higher, 2 * RADIUS - first - count), (lower, first)):
+            at = start if start < RADIUS else start + planes
+            out[:, :EDGE, :] = before[start : start + count] * has_before
+            out[:, EDGE : EDGE + rows, :] = conv[at : at + count]
+            out[:, EDGE + rows :, :] = after[start : start + count] * has_after
 
 
 def edges(conv, before, after):
@@ -162,7 +191,7 @@
         out_shape=shapes,
         in_specs=vmem(3),
         out_specs=vmem(len(shapes)),
-        compiler_params=params(16),
+        compiler_params=params(8),
         cost_estimate=cost(5_000_000),
         name="edges",
     )(conv, before, after)
@@ -184,24 +213,32 @@
     corner = jnp.where(out_last == in_last, jnp.maximum(BOX - distance, 0), 0)
     corner = corner.astype(jnp.float32).astype(jnp.bfloat16)
     me = lax.axis_index("gx")
+    has_before, has_after = inside("gy", True), inside("gy", False)
     for d in range(4):
         quarter = lax.rem(me + d, 4)
-        take_lower = (quarter == 0).astype(jnp.float32)
-        take_upper = (quarter == 3).astype(jnp.float32)
-        base = RADIUS + 8 * quarter + plane_offset(stage, quarter)
+        take_lower = (quarter == 0).astype(jnp.float32) * inside("gz", True)
+        take_upper = (quarter == 3).astype(jnp.float32) * inside("gz", False)
+        base = 8 * quarter + plane_offset(stage, quarter)
         for j in range(count):
-            plane = jnp.concatenate([before[base + j], conv[base + j], after[base + j]], axis=0)
+            plane = jnp.concatenate(
+                [
+                    before[base + j] * has_before,
+                    conv[RADIUS + base + j],
+                    after[base + j] * has_after,
+                ],
+                axis=0,
+            )
             plane = plane + take_lower * lower[j] + take_upper * upper[j]
             sends[d][j * rows : (j + 1) * rows, :] = along_rows(kernel, plane)
         if stage == 1:
-            base = RADIUS + 8 * quarter + plane_offset(0, quarter)
+            base = 8 * quarter + plane_offset(0, quarter)
             for j in range(STAGES[0]):
                 part = jnp.concatenate(
                     [
-                        before[base + j],
-                        conv[base + j, : 2 * EDGE, :],
-                        conv[base + j, rows - 2 * EDGE :, :],
-                        after[base + j],
+                        before[base + j] * has_before,
+                        conv[RADIUS + base + j, : 2 * EDGE, :],
+                        conv[RADIUS + base + j, rows - 2 * EDGE :, :],
+                        after[base + j] * has_after,
                     ],
                     axis=0,
                 )
@@ -282,12 +319,12 @@
         inner = rows - 2 * EDGE
         for j in range(STAGES[0]):
             here = slice(j * inner, (j + 1) * inner)
-            rows_of(lambda s: s[j], here, slice(EDGE, rows - EDGE), plane_scale[offset + j])
+            rows_of(lambda s: s[j], here, slice(EDGE, rows - EDGE), plane_scale[pl.ds(offset + j, 1), :])
             send(pl.ds(j * inner, inner), offset + j, pl.ds(EDGE, inner))
     else:
         for j in range(STAGES[stage]):
             here = slice(j * rows, (j + 1) * rows)
-            rows_of(lambda s: s[here, :], here, slice(0, rows), plane_scale[offset + j])
+            rows_of(lambda s: s[here, :], here, slice(0, rows), plane_scale[pl.ds(offset + j, 1), :])
             send(pl.ds(j * rows, rows), offset + j, pl.ds(0, rows))
     if stage == 1:
         first = plane_offset(0, me)
@@ -296,7 +333,7 @@
             for put in (0, rows - EDGE):
                 here = slice(at, at + EDGE)
                 rows_of(
-                    lambda s: s[here, :], here, slice(put, put + EDGE), plane_scale[first + j]
+                    lambda s: s[here, :], here, slice(put, put + EDGE), plane_scale[pl.ds(first + j, 1), :]
                 )
                 send(pl.ds(at, EDGE), first + j, pl.ds(put, EDGE))
                 at += EDGE
@@ -312,11 +349,7 @@
     return pl.pallas_call(
         functools.partial(finish_kernel, stage),
         out_shape=[whole, whole],
-        in_specs=[
-            pl.BlockSpec(memory_space=pltpu.VMEM),
-            pl.BlockSpec(memory_space=pltpu.SMEM),
-        ]
-        + vmem(4)
+        in_specs=vmem(6)
         + [pl.BlockSpec(memory_space=pl.ANY)] * len(results),
         out_specs=[pl.BlockSpec(memory_space=pl.ANY)] * 2,
         scratch_shapes=[
@@ -334,26 +367,50 @@
     return reach * (RADIUS + 1) - reach * (reach + 1) // 2
 
 
-def edge_sums(start, length, length_all):
-    position = start + lax.iota(jnp.int32, length)
+def edge_sums(position, length):
     reach_left = jnp.minimum(position, RADIUS)
-    reach_right = jnp.minimum(length_all - 1 - position, RADIUS)
+    reach_right = jnp.minimum(length - 1 - position, RADIUS)
     return (RADIUS + 1 + one_side(reach_left) + one_side(reach_right)).astype(jnp.float32)
+
+
+def scale_kernel(scale, plane_scale):
+    rows, width = scale.shape
+    layers = plane_scale.shape[0]
+    row = lax.axis_index("gy") * rows + lax.broadcasted_iota(jnp.int32, (rows, 128), 0)
+    count_y = edge_sums(row, rows * lax.axis_size("gy"))
+    for c in range(width // 128):
+        column = c * 128 + lax.broadcasted_iota(jnp.int32, (8, 128), 1)
+        count_x = edge_sums(column, width)[:1]
+        scale[:, c * 128 : (c + 1) * 128] = 1.0 / (count_y * count_x)
+    section_place = lax.axis_index("gz") * lax.axis_size("gx") + lax.axis_index("gx")
+    plane = section_place * layers + lax.broadcasted_iota(jnp.int32, plane_scale.shape, 0)
+    plane_scale[...] = 1.0 / edge_sums(
+        plane, layers * lax.axis_size("gx") * lax.axis_size("gz")
+    )
+
+
+def scales(rows, width, columns, layers):
+    return pl.pallas_call(
+        scale_kernel,
+        out_shape=[
+            jax.ShapeDtypeStruct((rows, width), jnp.float32),
+            jax.ShapeDtypeStruct((layers, columns), jnp.float32),
+        ],
+        out_specs=vmem(2),
+        compiler_params=params(4),
+        cost_estimate=cost(5_000_000),
+        name="scales",
+    )()
 
 
 def shifted(block, axis, distance):
     peers = lax.axis_size(axis)
-    route = [(i, i + distance) for i in range(peers) if 0 <= i + distance < peers]
+    route = [(i, (i + distance) % peers) for i in range(peers)]
     return lax.ppermute(block, axis, route)
 
 
-def turned(block, distance):
-    peers = lax.axis_size("gx")
-    return lax.ppermute(block, "gx", [(i, (i + distance) % peers) for i in range(peers)])
-
-
 def around(sends):
-    return [sends[0]] + [turned(sends[d], d) for d in (1, 2, 3)]
+    return [sends[0]] + [shifted(sends[d], "gx", d) for d in (1, 2, 3)]
 
 
 def program(density, mask):
@@ -361,21 +418,14 @@
     groups = lax.axis_size("gx")
     layers = planes // groups
     width = columns * groups
-    count_x = edge_sums(0, width, width)
-    count_y = edge_sums(
-        lax.axis_index("gy") * row_count, row_count, row_count * lax.axis_size("gy")
-    )
-    count_z = edge_sums(
-        lax.axis_index(("gz", "gx")) * layers, layers, planes * lax.axis_size("gz")
-    )
-    scale = 1.0 / (count_y[:, None] * count_x[None, :])
-    plane_scale = 1.0 / count_z
-
-    conv, first_rows, last_rows, *sends = section(density, mask)
+    conv, near_first, near_last, far_first, far_last, *sends = section(density, mask)
     received = [around(sends)]
-    before = shifted(last_rows, "gy", 1)
-    after = shifted(first_rows, "gy", -1)
-    outgoing = edges(conv, before, after)
+    near_before = shifted(near_last, "gy", 1)
+    near_after = shifted(near_first, "gy", -1)
+    before = shifted(far_last, "gy", 1)
+    after = shifted(far_first, "gy", -1)
+    outgoing = edges(conv, near_before, near_after)
+    scale, plane_scale = scales(row_count, width, columns, layers)
     halos = []
     for k in range(len(STAGES) - 1):
         halos.append((shifted(outgoing[2 * k], "gz", 1), shifted(outgoing[2 * k + 1], "gz", -1)))

time: 106 us -> 90.3 us (0.85)
  the two profiles are of different devices: /device:TPU:105 before, /device:TPU:1 now
where the time goes in v2:
time: 90.3 us; the launch traced here: 90.2 us
  waiting for transfers between devices  48.3 us (53%)
  starting transfers between devices  28.7 us (32%)
  Pallas kernels  12.3 us (14%)
    ppermute x17, waiting for transfers between devices, shifted(): return lax.ppermute(block, axis, route)  48.3 us
    ppermute x17, starting transfers between devices, shifted(): return lax.ppermute(block, axis, route)  28.7 us
    pallas_call x3, Pallas kernels, finish(): pl.pallas_call(functools.partial(finish_kernel, stage), out_shape=[whole,...  7.39 us
    pallas_call x1, Pallas kernels, section(): pl.pallas_call(section_kernel, out_shape=[f32((span, rows, columns))] + [...  3.12 us
  transfers between devices with their start and end apart: 17, of which 6 were waited for; matrix products, arithmetic and copies ran while one was open for 0% of the time, Pallas kernels for 7%

profile of v2, /device:TPU:1, one launch (start us, length us, event | category | flops | bytes accessed | tf_op | source)
XLA Modules:
  0.0 90.2 jit_solution(9708806062881462849)
XLA Ops:
  0.6 3.1 %section.1 = (f32[44,128,256]{2,1,0:T(8,128)S(1)}, f32[12,8,256]{2,1,0:T(8,128)S(1)}, f32[12,8,256]{2,1,0:T(8,128)S(1)}, f32[32,8,256]{2,1,0:T(8,128)S(1)}, f32[...) custom-call(f32[32,128,256]{2,1,0:T(8,128)} %density.1, ...), custom_call_target="tpu_custom_call" | custom-call | flops 40000000 | bytes 8388608 | tf_op jit(solution)/shard_map/section/pallas_call | solution.py:138
  3.8 2.7 %collective-permute-start.2 = (f32[12,8,256]{2,1,0:T(8,128)S(1)}, f32[12,8,256]{2,1,0:T(8,128)S(1)}, u32[]{:S(2)}, u32[]{:S(2)}) collective-permute-start(f32[12,8,256]{2,1,0:T(8,128)S(1)} %get-tuple-element.34), channel_id=1, source_target_pairs={{0,1},{1,2},{2,3},{3,4},{4,5},{5,6},{6,7},{7,0},{8,9},{9,10},{10,1... | collective-permute-start | bytes 294920 | tf_op jit(solution)/shard_map/ppermute | solution.py:409
  6.5 0.5 collective-permute-start.3
  7.0 1.2 %collective-permute-start = (f32[32,8,256]{2,1,0:T(8,128)S(1)}, f32[32,8,256]{2,1,0:T(8,128)S(1)}, u32[]{:S(2)}, u32[]{:S(2)}) collective-permute-start(f32[32,8,256]{2,1,0:T(8,128)S(1)} %get-tuple-element.32), channel_id=1, source_target_pairs={{0,1},{1,2},{2,3},{3,4},{4,5},{5,6},{6,7},{7,0},{8,9},{9,10},{10,1... | collective-permute-start | bytes 786440 | tf_op jit(solution)/shard_map/ppermute | solution.py:409
  8.2 2.6 %collective-permute-done.3.after = f32[12,8,256]{2,1,0:T(8,128)S(1)} collective-permute-done((f32[12,8,256]{2,1,0:T(8,128)S(1)}, f32[12,8,256]{2,1,0:T(8,128)S(1)}, u32[]{:S(2)}, u32[]{:S(2)}) %collective-permute-start.3) | collective-permute-done | bytes 98336 | tf_op jit(solution)/shard_map/ppermute | solution.py:409
  10.8 0.1 edges.1
  10.9 1.4 %collective-permute-start.4 = (f32[4,144,256]{2,1,0:T(8,128)S(1)}, f32[4,144,256]{2,1,0:T(8,128)S(1)}, u32[]{:S(2)}, u32[]{:S(2)}) collective-permute-start(f32[4,144,256]{2,1,0:T(8,128)S(1)} %get-tuple-element.36), channel_id=1, source_target_pairs={{0,32},{32,64},{64,96},{96,128},{128,160},{160,192},{192,224},{224... | collective-permute-start | bytes 1769480 | tf_op jit(solution)/shard_map/ppermute | solution.py:409
  12.3 4.0 %collective-permute-start.5 = (f32[4,144,256]{2,1,0:T(8,128)S(1)}, f32[4,144,256]{2,1,0:T(8,128)S(1)}, u32[]{:S(2)}, u32[]{:S(2)}) collective-permute-start(f32[4,144,256]{2,1,0:T(8,128)S(1)} %get-tuple-element.37), channel_id=1, source_target_pairs={{0,224},{32,0},{64,32},{96,64},{128,96},{160,128},{192,160},{224,1... | collective-permute-start | bytes 1769480 | tf_op jit(solution)/shard_map/ppermute | solution.py:409
  16.4 0.0 collective-permute-start.9
  16.4 0.3 collective-permute-start.1
  16.7 3.0 %collective-permute-start.10 = (f32[2,144,256]{2,1,0:T(8,128)S(1)}, f32[2,144,256]{2,1,0:T(8,128)S(1)}, u32[]{:S(2)}, u32[]{:S(2)}) collective-permute-start(f32[2,144,256]{2,1,0:T(8,128)S(1)} %get-tuple-element.43), channel_id=1, source_target_pairs={{0,224},{32,0},{64,32},{96,64},{128,96},{160,128},{192,160},{224,1... | collective-permute-start | bytes 884744 | tf_op jit(solution)/shard_map/ppermute | solution.py:409
  19.6 2.8 %collective-permute-done.1.after = f32[32,8,256]{2,1,0:T(8,128)S(1)} collective-permute-done((f32[32,8,256]{2,1,0:T(8,128)S(1)}, f32[32,8,256]{2,1,0:T(8,128)S(1)}, u32[]{:S(2)}, u32[]{:S(2)}) %collective-permute-start.1) | collective-permute-done | bytes 262176 | tf_op jit(solution)/shard_map/ppermute | solution.py:409
  22.5 1.2 %collective-permute-start.14 = (f32[2,112,256]{2,1,0:T(8,128)S(1)}, f32[2,112,256]{2,1,0:T(8,128)S(1)}, u32[]{:S(2)}, u32[]{:S(2)}) collective-permute-start(f32[2,112,256]{2,1,0:T(8,128)S(1)} %get-tuple-element.49), channel_id=1, source_target_pairs={{0,8},{8,16},{16,24},{24,0},{1,9},{9,17},{17,25},{25,1},{2,10},{10... | collective-permute-start | bytes 688136 | tf_op jit(solution)/shard_map/ppermute | solution.py:409
  23.7 12.6 %collective-permute-done.9.lower = f32[2,144,256]{2,1,0:T(8,128)S(1)} collective-permute-done((f32[2,144,256]{2,1,0:T(8,128)S(1)}, f32[2,144,256]{2,1,0:T(8,128)S(1)}, u32[]{:S(2)}, u32[]{:S(2)}) %collective-permute-start.9) | collective-permute-done | bytes 294944 | tf_op jit(solution)/shard_map/ppermute | solution.py:409
  36.3 2.7 %collective-permute-start.15 = (f32[2,112,256]{2,1,0:T(8,128)S(1)}, f32[2,112,256]{2,1,0:T(8,128)S(1)}, u32[]{:S(2)}, u32[]{:S(2)}) collective-permute-start(f32[2,112,256]{2,1,0:T(8,128)S(1)} %get-tuple-element.50), channel_id=1, source_target_pairs={{0,16},{8,24},{16,0},{24,8},{1,17},{9,25},{17,1},{25,9},{2,18},{10... | collective-permute-start | bytes 688136 | tf_op jit(solution)/shard_map/ppermute | solution.py:409
  39.0 0.7 shard_map.42
  39.7 0.4 collective-permute-start.11
  40.1 2.4 %collective-permute-start.16 = (f32[2,112,256]{2,1,0:T(8,128)S(1)}, f32[2,112,256]{2,1,0:T(8,128)S(1)}, u32[]{:S(2)}, u32[]{:S(2)}) collective-permute-start(f32[2,112,256]{2,1,0:T(8,128)S(1)} %get-tuple-element.51), channel_id=1, source_target_pairs={{0,24},{8,0},{16,8},{24,16},{1,25},{9,1},{17,9},{25,17},{2,26},{10... | collective-permute-start | bytes 688136 | tf_op jit(solution)/shard_map/ppermute | solution.py:409
  42.4 0.0 collective-permute-done.5.upper
  42.4 0.9 shard_map.41
  43.3 0.1 collective-permute-start.6
  43.4 1.2 %collective-permute-start.7 = (f32[512,256]{1,0:T(8,128)S(1)}, f32[512,256]{1,0:T(8,128)S(1)}, u32[]{:S(2)}, u32[]{:S(2)}) collective-permute-start(f32[512,256]{1,0:T(8,128)S(1)} %get-tuple-element.40), channel_id=1, source_target_pairs={{0,16},{8,24},{16,0},{24,8},{1,17},{9,25},{17,1},{25,9},{2,18},{10... | collective-permute-start | bytes 1572872 | tf_op jit(solution)/shard_map/ppermute | solution.py:409
  44.6 2.2 %collective-permute-start.8 = (f32[512,256]{1,0:T(8,128)S(1)}, f32[512,256]{1,0:T(8,128)S(1)}, u32[]{:S(2)}, u32[]{:S(2)}) collective-permute-start(f32[512,256]{1,0:T(8,128)S(1)} %get-tuple-element.41), channel_id=1, source_target_pairs={{0,24},{8,0},{16,8},{24,16},{1,25},{9,1},{17,9},{25,17},{2,26},{10... | collective-permute-start | bytes 1572872 | tf_op jit(solution)/shard_map/ppermute | solution.py:409
  46.8 2.5 %collective-permute-done.16.refs_5_ = f32[2,112,256]{2,1,0:T(8,128)S(1)} collective-permute-done((f32[2,112,256]{2,1,0:T(8,128)S(1)}, f32[2,112,256]{2,1,0:T(8,128)S(1)}, u32[]{:S(2)}, u32[]{:S(2)}) %collective-permute-start.16) | collective-permute-done | bytes 229408 | tf_op jit(solution)/shard_map/ppermute | solution.py:409
  49.3 2.1 %collective-permute-start.12 = (f32[288,256]{1,0:T(8,128)S(1)}, f32[288,256]{1,0:T(8,128)S(1)}, u32[]{:S(2)}, u32[]{:S(2)}) collective-permute-start(f32[288,256]{1,0:T(8,128)S(1)} %get-tuple-element.46), channel_id=1, source_target_pairs={{0,16},{8,24},{16,0},{24,8},{1,17},{9,25},{17,1},{25,9},{2,18},{10... | collective-permute-start | bytes 884744 | tf_op jit(solution)/shard_map/ppermute | solution.py:409
  51.4 3.3 %collective-permute-start.13 = (f32[288,256]{1,0:T(8,128)S(1)}, f32[288,256]{1,0:T(8,128)S(1)}, u32[]{:S(2)}, u32[]{:S(2)}) collective-permute-start(f32[288,256]{1,0:T(8,128)S(1)} %get-tuple-element.47), channel_id=1, source_target_pairs={{0,24},{8,0},{16,8},{24,16},{1,25},{9,1},{17,9},{25,17},{2,26},{10... | collective-permute-start | bytes 884744 | tf_op jit(solution)/shard_map/ppermute | solution.py:409
  54.7 0.2 scales.1
  54.9 1.9 %shard_map.43 = (f32[8,128,1024]{2,1,0:T(8,128)}, f32[8,128,1024]{2,1,0:T(8,128)}) custom-call(f32[128,1024]{1,0:T(8,128)S(1)} %get-tuple-element.29.refs_0_, f32[8,256]{1,0:T(8,128)S(1)} %get-tuple-element.30.refs_1_, f32[2,112,256]{2,1,0:T(8,128)S(1)} %get-tuple-element.48.refs_2_, f32[2,112,256]{2,1,0:T(8,128)S(1)} %collective-permute-done.14.refs_3_, ...), custom_call_target="tpu_custom_call" | custom-call | flops 40000000 | bytes 8388608 | tf_op jit(solution)/shard_map/pallas_call | solution.py:349
  56.8 22.7 %collective-permute-done.12.refs_4_ = f32[288,256]{1,0:T(8,128)S(1)} collective-permute-done((f32[288,256]{1,0:T(8,128)S(1)}, f32[288,256]{1,0:T(8,128)S(1)}, u32[]{:S(2)}, u32[]{:S(2)}) %collective-permute-start.12) | collective-permute-done | bytes 294944 | tf_op jit(solution)/shard_map/ppermute | solution.py:409
  79.4 5.1 %collective-permute-done.13.refs_5_ = f32[288,256]{1,0:T(8,128)S(1)} collective-permute-done((f32[288,256]{1,0:T(8,128)S(1)}, f32[288,256]{1,0:T(8,128)S(1)}, u32[]{:S(2)}, u32[]{:S(2)}) %collective-permute-start.13) | collective-permute-done | bytes 294944 | tf_op jit(solution)/shard_map/ppermute | solution.py:409
  84.5 2.7 %shard_map.44 = (f32[8,128,1024]{2,1,0:T(8,128)}, f32[8,128,1024]{2,1,0:T(8,128)}) custom-call(f32[128,1024]{1,0:T(8,128)S(1)} %get-tuple-element.29.refs_0_, f32[8,256]{1,0:T(8,128)S(1)} %get-tuple-element.30.refs_1_, f32[288,256]{1,0:T(8,128)S(1)} %get-tuple-element.44.refs_2_, ...), custom_call_target="tpu_custom_call", output_to_operand_aliasing={{0}: (6, {}), {1}: (7, {})} | custom-call | flops 40000000 | bytes 8388608 | tf_op jit(solution)/shard_map/pallas_call | solution.py:349
  87.3 2.8 %shard_map.45 = (f32[8,128,1024]{2,1,0:T(8,128)}, f32[8,128,1024]{2,1,0:T(8,128)}) custom-call(f32[128,1024]{1,0:T(8,128)S(1)} %get-tuple-element.29.refs_0_, f32[8,256]{1,0:T(8,128)S(1)} %get-tuple-element.30.refs_1_, f32[512,256]{1,0:T(8,128)S(1)} %get-tuple-element.38.refs_2_, ...), custom_call_target="tpu_custom_call", output_to_operand_aliasing={{0}: (6, {}), {1}: (7, {})} | custom-call | flops 40000000 | bytes 8388608 | tf_op jit(solution)/shard_map/pallas_call | solution.py:349
  (10 shorter events, 0.0 us)
Async XLA Ops:
  3.8 4.4 %collective-permute-start.2 = (f32[12,8,256]{2,1,0:T(8,128)S(1)}, f32[12,8,256]{2,1,0:T(8,128)S(1)}, u32[]{:S(2)}, u32[]{:S(2)}) collective-permute-start(f32[12,8,256]{2,1,0:T(8,128)S(1)} %get-tuple-element.34), channel_id=1, source_target_pairs={{0,1},{1,2},{2,3},{3,4},{4,5},{5,6},{6,7},{7,0},{8,9},{9,10},{10,1... | collective-permute-start | bytes 294920 | tf_op jit(solution)/shard_map/ppermute | solution.py:409
  6.5 4.3 %collective-permute-start.3 = (f32[12,8,256]{2,1,0:T(8,128)S(1)}, f32[12,8,256]{2,1,0:T(8,128)S(1)}, u32[]{:S(2)}, u32[]{:S(2)}) collective-permute-start(f32[12,8,256]{2,1,0:T(8,128)S(1)} %get-tuple-element.35), channel_id=1, source_target_pairs={{0,7},{1,0},{2,1},{3,2},{4,3},{5,4},{6,5},{7,6},{8,15},{9,8},{10,9... | collective-permute-start | bytes 294920 | tf_op jit(solution)/shard_map/ppermute | solution.py:409
  7.0 9.7 %collective-permute-start = (f32[32,8,256]{2,1,0:T(8,128)S(1)}, f32[32,8,256]{2,1,0:T(8,128)S(1)}, u32[]{:S(2)}, u32[]{:S(2)}) collective-permute-start(f32[32,8,256]{2,1,0:T(8,128)S(1)} %get-tuple-element.32), channel_id=1, source_target_pairs={{0,1},{1,2},{2,3},{3,4},{4,5},{5,6},{6,7},{7,0},{8,9},{9,10},{10,1... | collective-permute-start | bytes 786440 | tf_op jit(solution)/shard_map/ppermute | solution.py:409
  10.9 29.2 %collective-permute-start.4 = (f32[4,144,256]{2,1,0:T(8,128)S(1)}, f32[4,144,256]{2,1,0:T(8,128)S(1)}, u32[]{:S(2)}, u32[]{:S(2)}) collective-permute-start(f32[4,144,256]{2,1,0:T(8,128)S(1)} %get-tuple-element.36), channel_id=1, source_target_pairs={{0,32},{32,64},{64,96},{96,128},{128,160},{160,192},{192,224},{224... | collective-permute-start | bytes 1769480 | tf_op jit(solution)/shard_map/ppermute | solution.py:409
  12.3 30.1 %collective-permute-start.5 = (f32[4,144,256]{2,1,0:T(8,128)S(1)}, f32[4,144,256]{2,1,0:T(8,128)S(1)}, u32[]{:S(2)}, u32[]{:S(2)}) collective-permute-start(f32[4,144,256]{2,1,0:T(8,128)S(1)} %get-tuple-element.37), channel_id=1, source_target_pairs={{0,224},{32,0},{64,32},{96,64},{128,96},{160,128},{192,160},{224,1... | collective-permute-start | bytes 1769480 | tf_op jit(solution)/shard_map/ppermute | solution.py:409
  16.4 19.9 %collective-permute-start.9 = (f32[2,144,256]{2,1,0:T(8,128)S(1)}, f32[2,144,256]{2,1,0:T(8,128)S(1)}, u32[]{:S(2)}, u32[]{:S(2)}) collective-permute-start(f32[2,144,256]{2,1,0:T(8,128)S(1)} %get-tuple-element.42), channel_id=1, source_target_pairs={{0,32},{32,64},{64,96},{96,128},{128,160},{160,192},{192,224},{224... | collective-permute-start | bytes 884744 | tf_op jit(solution)/shard_map/ppermute | solution.py:409
  16.4 6.1 %collective-permute-start.1 = (f32[32,8,256]{2,1,0:T(8,128)S(1)}, f32[32,8,256]{2,1,0:T(8,128)S(1)}, u32[]{:S(2)}, u32[]{:S(2)}) collective-permute-start(f32[32,8,256]{2,1,0:T(8,128)S(1)} %get-tuple-element.33), channel_id=1, source_target_pairs={{0,7},{1,0},{2,1},{3,2},{4,3},{5,4},{6,5},{7,6},{8,15},{9,8},{10,9... | collective-permute-start | bytes 786440 | tf_op jit(solution)/shard_map/ppermute | solution.py:409
  16.7 22.3 %collective-permute-start.10 = (f32[2,144,256]{2,1,0:T(8,128)S(1)}, f32[2,144,256]{2,1,0:T(8,128)S(1)}, u32[]{:S(2)}, u32[]{:S(2)}) collective-permute-start(f32[2,144,256]{2,1,0:T(8,128)S(1)} %get-tuple-element.43), channel_id=1, source_target_pairs={{0,224},{32,0},{64,32},{96,64},{128,96},{160,128},{192,160},{224,1... | collective-permute-start | bytes 884744 | tf_op jit(solution)/shard_map/ppermute | solution.py:409
  22.5 20.9 %collective-permute-start.14 = (f32[2,112,256]{2,1,0:T(8,128)S(1)}, f32[2,112,256]{2,1,0:T(8,128)S(1)}, u32[]{:S(2)}, u32[]{:S(2)}) collective-permute-start(f32[2,112,256]{2,1,0:T(8,128)S(1)} %get-tuple-element.49), channel_id=1, source_target_pairs={{0,8},{8,16},{16,24},{24,0},{1,9},{9,17},{17,25},{25,1},{2,10},{10... | collective-permute-start | bytes 688136 | tf_op jit(solution)/shard_map/ppermute | solution.py:409
  36.3 8.3 %collective-permute-start.15 = (f32[2,112,256]{2,1,0:T(8,128)S(1)}, f32[2,112,256]{2,1,0:T(8,128)S(1)}, u32[]{:S(2)}, u32[]{:S(2)}) collective-permute-start(f32[2,112,256]{2,1,0:T(8,128)S(1)} %get-tuple-element.50), channel_id=1, source_target_pairs={{0,16},{8,24},{16,0},{24,8},{1,17},{9,25},{17,1},{25,9},{2,18},{10... | collective-permute-start | bytes 688136 | tf_op jit(solution)/shard_map/ppermute | solution.py:409
  39.7 11.8 %collective-permute-start.11 = (f32[288,256]{1,0:T(8,128)S(1)}, f32[288,256]{1,0:T(8,128)S(1)}, u32[]{:S(2)}, u32[]{:S(2)}) collective-permute-start(f32[288,256]{1,0:T(8,128)S(1)} %get-tuple-element.45), channel_id=1, source_target_pairs={{0,8},{8,16},{16,24},{24,0},{1,9},{9,17},{17,25},{25,1},{2,10},{10... | collective-permute-start | bytes 884744 | tf_op jit(solution)/shard_map/ppermute | solution.py:409
  40.1 9.3 %collective-permute-start.16 = (f32[2,112,256]{2,1,0:T(8,128)S(1)}, f32[2,112,256]{2,1,0:T(8,128)S(1)}, u32[]{:S(2)}, u32[]{:S(2)}) collective-permute-start(f32[2,112,256]{2,1,0:T(8,128)S(1)} %get-tuple-element.51), channel_id=1, source_target_pairs={{0,24},{8,0},{16,8},{24,16},{1,25},{9,1},{17,9},{25,17},{2,26},{10... | collective-permute-start | bytes 688136 | tf_op jit(solution)/shard_map/ppermute | solution.py:409
  43.3 44.0 %collective-permute-start.6 = (f32[512,256]{1,0:T(8,128)S(1)}, f32[512,256]{1,0:T(8,128)S(1)}, u32[]{:S(2)}, u32[]{:S(2)}) collective-permute-start(f32[512,256]{1,0:T(8,128)S(1)} %get-tuple-element.39), channel_id=1, source_target_pairs={{0,8},{8,16},{16,24},{24,0},{1,9},{9,17},{17,25},{25,1},{2,10},{10... | collective-permute-start | bytes 1572872 | tf_op jit(solution)/shard_map/ppermute | solution.py:409
  43.4 43.9 %collective-permute-start.7 = (f32[512,256]{1,0:T(8,128)S(1)}, f32[512,256]{1,0:T(8,128)S(1)}, u32[]{:S(2)}, u32[]{:S(2)}) collective-permute-start(f32[512,256]{1,0:T(8,128)S(1)} %get-tuple-element.40), channel_id=1, source_target_pairs={{0,16},{8,24},{16,0},{24,8},{1,17},{9,25},{17,1},{25,9},{2,18},{10... | collective-permute-start | bytes 1572872 | tf_op jit(solution)/shard_map/ppermute | solution.py:409
  44.6 42.7 %collective-permute-start.8 = (f32[512,256]{1,0:T(8,128)S(1)}, f32[512,256]{1,0:T(8,128)S(1)}, u32[]{:S(2)}, u32[]{:S(2)}) collective-permute-start(f32[512,256]{1,0:T(8,128)S(1)} %get-tuple-element.41), channel_id=1, source_target_pairs={{0,24},{8,0},{16,8},{24,16},{1,25},{9,1},{17,9},{25,17},{2,26},{10... | collective-permute-start | bytes 1572872 | tf_op jit(solution)/shard_map/ppermute | solution.py:409
  49.3 30.1 %collective-permute-start.12 = (f32[288,256]{1,0:T(8,128)S(1)}, f32[288,256]{1,0:T(8,128)S(1)}, u32[]{:S(2)}, u32[]{:S(2)}) collective-permute-start(f32[288,256]{1,0:T(8,128)S(1)} %get-tuple-element.46), channel_id=1, source_target_pairs={{0,16},{8,24},{16,0},{24,8},{1,17},{9,25},{17,1},{25,9},{2,18},{10... | collective-permute-start | bytes 884744 | tf_op jit(solution)/shard_map/ppermute | solution.py:409
  51.4 33.1 %collective-permute-start.13 = (f32[288,256]{1,0:T(8,128)S(1)}, f32[288,256]{1,0:T(8,128)S(1)}, u32[]{:S(2)}, u32[]{:S(2)}) collective-permute-start(f32[288,256]{1,0:T(8,128)S(1)} %get-tuple-element.47), channel_id=1, source_target_pairs={{0,24},{8,0},{16,8},{24,16},{1,25},{9,1},{17,9},{25,17},{2,26},{10... | collective-permute-start | bytes 884744 | tf_op jit(solution)/shard_map/ppermute | solution.py:409

commit v3 on v2

--- a/solution.py
+++ b/solution.py
@@ -17,7 +17,7 @@
 threshold = 0.5
 
 
-STAGES = (2, 2, 4)
+STAGES = (2, 1, 2, 3)
 CHUNKS = 4
 
 
@@ -25,10 +25,31 @@
     return sum(STAGES[:stage])
 
 
+def both_offsets(stage):
+    ascending = first_of(stage)
+    return sum(STAGES) - ascending - STAGES[stage], ascending
+
+
 def plane_offset(stage, quarter):
-    ascending = first_of(stage)
-    descending = sum(STAGES) - ascending - STAGES[stage]
+    descending, ascending = both_offsets(stage)
     return jnp.where(quarter == 0, descending, ascending)
+
+
+def planes_of(stage):
+    places = []
+    for quarter in range(4):
+        start = RADIUS + sum(STAGES) * quarter + both_offsets(stage)[min(quarter, 1)]
+        places += range(start, start + STAGES[stage])
+    return places
+
+
+def outer_planes():
+    span = 4 * sum(STAGES) + 2 * RADIUS
+    return list(range(RADIUS)) + list(range(span - RADIUS, span))
+
+
+NEAR = outer_planes() + planes_of(0) + planes_of(1)
+FAR = [place for stage in range(2, len(STAGES)) for place in planes_of(stage)]
 
 
 def hat(shape, shift):
@@ -101,16 +122,18 @@
                     code = jnp.broadcast_to(
                         codes[pl.ds(z // CELLS * blocks + i, 1), :], (CELLS, columns)
                     )
-                    void, solid = code < 0.5, code < 1.5
-                value = jnp.where(void, 0.0, jnp.where(solid, 1.0, held[z, row, :]))
+                    fixed, given = code < 1.5, jnp.where(code < 0.5, 0.0, 1.0)
+                value = jnp.where(fixed, given, held[z, row, :])
                 values.append(value)
-                box = value if box is None else box + value
+                change = value - values[z - BOX] if z >= BOX else value
+                box = change if box is None else box + change
+            elif z < planes + RADIUS:
+                box = box - values[z - BOX]
             if z < planes + RADIUS:
-                if z >= BOX:
-                    box = box - values[z - BOX]
                 boxes.append(box)
-                total = box if total is None else total + box
-            if z >= BOX:
+                change = box - boxes[z - BOX] if z >= BOX else box
+                total = change if total is None else total + change
+            else:
                 total = total - boxes[z - BOX]
             conv[z, row, :] = total
         return carry
@@ -119,9 +142,9 @@
         copies[c].wait()
         lax.fori_loop(c * blocks // CHUNKS, (c + 1) * blocks // CHUNKS, tile, 0)
     for k, part in enumerate((slice(0, EDGE), slice(rows - EDGE, rows))):
-        near_edges[k][:RADIUS] = conv[:RADIUS, part, :]
-        near_edges[k][RADIUS:] = conv[planes + RADIUS :, part, :]
-        far_edges[k][...] = conv[RADIUS : planes + RADIUS, part, :]
+        for edge, places in ((near_edges[k], NEAR), (far_edges[k], FAR)):
+            for at, place in enumerate(places):
+                edge[at] = conv[place, part, :]
     kernel = hat((rows - 2 * EDGE, rows), -EDGE).astype(jnp.float32).astype(jnp.bfloat16)
     me = lax.axis_index("gx")
     for distance in range(4):
@@ -138,8 +161,8 @@
     return pl.pallas_call(
         section_kernel,
         out_shape=[f32((span, rows, columns))]
-        + [f32((2 * RADIUS, EDGE, columns))] * 2
-        + [f32((planes, EDGE, columns))] * 2
+        + [f32((len(NEAR), EDGE, columns))] * 2
+        + [f32((len(FAR), EDGE, columns))] * 2
         + [f32((STAGES[0], rows - 2 * EDGE, columns))] * 4,
         in_specs=[pl.BlockSpec(memory_space=pltpu.HBM)] * 2,
         out_specs=vmem(9),
@@ -164,14 +187,14 @@
     return (place != edge).astype(jnp.float32)
 
 
-def edges_kernel(conv, before, after, *outs):
+def edges_kernel(stages, conv, before, after, *outs):
     planes = conv.shape[0] - 2 * RADIUS
     rows = conv.shape[1]
     has_before, has_after = inside("gy", True), inside("gy", False)
-    for stage in range(1, len(STAGES)):
+    for k, stage in enumerate(stages):
         first = first_of(stage) - STAGES[0]
         count = STAGES[stage]
-        higher, lower = outs[2 * stage - 2 : 2 * stage]
+        higher, lower = outs[2 * k : 2 * k + 2]
         for out, start in ((higher, 2 * RADIUS - first - count), (lower, first)):
             at = start if start < RADIUS else start + planes
             out[:, :EDGE, :] = before[start : start + count] * has_before
@@ -179,15 +202,15 @@
             out[:, EDGE + rows :, :] = after[start : start + count] * has_after
 
 
-def edges(conv, before, after):
+def edges(stages, conv, before, after):
     rows, columns = conv.shape[1:]
     shapes = []
-    for stage in range(1, len(STAGES)):
+    for stage in stages:
         shapes += [
             jax.ShapeDtypeStruct((STAGES[stage], rows + 2 * EDGE, columns), jnp.float32)
         ] * 2
     return pl.pallas_call(
-        edges_kernel,
+        functools.partial(edges_kernel, stages),
         out_shape=shapes,
         in_specs=vmem(3),
         out_specs=vmem(len(shapes)),
@@ -218,27 +241,32 @@
         quarter = lax.rem(me + d, 4)
         take_lower = (quarter == 0).astype(jnp.float32) * inside("gz", True)
         take_upper = (quarter == 3).astype(jnp.float32) * inside("gz", False)
-        base = 8 * quarter + plane_offset(stage, quarter)
+        base = RADIUS + 8 * quarter + plane_offset(stage, quarter)
+        if stage == 1:
+            edge = len(NEAR) + count * (quarter - 4)
+        else:
+            edge = 4 * (first_of(stage) - first_of(2)) + count * quarter
         for j in range(count):
             plane = jnp.concatenate(
                 [
-                    before[base + j] * has_before,
-                    conv[RADIUS + base + j],
-                    after[base + j] * has_after,
+                    before[edge + j] * has_before,
+                    conv[base + j],
+                    after[edge + j] * has_after,
                 ],
                 axis=0,
             )
             plane = plane + take_lower * lower[j] + take_upper * upper[j]
             sends[d][j * rows : (j + 1) * rows, :] = along_rows(kernel, plane)
         if stage == 1:
-            base = 8 * quarter + plane_offset(0, quarter)
+            base = RADIUS + 8 * quarter + plane_offset(0, quarter)
+            edge = 2 * RADIUS + STAGES[0] * quarter
             for j in range(STAGES[0]):
                 part = jnp.concatenate(
                     [
-                        before[base + j] * has_before,
-                        conv[RADIUS + base + j, : 2 * EDGE, :],
-                        conv[RADIUS + base + j, rows - 2 * EDGE :, :],
-                        after[base + j] * has_after,
+                        before[edge + j] * has_before,
+                        conv[base + j, : 2 * EDGE, :],
+                        conv[base + j, rows - 2 * EDGE :, :],
+                        after[edge + j] * has_after,
                     ],
                     axis=0,
                 )
@@ -261,19 +289,12 @@
 
 def finish_kernel(stage, *refs):
     aliased = 0 if stage == 0 else 2
-    scale, plane_scale, own, up, across, down = refs[:6]
-    filtered, projected = refs[6 + aliased : 8 + aliased]
-    smooth, sharp, sem = refs[8 + aliased :]
+    scale, plane_scale, weights, own, up, across, down = refs[:7]
+    filtered, projected = refs[7 + aliased : 9 + aliased]
+    smooth, sharp, sem = refs[9 + aliased :]
     columns = own.shape[-1]
     half = columns // 2
     me = lax.axis_index("gx")
-    center = hat((columns, columns), 0)
-    row = lax.broadcasted_iota(jnp.int32, (columns, columns), 0)
-    column = lax.broadcasted_iota(jnp.int32, (columns, columns), 1)
-    place = jnp.where(row < half, row - half, row + half)
-    outer = jnp.maximum(BOX - jnp.abs(place - column), 0)
-    weights = jnp.concatenate([center, center, outer, outer], axis=0)
-    weights = weights.astype(jnp.float32).astype(jnp.bfloat16)
     top = jnp.tanh(jnp.float32(sharpness * threshold))
     inverse = 1.0 / (top + jnp.tanh(jnp.float32(sharpness * (1.0 - threshold))))
 
@@ -285,16 +306,14 @@
             block = lax.rem(me + 3 + r, 4)
             has_before = (block != 0).astype(jnp.float32)
             has_after = (block != 3).astype(jnp.float32)
-            outer_values = jnp.concatenate(
-                [
-                    values[(r + 3) % 4][:, half:] * has_before,
-                    values[(r + 1) % 4][:, :half] * has_after,
-                ],
-                axis=1,
+            outer_values = jnp.where(
+                lax.broadcasted_iota(jnp.int32, (values[r].shape[0], half), 1) < half // 2,
+                values[(r + 1) % 4][:, :half] * has_after,
+                values[(r + 3) % 4][:, half:] * has_before,
             )
             parts = two_parts(values[r]) + two_parts(outer_values)
             summed = jnp.dot(
-                jnp.concatenate(parts, axis=1), weights, preferred_element_type=jnp.float32
+                jnp.concatenate(parts, axis=1), weights[...], preferred_element_type=jnp.float32
             )
             lanes = pl.ds(pl.multiple_of(block * columns, columns), columns)
             smoothed = summed * (scale[scale_rows, lanes] * plane_factor)
@@ -341,7 +360,7 @@
         copy.wait()
 
 
-def finish(stage, scale, plane_scale, received, results):
+def finish(stage, scale, plane_scale, weights, received, results):
     rows, width = scale.shape
     whole = jax.ShapeDtypeStruct((plane_scale.shape[0], rows, width), jnp.float32)
     count = received[0].size // received[0].shape[-1]
@@ -349,7 +368,7 @@
     return pl.pallas_call(
         functools.partial(finish_kernel, stage),
         out_shape=[whole, whole],
-        in_specs=vmem(6)
+        in_specs=vmem(7)
         + [pl.BlockSpec(memory_space=pl.ANY)] * len(results),
         out_specs=[pl.BlockSpec(memory_space=pl.ANY)] * 2,
         scratch_shapes=[
@@ -357,10 +376,10 @@
             pltpu.VMEM((count, width), jnp.float32),
             pltpu.SemaphoreType.DMA((copies,)),
         ],
-        input_output_aliases={6: 0, 7: 1} if results else {},
+        input_output_aliases={7: 0, 8: 1} if results else {},
         compiler_params=params(20),
         cost_estimate=cost(40_000_000),
-    )(scale, plane_scale, *received, *results)
+    )(scale, plane_scale, weights, *received, *results)
 
 
 def one_side(reach):
@@ -373,7 +392,7 @@
     return (RADIUS + 1 + one_side(reach_left) + one_side(reach_right)).astype(jnp.float32)
 
 
-def scale_kernel(scale, plane_scale):
+def scale_kernel(scale, plane_scale, weights):
     rows, width = scale.shape
     layers = plane_scale.shape[0]
     row = lax.axis_index("gy") * rows + lax.broadcasted_iota(jnp.int32, (rows, 128), 0)
@@ -387,6 +406,17 @@
     plane_scale[...] = 1.0 / edge_sums(
         plane, layers * lax.axis_size("gx") * lax.axis_size("gz")
     )
+    columns = weights.shape[1]
+    half = columns // 2
+    center = hat((columns, columns), 0)
+    row = lax.broadcasted_iota(jnp.int32, (half, columns), 0)
+    column = lax.broadcasted_iota(jnp.int32, (half, columns), 1)
+    place = jnp.where(row < half // 2, row + columns, row - half)
+    outer = jnp.maximum(BOX - jnp.abs(place - column), 0)
+    at = 0
+    for part in (center, center, outer, outer):
+        weights[at : at + part.shape[0], :] = part.astype(jnp.float32).astype(jnp.bfloat16)
+        at += part.shape[0]
 
 
 def scales(rows, width, columns, layers):
@@ -395,8 +425,9 @@
         out_shape=[
             jax.ShapeDtypeStruct((rows, width), jnp.float32),
             jax.ShapeDtypeStruct((layers, columns), jnp.float32),
+            jax.ShapeDtypeStruct((3 * columns, columns), jnp.bfloat16),
         ],
-        out_specs=vmem(2),
+        out_specs=vmem(3),
         compiler_params=params(4),
         cost_estimate=cost(5_000_000),
         name="scales",
@@ -420,21 +451,21 @@
     width = columns * groups
     conv, near_first, near_last, far_first, far_last, *sends = section(density, mask)
     received = [around(sends)]
-    near_before = shifted(near_last, "gy", 1)
-    near_after = shifted(near_first, "gy", -1)
-    before = shifted(far_last, "gy", 1)
-    after = shifted(far_first, "gy", -1)
-    outgoing = edges(conv, near_before, near_after)
-    scale, plane_scale = scales(row_count, width, columns, layers)
+    near = (shifted(near_last, "gy", 1), shifted(near_first, "gy", -1))
+    far = (shifted(far_last, "gy", 1), shifted(far_first, "gy", -1))
+    outgoing = edges((1,), conv, *near)
+    outgoing += edges(tuple(range(2, len(STAGES))), conv, *near)
     halos = []
     for k in range(len(STAGES) - 1):
         halos.append((shifted(outgoing[2 * k], "gz", 1), shifted(outgoing[2 * k + 1], "gz", -1)))
+    tables = scales(row_count, width, columns, layers)
     for stage in range(1, len(STAGES)):
-        sends = stage_sends(stage, conv, before, after, *halos[stage - 1])
+        ends = near if stage == 1 else far
+        sends = stage_sends(stage, conv, *ends, *halos[stage - 1])
         received.append(around(sends))
     results = []
     for stage in range(len(STAGES)):
-        results = finish(stage, scale, plane_scale, received[stage], results)
+        results = finish(stage, *tables, received[stage], results)
     return tuple(results)
 
 

time: 90.3 us -> 86.8 us (0.961)
  the two profiles are of different devices: /device:TPU:1 before, /device:TPU:17 now
where the time goes in v3:
time: 86.8 us; the launch traced here: 86.7 us
  waiting for transfers between devices  42.8 us (49%)
  starting transfers between devices  30.4 us (35%)
  Pallas kernels  12.6 us (15%)
  between operations  0.93 us (1%)
    ppermute x22, waiting for transfers between devices, shifted(): return lax.ppermute(block, axis, route)  42.8 us
    ppermute x22, starting transfers between devices, shifted(): return lax.ppermute(block, axis, route)  30.4 us
    pallas_call x4, Pallas kernels, finish(): pl.pallas_call(functools.partial(finish_kernel, stage), out_shape=[whole,...  7.67 us
    pallas_call x1, Pallas kernels, section(): pl.pallas_call(section_kernel, out_shape=[f32((span, rows, columns))] + [...  2.95 us
  transfers between devices with their start and end apart: 22, of which 9 were waited for; matrix products, arithmetic and copies ran while one was open for 0% of the time, Pallas kernels for 9%

profile of v3, /device:TPU:17, one launch (start us, length us, event | category | flops | bytes accessed | tf_op | source)
XLA Modules:
  0.0 86.7 jit_solution(8227439203100016588)
XLA Ops:
  0.6 3.0 %section.1 = (f32[44,128,256]{2,1,0:T(8,128)S(1)}, f32[24,8,256]{2,1,0:T(8,128)S(1)}, f32[24,8,256]{2,1,0:T(8,128)S(1)}, f32[20,8,256]{2,1,0:T(8,128)S(1)}, f32[...) custom-call(f32[32,128,256]{2,1,0:T(8,128)} %density.1, ...), custom_call_target="tpu_custom_call" | custom-call | flops 40000000 | bytes 8388608 | tf_op jit(solution)/shard_map/section/pallas_call | solution.py:161
  3.6 1.6 %collective-permute-start.2 = (f32[24,8,256]{2,1,0:T(8,128)S(1)}, f32[24,8,256]{2,1,0:T(8,128)S(1)}, u32[]{:S(2)}, u32[]{:S(2)}) collective-permute-start(f32[24,8,256]{2,1,0:T(8,128)S(1)} %get-tuple-element.44), channel_id=1, source_target_pairs={{0,1},{1,2},{2,3},{3,4},{4,5},{5,6},{6,7},{7,0},{8,9},{9,10},{10,1... | collective-permute-start | bytes 589832 | tf_op jit(solution)/shard_map/ppermute | solution.py:440
  5.2 1.7 %collective-permute-start = (f32[20,8,256]{2,1,0:T(8,128)S(1)}, f32[20,8,256]{2,1,0:T(8,128)S(1)}, u32[]{:S(2)}, u32[]{:S(2)}) collective-permute-start(f32[20,8,256]{2,1,0:T(8,128)S(1)} %get-tuple-element.42), channel_id=1, source_target_pairs={{0,1},{1,2},{2,3},{3,4},{4,5},{5,6},{6,7},{7,0},{8,9},{9,10},{10,1... | collective-permute-start | bytes 491528 | tf_op jit(solution)/shard_map/ppermute | solution.py:440
  6.9 1.2 %collective-permute-start.19 = (f32[2,112,256]{2,1,0:T(8,128)S(1)}, f32[2,112,256]{2,1,0:T(8,128)S(1)}, u32[]{:S(2)}, u32[]{:S(2)}) collective-permute-start(f32[2,112,256]{2,1,0:T(8,128)S(1)} %get-tuple-element.65), channel_id=1, source_target_pairs={{0,8},{8,16},{16,24},{24,0},{1,9},{9,17},{17,25},{25,1},{2,10},{10... | collective-permute-start | bytes 688136 | tf_op jit(solution)/shard_map/ppermute | solution.py:440
  8.1 2.4 %collective-permute-start.20 = (f32[2,112,256]{2,1,0:T(8,128)S(1)}, f32[2,112,256]{2,1,0:T(8,128)S(1)}, u32[]{:S(2)}, u32[]{:S(2)}) collective-permute-start(f32[2,112,256]{2,1,0:T(8,128)S(1)} %get-tuple-element.66), channel_id=1, source_target_pairs={{0,16},{8,24},{16,0},{24,8},{1,17},{9,25},{17,1},{25,9},{2,18},{10... | collective-permute-start | bytes 688136 | tf_op jit(solution)/shard_map/ppermute | solution.py:440
  10.7 1.7 %collective-permute-start.4 = (f32[3,144,256]{2,1,0:T(8,128)S(1)}, f32[3,144,256]{2,1,0:T(8,128)S(1)}, u32[]{:S(2)}, u32[]{:S(2)}) collective-permute-start(f32[3,144,256]{2,1,0:T(8,128)S(1)} %get-tuple-element.46), channel_id=1, source_target_pairs={{0,32},{32,64},{64,96},{96,128},{128,160},{160,192},{192,224},{224... | collective-permute-start | bytes 1327112 | tf_op jit(solution)/shard_map/ppermute | solution.py:440
  12.4 1.7 %collective-permute-start.14 = (f32[1,144,256]{2,1,0:T(8,128)S(1)}, f32[1,144,256]{2,1,0:T(8,128)S(1)}, u32[]{:S(2)}, u32[]{:S(2)}) collective-permute-start(f32[1,144,256]{2,1,0:T(8,128)S(1)} %get-tuple-element.58), channel_id=1, source_target_pairs={{0,32},{32,64},{64,96},{96,128},{128,160},{160,192},{192,224},{224... | collective-permute-start | bytes 442376 | tf_op jit(solution)/shard_map/ppermute | solution.py:440
  14.2 1.2 %collective-permute-done.1.after = f32[20,8,256]{2,1,0:T(8,128)S(1)} collective-permute-done((f32[20,8,256]{2,1,0:T(8,128)S(1)}, f32[20,8,256]{2,1,0:T(8,128)S(1)}, u32[]{:S(2)}, u32[]{:S(2)}) %collective-permute-start.1) | collective-permute-done | bytes 163872 | tf_op jit(solution)/shard_map/ppermute | solution.py:440
  15.3 5.9 %collective-permute-start.5 = (f32[3,144,256]{2,1,0:T(8,128)S(1)}, f32[3,144,256]{2,1,0:T(8,128)S(1)}, u32[]{:S(2)}, u32[]{:S(2)}) collective-permute-start(f32[3,144,256]{2,1,0:T(8,128)S(1)} %get-tuple-element.47), channel_id=1, source_target_pairs={{0,224},{32,0},{64,32},{96,64},{128,96},{160,128},{192,160},{224,1... | collective-permute-start | bytes 1327112 | tf_op jit(solution)/shard_map/ppermute | solution.py:440
  21.2 5.3 %collective-permute-start.10 = (f32[2,144,256]{2,1,0:T(8,128)S(1)}, f32[2,144,256]{2,1,0:T(8,128)S(1)}, u32[]{:S(2)}, u32[]{:S(2)}) collective-permute-start(f32[2,144,256]{2,1,0:T(8,128)S(1)} %get-tuple-element.53), channel_id=1, source_target_pairs={{0,224},{32,0},{64,32},{96,64},{128,96},{160,128},{192,160},{224,1... | collective-permute-start | bytes 884744 | tf_op jit(solution)/shard_map/ppermute | solution.py:440
  26.5 2.7 %collective-permute-done.14.lower = f32[1,144,256]{2,1,0:T(8,128)S(1)} collective-permute-done((f32[1,144,256]{2,1,0:T(8,128)S(1)}, f32[1,144,256]{2,1,0:T(8,128)S(1)}, u32[]{:S(2)}, u32[]{:S(2)}) %collective-permute-start.14) | collective-permute-done | bytes 147488 | tf_op jit(solution)/shard_map/ppermute | solution.py:440
  29.2 1.2 %collective-permute-start.15 = (f32[1,144,256]{2,1,0:T(8,128)S(1)}, f32[1,144,256]{2,1,0:T(8,128)S(1)}, u32[]{:S(2)}, u32[]{:S(2)}) collective-permute-start(f32[1,144,256]{2,1,0:T(8,128)S(1)} %get-tuple-element.59), channel_id=1, source_target_pairs={{0,224},{32,0},{64,32},{96,64},{128,96},{160,128},{192,160},{224,1... | collective-permute-start | bytes 442376 | tf_op jit(solution)/shard_map/ppermute | solution.py:440
  30.4 9.4 %collective-permute-done.15.upper = f32[1,144,256]{2,1,0:T(8,128)S(1)} collective-permute-done((f32[1,144,256]{2,1,0:T(8,128)S(1)}, f32[1,144,256]{2,1,0:T(8,128)S(1)}, u32[]{:S(2)}, u32[]{:S(2)}) %collective-permute-start.15) | collective-permute-done | bytes 147488 | tf_op jit(solution)/shard_map/ppermute | solution.py:440
  39.8 1.1 %collective-permute-start.21 = (f32[2,112,256]{2,1,0:T(8,128)S(1)}, f32[2,112,256]{2,1,0:T(8,128)S(1)}, u32[]{:S(2)}, u32[]{:S(2)}) collective-permute-start(f32[2,112,256]{2,1,0:T(8,128)S(1)} %get-tuple-element.67), channel_id=1, source_target_pairs={{0,24},{8,0},{16,8},{24,16},{1,25},{9,1},{17,9},{25,17},{2,26},{10... | collective-permute-start | bytes 688136 | tf_op jit(solution)/shard_map/ppermute | solution.py:440
  40.9 0.4 shard_map.43
  41.8 0.9 %collective-permute-start.17 = (f32[160,256]{1,0:T(8,128)S(1)}, f32[160,256]{1,0:T(8,128)S(1)}, u32[]{:S(2)}, u32[]{:S(2)}) collective-permute-start(f32[160,256]{1,0:T(8,128)S(1)} %get-tuple-element.62), channel_id=1, source_target_pairs={{0,16},{8,24},{16,0},{24,8},{1,17},{9,25},{17,1},{25,9},{2,18},{10... | collective-permute-start | bytes 491528 | tf_op jit(solution)/shard_map/ppermute | solution.py:440
  42.6 0.5 shard_map.42
  43.2 2.1 %collective-permute-start.11 = (f32[256,256]{1,0:T(8,128)S(1)}, f32[256,256]{1,0:T(8,128)S(1)}, u32[]{:S(2)}, u32[]{:S(2)}) collective-permute-start(f32[256,256]{1,0:T(8,128)S(1)} %get-tuple-element.55), channel_id=1, source_target_pairs={{0,8},{8,16},{16,24},{24,0},{1,9},{9,17},{17,25},{25,1},{2,10},{10... | collective-permute-start | bytes 786440 | tf_op jit(solution)/shard_map/ppermute | solution.py:440
  45.3 0.6 collective-permute-start.18
  45.9 0.7 shard_map.41
  46.7 0.7 collective-permute-done.21.refs_6_
  47.8 4.3 %collective-permute-done.16.refs_4_ = f32[160,256]{1,0:T(8,128)S(1)} collective-permute-done((f32[160,256]{1,0:T(8,128)S(1)}, f32[160,256]{1,0:T(8,128)S(1)}, u32[]{:S(2)}, u32[]{:S(2)}) %collective-permute-start.16) | collective-permute-done | bytes 163872 | tf_op jit(solution)/shard_map/ppermute | solution.py:440
  52.1 1.2 %collective-permute-start.8 = (f32[384,256]{1,0:T(8,128)S(1)}, f32[384,256]{1,0:T(8,128)S(1)}, u32[]{:S(2)}, u32[]{:S(2)}) collective-permute-start(f32[384,256]{1,0:T(8,128)S(1)} %get-tuple-element.51), channel_id=1, source_target_pairs={{0,24},{8,0},{16,8},{24,16},{1,25},{9,1},{17,9},{25,17},{2,26},{10... | collective-permute-start | bytes 1179656 | tf_op jit(solution)/shard_map/ppermute | solution.py:440
  53.3 1.2 %collective-permute-done.18.refs_6_ = f32[160,256]{1,0:T(8,128)S(1)} collective-permute-done((f32[160,256]{1,0:T(8,128)S(1)}, f32[160,256]{1,0:T(8,128)S(1)}, u32[]{:S(2)}, u32[]{:S(2)}) %collective-permute-start.18) | collective-permute-done | bytes 163872 | tf_op jit(solution)/shard_map/ppermute | solution.py:440
  54.4 0.9 %collective-permute-start.12 = (f32[256,256]{1,0:T(8,128)S(1)}, f32[256,256]{1,0:T(8,128)S(1)}, u32[]{:S(2)}, u32[]{:S(2)}) collective-permute-start(f32[256,256]{1,0:T(8,128)S(1)} %get-tuple-element.56), channel_id=1, source_target_pairs={{0,16},{8,24},{16,0},{24,8},{1,17},{9,25},{17,1},{25,9},{2,18},{10... | collective-permute-start | bytes 786440 | tf_op jit(solution)/shard_map/ppermute | solution.py:440
  55.3 2.4 %collective-permute-done.11.refs_4_ = f32[256,256]{1,0:T(8,128)S(1)} collective-permute-done((f32[256,256]{1,0:T(8,128)S(1)}, f32[256,256]{1,0:T(8,128)S(1)}, u32[]{:S(2)}, u32[]{:S(2)}) %collective-permute-start.11) | collective-permute-done | bytes 262176 | tf_op jit(solution)/shard_map/ppermute | solution.py:440
  58.0 1.7 %shard_map.44 = (f32[8,128,1024]{2,1,0:T(8,128)}, f32[8,128,1024]{2,1,0:T(8,128)}) custom-call(f32[128,1024]{1,0:T(8,128)S(1)} %get-tuple-element.38.refs_0_, f32[8,256]{1,0:T(8,128)S(1)} %get-tuple-element.39.refs_1_, bf16[768,256]{1,0:T(8,128)(2,1)S(1)} %get-tuple-element.40.refs_2_, f32[2,112,256]{2,1,0:T(8,128)S(1)} %get-tuple-element.64.refs_3_, ...), custom_call_target="tpu_custom_call" | custom-call | flops 40000000 | bytes 8388608 | tf_op jit(solution)/shard_map/pallas_call | solution.py:368
  59.7 1.9 %shard_map.45 = (f32[8,128,1024]{2,1,0:T(8,128)}, f32[8,128,1024]{2,1,0:T(8,128)}) custom-call(f32[128,1024]{1,0:T(8,128)S(1)} %get-tuple-element.38.refs_0_, f32[8,256]{1,0:T(8,128)S(1)} %get-tuple-element.39.refs_1_, bf16[768,256]{1,0:T(8,128)(2,1)S(1)} %get-tuple-element.40.refs_2_, ...), custom_call_target="tpu_custom_call", output_to_operand_aliasing={{0}: (7, {}), {1}: (8, {})} | custom-call | flops 40000000 | bytes 8388608 | tf_op jit(solution)/shard_map/pallas_call | solution.py:368
  61.6 17.4 %collective-permute-done.12.refs_5_ = f32[256,256]{1,0:T(8,128)S(1)} collective-permute-done((f32[256,256]{1,0:T(8,128)S(1)}, f32[256,256]{1,0:T(8,128)S(1)}, u32[]{:S(2)}, u32[]{:S(2)}) %collective-permute-start.12) | collective-permute-done | bytes 262176 | tf_op jit(solution)/shard_map/ppermute | solution.py:440
  79.0 3.5 %collective-permute-done.13.refs_6_ = f32[256,256]{1,0:T(8,128)S(1)} collective-permute-done((f32[256,256]{1,0:T(8,128)S(1)}, f32[256,256]{1,0:T(8,128)S(1)}, u32[]{:S(2)}, u32[]{:S(2)}) %collective-permute-start.13) | collective-permute-done | bytes 262176 | tf_op jit(solution)/shard_map/ppermute | solution.py:440
  82.5 1.8 %shard_map.46 = (f32[8,128,1024]{2,1,0:T(8,128)}, f32[8,128,1024]{2,1,0:T(8,128)}) custom-call(f32[128,1024]{1,0:T(8,128)S(1)} %get-tuple-element.38.refs_0_, f32[8,256]{1,0:T(8,128)S(1)} %get-tuple-element.39.refs_1_, bf16[768,256]{1,0:T(8,128)(2,1)S(1)} %get-tuple-element.40.refs_2_, ...), custom_call_target="tpu_custom_call", output_to_operand_aliasing={{0}: (7, {}), {1}: (8, {})} | custom-call | flops 40000000 | bytes 8388608 | tf_op jit(solution)/shard_map/pallas_call | solution.py:368
  84.4 2.2 %shard_map.47 = (f32[8,128,1024]{2,1,0:T(8,128)}, f32[8,128,1024]{2,1,0:T(8,128)}) custom-call(f32[128,1024]{1,0:T(8,128)S(1)} %get-tuple-element.38.refs_0_, f32[8,256]{1,0:T(8,128)S(1)} %get-tuple-element.39.refs_1_, bf16[768,256]{1,0:T(8,128)(2,1)S(1)} %get-tuple-element.40.refs_2_, ...), custom_call_target="tpu_custom_call", output_to_operand_aliasing={{0}: (7, {}), {1}: (8, {})} | custom-call | flops 40000000 | bytes 8388608 | tf_op jit(solution)/shard_map/pallas_call | solution.py:368
  (23 shorter events, 1.2 us)
Async XLA Ops:
  3.6 7.0 %collective-permute-start.2 = (f32[24,8,256]{2,1,0:T(8,128)S(1)}, f32[24,8,256]{2,1,0:T(8,128)S(1)}, u32[]{:S(2)}, u32[]{:S(2)}) collective-permute-start(f32[24,8,256]{2,1,0:T(8,128)S(1)} %get-tuple-element.44), channel_id=1, source_target_pairs={{0,1},{1,2},{2,3},{3,4},{4,5},{5,6},{6,7},{7,0},{8,9},{9,10},{10,1... | collective-permute-start | bytes 589832 | tf_op jit(solution)/shard_map/ppermute | solution.py:440
  5.2 5.4 %collective-permute-start.3 = (f32[24,8,256]{2,1,0:T(8,128)S(1)}, f32[24,8,256]{2,1,0:T(8,128)S(1)}, u32[]{:S(2)}, u32[]{:S(2)}) collective-permute-start(f32[24,8,256]{2,1,0:T(8,128)S(1)} %get-tuple-element.45), channel_id=1, source_target_pairs={{0,7},{1,0},{2,1},{3,2},{4,3},{5,4},{6,5},{7,6},{8,15},{9,8},{10,9... | collective-permute-start | bytes 589832 | tf_op jit(solution)/shard_map/ppermute | solution.py:440
  5.2 7.3 %collective-permute-start = (f32[20,8,256]{2,1,0:T(8,128)S(1)}, f32[20,8,256]{2,1,0:T(8,128)S(1)}, u32[]{:S(2)}, u32[]{:S(2)}) collective-permute-start(f32[20,8,256]{2,1,0:T(8,128)S(1)} %get-tuple-element.42), channel_id=1, source_target_pairs={{0,1},{1,2},{2,3},{3,4},{4,5},{5,6},{6,7},{7,0},{8,9},{9,10},{10,1... | collective-permute-start | bytes 491528 | tf_op jit(solution)/shard_map/ppermute | solution.py:440
  6.9 14.3 %collective-permute-start.19 = (f32[2,112,256]{2,1,0:T(8,128)S(1)}, f32[2,112,256]{2,1,0:T(8,128)S(1)}, u32[]{:S(2)}, u32[]{:S(2)}) collective-permute-start(f32[2,112,256]{2,1,0:T(8,128)S(1)} %get-tuple-element.65), channel_id=1, source_target_pairs={{0,8},{8,16},{16,24},{24,0},{1,9},{9,17},{17,25},{25,1},{2,10},{10... | collective-permute-start | bytes 688136 | tf_op jit(solution)/shard_map/ppermute | solution.py:440
  8.1 13.1 %collective-permute-start.20 = (f32[2,112,256]{2,1,0:T(8,128)S(1)}, f32[2,112,256]{2,1,0:T(8,128)S(1)}, u32[]{:S(2)}, u32[]{:S(2)}) collective-permute-start(f32[2,112,256]{2,1,0:T(8,128)S(1)} %get-tuple-element.66), channel_id=1, source_target_pairs={{0,16},{8,24},{16,0},{24,8},{1,17},{9,25},{17,1},{25,9},{2,18},{10... | collective-permute-start | bytes 688136 | tf_op jit(solution)/shard_map/ppermute | solution.py:440
  10.6 4.7 %collective-permute-start.1 = (f32[20,8,256]{2,1,0:T(8,128)S(1)}, f32[20,8,256]{2,1,0:T(8,128)S(1)}, u32[]{:S(2)}, u32[]{:S(2)}) collective-permute-start(f32[20,8,256]{2,1,0:T(8,128)S(1)} %get-tuple-element.43), channel_id=1, source_target_pairs={{0,7},{1,0},{2,1},{3,2},{4,3},{5,4},{6,5},{7,6},{8,15},{9,8},{10,9... | collective-permute-start | bytes 491528 | tf_op jit(solution)/shard_map/ppermute | solution.py:440
  10.7 32.5 %collective-permute-start.4 = (f32[3,144,256]{2,1,0:T(8,128)S(1)}, f32[3,144,256]{2,1,0:T(8,128)S(1)}, u32[]{:S(2)}, u32[]{:S(2)}) collective-permute-start(f32[3,144,256]{2,1,0:T(8,128)S(1)} %get-tuple-element.46), channel_id=1, source_target_pairs={{0,32},{32,64},{64,96},{96,128},{128,160},{160,192},{192,224},{224... | collective-permute-start | bytes 1327112 | tf_op jit(solution)/shard_map/ppermute | solution.py:440
  12.4 16.8 %collective-permute-start.14 = (f32[1,144,256]{2,1,0:T(8,128)S(1)}, f32[1,144,256]{2,1,0:T(8,128)S(1)}, u32[]{:S(2)}, u32[]{:S(2)}) collective-permute-start(f32[1,144,256]{2,1,0:T(8,128)S(1)} %get-tuple-element.58), channel_id=1, source_target_pairs={{0,32},{32,64},{64,96},{96,128},{128,160},{160,192},{192,224},{224... | collective-permute-start | bytes 442376 | tf_op jit(solution)/shard_map/ppermute | solution.py:440
  15.3 30.0 %collective-permute-start.5 = (f32[3,144,256]{2,1,0:T(8,128)S(1)}, f32[3,144,256]{2,1,0:T(8,128)S(1)}, u32[]{:S(2)}, u32[]{:S(2)}) collective-permute-start(f32[3,144,256]{2,1,0:T(8,128)S(1)} %get-tuple-element.47), channel_id=1, source_target_pairs={{0,224},{32,0},{64,32},{96,64},{128,96},{160,128},{192,160},{224,1... | collective-permute-start | bytes 1327112 | tf_op jit(solution)/shard_map/ppermute | solution.py:440
  21.2 20.1 %collective-permute-start.9 = (f32[2,144,256]{2,1,0:T(8,128)S(1)}, f32[2,144,256]{2,1,0:T(8,128)S(1)}, u32[]{:S(2)}, u32[]{:S(2)}) collective-permute-start(f32[2,144,256]{2,1,0:T(8,128)S(1)} %get-tuple-element.52), channel_id=1, source_target_pairs={{0,32},{32,64},{64,96},{96,128},{128,160},{160,192},{192,224},{224... | collective-permute-start | bytes 884744 | tf_op jit(solution)/shard_map/ppermute | solution.py:440
  21.2 20.5 %collective-permute-start.10 = (f32[2,144,256]{2,1,0:T(8,128)S(1)}, f32[2,144,256]{2,1,0:T(8,128)S(1)}, u32[]{:S(2)}, u32[]{:S(2)}) collective-permute-start(f32[2,144,256]{2,1,0:T(8,128)S(1)} %get-tuple-element.53), channel_id=1, source_target_pairs={{0,224},{32,0},{64,32},{96,64},{128,96},{160,128},{192,160},{224,1... | collective-permute-start | bytes 884744 | tf_op jit(solution)/shard_map/ppermute | solution.py:440
  29.2 10.6 %collective-permute-start.15 = (f32[1,144,256]{2,1,0:T(8,128)S(1)}, f32[1,144,256]{2,1,0:T(8,128)S(1)}, u32[]{:S(2)}, u32[]{:S(2)}) collective-permute-start(f32[1,144,256]{2,1,0:T(8,128)S(1)} %get-tuple-element.59), channel_id=1, source_target_pairs={{0,224},{32,0},{64,32},{96,64},{128,96},{160,128},{192,160},{224,1... | collective-permute-start | bytes 442376 | tf_op jit(solution)/shard_map/ppermute | solution.py:440
  39.8 7.6 %collective-permute-start.21 = (f32[2,112,256]{2,1,0:T(8,128)S(1)}, f32[2,112,256]{2,1,0:T(8,128)S(1)}, u32[]{:S(2)}, u32[]{:S(2)}) collective-permute-start(f32[2,112,256]{2,1,0:T(8,128)S(1)} %get-tuple-element.67), channel_id=1, source_target_pairs={{0,24},{8,0},{16,8},{24,16},{1,25},{9,1},{17,9},{25,17},{2,26},{10... | collective-permute-start | bytes 688136 | tf_op jit(solution)/shard_map/ppermute | solution.py:440
  41.4 10.8 %collective-permute-start.16 = (f32[160,256]{1,0:T(8,128)S(1)}, f32[160,256]{1,0:T(8,128)S(1)}, u32[]{:S(2)}, u32[]{:S(2)}) collective-permute-start(f32[160,256]{1,0:T(8,128)S(1)} %get-tuple-element.61), channel_id=1, source_target_pairs={{0,8},{8,16},{16,24},{24,0},{1,9},{9,17},{17,25},{25,1},{2,10},{10... | collective-permute-start | bytes 491528 | tf_op jit(solution)/shard_map/ppermute | solution.py:440
  41.8 10.4 %collective-permute-start.17 = (f32[160,256]{1,0:T(8,128)S(1)}, f32[160,256]{1,0:T(8,128)S(1)}, u32[]{:S(2)}, u32[]{:S(2)}) collective-permute-start(f32[160,256]{1,0:T(8,128)S(1)} %get-tuple-element.62), channel_id=1, source_target_pairs={{0,16},{8,24},{16,0},{24,8},{1,17},{9,25},{17,1},{25,9},{2,18},{10... | collective-permute-start | bytes 491528 | tf_op jit(solution)/shard_map/ppermute | solution.py:440
  43.2 14.6 %collective-permute-start.11 = (f32[256,256]{1,0:T(8,128)S(1)}, f32[256,256]{1,0:T(8,128)S(1)}, u32[]{:S(2)}, u32[]{:S(2)}) collective-permute-start(f32[256,256]{1,0:T(8,128)S(1)} %get-tuple-element.55), channel_id=1, source_target_pairs={{0,8},{8,16},{16,24},{24,0},{1,9},{9,17},{17,25},{25,1},{2,10},{10... | collective-permute-start | bytes 786440 | tf_op jit(solution)/shard_map/ppermute | solution.py:440
  45.3 9.1 %collective-permute-start.18 = (f32[160,256]{1,0:T(8,128)S(1)}, f32[160,256]{1,0:T(8,128)S(1)}, u32[]{:S(2)}, u32[]{:S(2)}) collective-permute-start(f32[160,256]{1,0:T(8,128)S(1)} %get-tuple-element.63), channel_id=1, source_target_pairs={{0,24},{8,0},{16,8},{24,16},{1,25},{9,1},{17,9},{25,17},{2,26},{10... | collective-permute-start | bytes 491528 | tf_op jit(solution)/shard_map/ppermute | solution.py:440
  47.4 36.9 %collective-permute-start.6 = (f32[384,256]{1,0:T(8,128)S(1)}, f32[384,256]{1,0:T(8,128)S(1)}, u32[]{:S(2)}, u32[]{:S(2)}) collective-permute-start(f32[384,256]{1,0:T(8,128)S(1)} %get-tuple-element.49), channel_id=1, source_target_pairs={{0,8},{8,16},{16,24},{24,0},{1,9},{9,17},{17,25},{25,1},{2,10},{10... | collective-permute-start | bytes 1179656 | tf_op jit(solution)/shard_map/ppermute | solution.py:440
  52.1 32.2 %collective-permute-start.7 = (f32[384,256]{1,0:T(8,128)S(1)}, f32[384,256]{1,0:T(8,128)S(1)}, u32[]{:S(2)}, u32[]{:S(2)}) collective-permute-start(f32[384,256]{1,0:T(8,128)S(1)} %get-tuple-element.50), channel_id=1, source_target_pairs={{0,16},{8,24},{16,0},{24,8},{1,17},{9,25},{17,1},{25,9},{2,18},{10... | collective-permute-start | bytes 1179656 | tf_op jit(solution)/shard_map/ppermute | solution.py:440
  52.1 32.2 %collective-permute-start.8 = (f32[384,256]{1,0:T(8,128)S(1)}, f32[384,256]{1,0:T(8,128)S(1)}, u32[]{:S(2)}, u32[]{:S(2)}) collective-permute-start(f32[384,256]{1,0:T(8,128)S(1)} %get-tuple-element.51), channel_id=1, source_target_pairs={{0,24},{8,0},{16,8},{24,16},{1,25},{9,1},{17,9},{25,17},{2,26},{10... | collective-permute-start | bytes 1179656 | tf_op jit(solution)/shard_map/ppermute | solution.py:440
  54.4 24.6 %collective-permute-start.12 = (f32[256,256]{1,0:T(8,128)S(1)}, f32[256,256]{1,0:T(8,128)S(1)}, u32[]{:S(2)}, u32[]{:S(2)}) collective-permute-start(f32[256,256]{1,0:T(8,128)S(1)} %get-tuple-element.56), channel_id=1, source_target_pairs={{0,16},{8,24},{16,0},{24,8},{1,17},{9,25},{17,1},{25,9},{2,18},{10... | collective-permute-start | bytes 786440 | tf_op jit(solution)/shard_map/ppermute | solution.py:440
  57.7 24.8 %collective-permute-start.13 = (f32[256,256]{1,0:T(8,128)S(1)}, f32[256,256]{1,0:T(8,128)S(1)}, u32[]{:S(2)}, u32[]{:S(2)}) collective-permute-start(f32[256,256]{1,0:T(8,128)S(1)} %get-tuple-element.57), channel_id=1, source_target_pairs={{0,24},{8,0},{16,8},{24,16},{1,25},{9,1},{17,9},{25,17},{2,26},{10... | collective-permute-start | bytes 786440 | tf_op jit(solution)/shard_map/ppermute | solution.py:440

commit v4 on v3

v4 whole, which is shorter than its diff:
```python
import functools

import jax
import jax.numpy as jnp
from jax import lax
from jax.experimental import pallas as pl
from jax.experimental.pallas import tpu as pltpu
from jax.sharding import PartitionSpec as P


RADIUS = 6
CELLS = 8
EDGE = 8
BOX = RADIUS + 1

sharpness = 8.0
threshold = 0.5


STAGES = (2, 2, 2, 2)
GROUPS = ((0, 1), (2,))
CHUNKS = 4


def first_of(stage):
    return sum(STAGES[:stage])


def both_offsets(stage):
    ascending = first_of(stage)
    return sum(STAGES) - ascending - STAGES[stage], ascending


def plane_offset(stage, quarter):
    descending, ascending = both_offsets(stage)
    return jnp.where(quarter == 0, descending, ascending)


def outer_places():
    span = 4 * sum(STAGES) + 2 * RADIUS
    places = {}
    for stage in range(1, len(STAGES)):
        first = first_of(stage) - STAGES[0]
        for j in range(STAGES[stage]):
            places[span - first - STAGES[stage] + j] = (stage, 0, j)
            places[first + j] = (stage, 1, j)
    return places


def hat(shape, shift):
    out_index = lax.broadcasted_iota(jnp.int32, shape, 0)
    in_index = lax.broadcasted_iota(jnp.int32, shape, 1)
    distance = jnp.abs(in_index + shift - out_index)
    return jnp.maximum(BOX - distance, 0)


def two_parts(values):
    high = values.astype(jnp.bfloat16)
    low = (values - high.astype(jnp.float32)).astype(jnp.bfloat16)
    return high, low


def along_rows(kernel, values):
    high, low = two_parts(values)
    return jnp.dot(kernel, high, preferred_element_type=jnp.float32) + jnp.dot(
        kernel, low, preferred_element_type=jnp.float32
    )


def vmem(count):
    return [pl.BlockSpec(memory_space=pltpu.VMEM)] * count


def params(mib):
    return pltpu.CompilerParams(vmem_limit_bytes=mib * 1024 * 1024)


def cost(flops):
    return pl.CostEstimate(flops=flops, bytes_accessed=8 * 1024 * 1024, transcendentals=0)


def section_kernel(density, mask, conv, *rest):
    sends, outer = rest[:4], rest[4:-4]
    held, table, codes, sems = rest[-4:]
    places = outer_places()
    planes, rows, columns = density.shape
    blocks = rows // CELLS
    copy_mask = pltpu.make_async_copy(mask, table, sems.at[CHUNKS])
    copy_mask.start()
    copies = []
    for c in range(CHUNKS):
        part = pl.ds(c * (rows // CHUNKS), rows // CHUNKS)
        copies.append(
            pltpu.make_async_copy(density.at[:, part, :], held.at[:, part, :], sems.at[c])
        )
        copies[-1].start()
    spread = (
        lax.broadcasted_iota(jnp.int32, (columns // CELLS, columns), 1) // CELLS
        == lax.broadcasted_iota(jnp.int32, (columns // CELLS, columns), 0)
    )
    copy_mask.wait()
    codes[...] = jnp.dot(
        table[...]
        .reshape(planes // CELLS * blocks, columns // CELLS)
        .astype(jnp.float32)
        .astype(jnp.bfloat16),
        spread.astype(jnp.float32).astype(jnp.bfloat16),
        preferred_element_type=jnp.float32,
    )

    def tile(i, carry):
        row = pl.ds(pl.multiple_of(i * CELLS, CELLS), CELLS)
        values, boxes = [], []
        box = total = None
        for z in range(planes + 2 * RADIUS):
            if z < planes:
                if z % CELLS == 0:
                    code = jnp.broadcast_to(
                        codes[pl.ds(z // CELLS * blocks + i, 1), :], (CELLS, columns)
                    )
                    fixed, given = code < 1.5, jnp.where(code < 0.5, 0.0, 1.0)
                value = jnp.where(fixed, given, held[z, row, :])
                values.append(value)
                change = value - values[z - BOX] if z >= BOX else value
                box = change if box is None else box + change
            elif z < planes + RADIUS:
                box = box - values[z - BOX]
            if z < planes + RADIUS:
                boxes.append(box)
                change = box - boxes[z - BOX] if z >= BOX else box
                total = change if total is None else total + change
            else:
                total = total - boxes[z - BOX]
            if z in places:
                stage, side, j = places[z]
                outer[2 * (stage - 1) + side][j, row, :] = total
            else:
                conv[z - RADIUS, row, :] = total
        return carry

    for c in range(CHUNKS):
        copies[c].wait()
        lax.fori_loop(c * blocks // CHUNKS, (c + 1) * blocks // CHUNKS, tile, 0)
    me = lax.axis_index("gx")
    for distance in range(4):
        quarter = lax.rem(me + distance, 4)
        base = 8 * quarter + plane_offset(0, quarter)
        for j in range(STAGES[0]):
            sends[distance][j] = conv[base + j]


def section(density, mask):
    planes, rows, columns = density.shape
    f32 = functools.partial(jax.ShapeDtypeStruct, dtype=jnp.float32)
    shapes = [f32(density.shape)] + [f32((STAGES[0], rows, columns))] * 4
    for count in STAGES[1:]:
        shapes += [f32((count, rows, columns))] * 2
    return pl.pallas_call(
        section_kernel,
        out_shape=shapes,
        in_specs=[pl.BlockSpec(memory_space=pltpu.HBM)] * 2,
        out_specs=vmem(len(shapes)),
        scratch_shapes=[
            pltpu.VMEM(density.shape, jnp.float32),
            pltpu.VMEM(mask.shape, jnp.int32),
            pltpu.VMEM((planes // CELLS * rows // CELLS, columns), jnp.float32),
            pltpu.SemaphoreType.DMA((CHUNKS + 1,)),
        ],
        compiler_params=params(24),
        cost_estimate=cost(40_000_000),
        name="section",
    )(
        pltpu.with_memory_space_constraint(density, pltpu.HBM),
        pltpu.with_memory_space_constraint(mask, pltpu.HBM),
    )


def inside(axis, first):
    place = lax.axis_index(axis)
    edge = 0 if first else lax.axis_size(axis) - 1
    return (place != edge).astype(jnp.float32)


def call(kernel, shapes, args, mib, flops=20_000_000):
    f32 = [jax.ShapeDtypeStruct(shape, jnp.float32) for shape in shapes]
    return pl.pallas_call(
        kernel,
        out_shape=f32,
        in_specs=vmem(len(args)),
        out_specs=vmem(len(f32)),
        compiler_params=params(mib),
        cost_estimate=cost(flops),
    )(*args)


def stage_kernel(stage, conv, lower, upper, *sends):
    me = lax.axis_index("gx")
    for d in range(4):
        quarter = lax.rem(me + d, 4)
        take_lower = (quarter == 0).astype(jnp.float32) * inside("gz", True)
        take_upper = (quarter == 3).astype(jnp.float32) * inside("gz", False)
        base = 8 * quarter + plane_offset(stage, quarter)
        for j in range(STAGES[stage]):
            sends[d][j] = conv[base + j] + take_lower * lower[j] + take_upper * upper[j]


def stage_sends(stage, conv, lower, upper):
    shapes = [(STAGES[stage],) + conv.shape[1:]] * 4
    kernel = functools.partial(stage_kernel, stage)
    return call(kernel, shapes, (conv, lower, upper), 12)


def fill_kernel(stage, conv, lower, upper, whole, first, last):
    count, rows = STAGES[stage], conv.shape[1]
    for quarter in range(4):
        base = 8 * quarter + both_offsets(stage)[min(quarter, 1)]
        for j in range(count):
            plane = conv[base + j]
            if quarter == 0:
                plane = plane + inside("gz", True) * lower[j]
            if quarter == 3:
                plane = plane + inside("gz", False) * upper[j]
            at = count * quarter + j
            whole[at] = plane
            first[at] = plane[:EDGE]
            last[at] = plane[rows - EDGE :]


def fill(stage, conv, lower, upper):
    total = 4 * STAGES[stage]
    shapes = [(total,) + conv.shape[1:]] + [(total, EDGE, conv.shape[2])] * 2
    kernel = functools.partial(fill_kernel, stage)
    return call(kernel, shapes, (conv, lower, upper), 12)


def row_weights(rows):
    return hat((rows, rows + 2 * EDGE), -EDGE).astype(jnp.float32).astype(jnp.bfloat16)


def with_edges(before, plane, after):
    has_before, has_after = inside("gy", True), inside("gy", False)
    return jnp.concatenate([before * has_before, plane, after * has_after], axis=0)


def last_kernel(whole, before, after, *sends):
    count = whole.shape[0] // 4
    kernel = row_weights(whole.shape[1])
    me = lax.axis_index("gx")
    for d in range(4):
        quarter = lax.rem(me + d, 4)
        for j in range(count):
            at = count * quarter + j
            sends[d][j] = along_rows(kernel, with_edges(before[at], whole[at], after[at]))


def last_sends(whole, before, after):
    shapes = [(whole.shape[0] // 4,) + whole.shape[1:]] * 4
    return call(last_kernel, shapes, (whole, before, after), 12, 40_000_000)


def rims_kernel(*refs):
    sources, (first, last) = refs[:-2], refs[-2:]
    at = 0
    for source in sources:
        count, rows = source.shape[:2]
        first[at : at + count] = source[:, :EDGE, :]
        last[at : at + count] = source[:, rows - EDGE :, :]
        at += count


def rims(received):
    sources = [array for stage in received for array in stage]
    total = sum(array.shape[0] for array in sources)
    shapes = [(total, EDGE, sources[0].shape[2])] * 2
    return call(rims_kernel, shapes, sources, 12)


def finish_kernel(stage, start, *refs):
    edged, aliased = 0 if start is None else 2, 0 if stage == 0 else 2
    scale, plane_scale, weights, own, up, across, down = refs[:7]
    filtered, projected = refs[7 + edged + aliased : 9 + edged + aliased]
    smooth, sharp, sem = refs[9 + edged + aliased :]
    count, rows, columns = own.shape
    half = columns // 2
    me = lax.axis_index("gx")
    top = jnp.tanh(jnp.float32(sharpness * threshold))
    inverse = 1.0 / (top + jnp.tanh(jnp.float32(sharpness * (1.0 - threshold))))
    sources = [(up, 1), (own, 0), (down, 3), (across, 2)]
    if edged:
        before, after = refs[7:9]
        kernel = row_weights(rows)
    offset = plane_offset(stage, me)
    copies = []
    for j in range(count):
        values = []
        for source, place in sources:
            value = source[j]
            if edged:
                at = start + count * place + j
                value = along_rows(kernel, with_edges(before[at], value, after[at]))
            values.append(value)
        plane_factor = plane_scale[pl.ds(offset + j, 1), :]
        put = pl.ds(j * rows, rows)
        for r in range(4):
            block = lax.rem(me + 3 + r, 4)
            has_before = (block != 0).astype(jnp.float32)
            has_after = (block != 3).astype(jnp.float32)
            outer_values = jnp.where(
                lax.broadcasted_iota(jnp.int32, (rows, half), 1) < half // 2,
                values[(r + 1) % 4][:, :half] * has_after,
                values[(r + 3) % 4][:, half:] * has_before,
            )
            parts = two_parts(values[r]) + two_parts(outer_values)
            summed = jnp.dot(
                jnp.concatenate(parts, axis=1), weights[...], preferred_element_type=jnp.float32
            )
            lanes = pl.ds(pl.multiple_of(block * columns, columns), columns)
            smoothed = summed * (scale[:, lanes] * plane_factor)
            smooth[put, lanes] = smoothed
            sharp[put, lanes] = (
                top + jnp.tanh(sharpness * (smoothed - threshold))
            ) * inverse
        for source, target in ((smooth, filtered), (sharp, projected)):
            copy = pltpu.make_async_copy(
                source.at[put, :], target.at[offset + j], sem.at[len(copies)]
            )
            copy.start()
            copies.append(copy)
    for copy in copies:
        copy.wait()


def finish(stage, tables, received, results, start=None, edges=()):
    scale, plane_scale = tables[:2]
    rows, width = scale.shape
    whole = jax.ShapeDtypeStruct((plane_scale.shape[0], rows, width), jnp.float32)
    count = STAGES[stage]
    args = (*tables, *received, *edges)
    return pl.pallas_call(
        functools.partial(finish_kernel, stage, start),
        out_shape=[whole, whole],
        in_specs=vmem(len(args)) + [pl.BlockSpec(memory_space=pl.ANY)] * len(results),
        out_specs=[pl.BlockSpec(memory_space=pl.ANY)] * 2,
        scratch_shapes=[
            pltpu.VMEM((count * rows, width), jnp.float32),
            pltpu.VMEM((count * rows, width), jnp.float32),
            pltpu.SemaphoreType.DMA((2 * count,)),
        ],
        input_output_aliases={len(args): 0, len(args) + 1: 1} if results else {},
        compiler_params=params(20),
        cost_estimate=cost(40_000_000),
    )(*args, *results)


def one_side(reach):
    return reach * (RADIUS + 1) - reach * (reach + 1) // 2


def edge_sums(position, length):
    reach_left = jnp.minimum(position, RADIUS)
    reach_right = jnp.minimum(length - 1 - position, RADIUS)
    return (RADIUS + 1 + one_side(reach_left) + one_side(reach_right)).astype(jnp.float32)


def scale_kernel(scale, plane_scale, weights):
    rows, width = scale.shape
    layers = plane_scale.shape[0]
    row = lax.axis_index("gy") * rows + lax.broadcasted_iota(jnp.int32, (rows, 128), 0)
    count_y = edge_sums(row, rows * lax.axis_size("gy"))
    for c in range(width // 128):
        column = c * 128 + lax.broadcasted_iota(jnp.int32, (8, 128), 1)
        count_x = edge_sums(column, width)[:1]
        scale[:, c * 128 : (c + 1) * 128] = 1.0 / (count_y * count_x)
    section_place = lax.axis_index("gz") * lax.axis_size("gx") + lax.axis_index("gx")
    plane = section_place * layers + lax.broadcasted_iota(jnp.int32, plane_scale.shape, 0)
    plane_scale[...] = 1.0 / edge_sums(
        plane, layers * lax.axis_size("gx") * lax.axis_size("gz")
    )
    columns = weights.shape[1]
    half = columns // 2
    center = hat((columns, columns), 0)
    row = lax.broadcasted_iota(jnp.int32, (half, columns), 0)
    column = lax.broadcasted_iota(jnp.int32, (half, columns), 1)
    place = jnp.where(row < half // 2, row + columns, row - half)
    outer = jnp.maximum(BOX - jnp.abs(place - column), 0)
    at = 0
    for part in (center, center, outer, outer):
        weights[at : at + part.shape[0], :] = part.astype(jnp.float32).astype(jnp.bfloat16)
        at += part.shape[0]


def scales(rows, width, columns, layers):
    return pl.pallas_call(
        scale_kernel,
        out_shape=[
            jax.ShapeDtypeStruct((rows, width), jnp.float32),
            jax.ShapeDtypeStruct((layers, columns), jnp.float32),
            jax.ShapeDtypeStruct((3 * columns, columns), jnp.bfloat16),
        ],
        out_specs=vmem(3),
        compiler_params=params(4),
        cost_estimate=cost(5_000_000),
        name="scales",
    )()


def shifted(block, axis, distance):
    peers = lax.axis_size(axis)
    route = [(i, (i + distance) % peers) for i in range(peers)]
    return lax.ppermute(block, axis, route)


def around(sends):
    return [sends[0]] + [shifted(sends[d], "gx", d) for d in (1, 2, 3)]


def program(density, mask):
    planes, row_count, columns = density.shape
    groups = lax.axis_size("gx")
    layers = planes // groups
    width = columns * groups
    last = len(STAGES) - 1
    conv, *rest = section(density, mask)
    received = [around(rest[:4])]
    outer = rest[4:]
    halos = []
    for k in range(last):
        halos.append(
            (shifted(outer[2 * k], "gz", 1), shifted(outer[2 * k + 1], "gz", -1))
        )
    tables = scales(row_count, width, columns, layers)
    for stage in range(1, last):
        sends = stage_sends(stage, conv, *halos[stage - 1])
        received.append(around(sends))
    whole, first, final = fill(last, conv, *halos[last - 1])
    before, after = shifted(final, "gy", 1), shifted(first, "gy", -1)
    sends = last_sends(whole, before, after)
    received.append(around(sends))
    results = []
    for group in GROUPS:
        first, final = rims([received[stage] for stage in group])
        ends = (shifted(final, "gy", 1), shifted(first, "gy", -1))
        start = 0
        for stage in group:
            results = finish(stage, tables, received[stage], results, start, ends)
            start += 4 * STAGES[stage]
    results = finish(last, tables, received[last], results)
    return tuple(results)


def solution(mesh):
    placed = (P("gz", "gy", "gx"), P("gz", "gy", "gx"))
    return jax.shard_map(
        program,
        mesh=mesh,
        in_specs=placed,
        out_specs=(P(("gz", "gx"), "gy", None), P(("gz", "gx"), "gy", None)),
        check_vma=False,
    )
```

time: 86.8 us -> 79.4 us (0.915)
  the two profiles are of different devices: /device:TPU:17 before, /device:TPU:6 now
where the time goes in v4:
time: 79.4 us; the launch traced here: 79.3 us
  waiting for transfers between devices  38.3 us (48%)
  starting transfers between devices  28.3 us (36%)
  Pallas kernels  11.8 us (15%)
  between operations  0.95 us (1%)
    ppermute x24, waiting for transfers between devices, shifted(): return lax.ppermute(block, axis, route)  38.3 us
    ppermute x24, starting transfers between devices, shifted(): return lax.ppermute(block, axis, route)  28.3 us
    pallas_call x4, Pallas kernels, finish(): pl.pallas_call(functools.partial(finish_kernel, stage, start), out_shape=...  7.92 us
    pallas_call x1, Pallas kernels, section(): pl.pallas_call(section_kernel, out_shape=shapes, in_specs=[pl.BlockSpec(m...  2.56 us
  transfers between devices with their start and end apart: 24, of which 10 were waited for; matrix products, arithmetic and copies ran while one was open for 0% of the time, Pallas kernels for 9%

profile of v4, /device:TPU:6, one launch (start us, length us, event | category | flops | bytes accessed | tf_op | source)
XLA Modules:
  0.0 79.3 jit_solution(5033467970019336750)
XLA Ops:
  0.6 2.6 %section.1 = (f32[32,128,256]{2,1,0:T(8,128)S(1)}, f32[2,128,256]{2,1,0:T(8,128)S(1)}, f32[2,128,256]{2,1,0:T(8,128)S(1)}, f32[2,128,256]{2,1,0:T(8,128)S(1)}, f...) custom-call(f32[32,128,256]{2,1,0:T(8,128)} %density.1, ...), custom_call_target="tpu_custom_call" | custom-call | flops 40000000 | bytes 8388608 | tf_op jit(solution)/shard_map/section/pallas_call | solution.py:158
  3.2 2.0 %collective-permute-start = (f32[2,128,256]{2,1,0:T(8,128)S(1)}, f32[2,128,256]{2,1,0:T(8,128)S(1)}, u32[]{:S(2)}, u32[]{:S(2)}) collective-permute-start(f32[2,128,256]{2,1,0:T(8,128)S(1)} %get-tuple-element.45), channel_id=1, source_target_pairs={{0,32},{32,64},{64,96},{96,128},{128,160},{160,192},{192,224},{224... | collective-permute-start | bytes 786440 | tf_op jit(solution)/shard_map/ppermute | solution.py:410
  5.2 4.0 %collective-permute-start.1 = (f32[2,128,256]{2,1,0:T(8,128)S(1)}, f32[2,128,256]{2,1,0:T(8,128)S(1)}, u32[]{:S(2)}, u32[]{:S(2)}) collective-permute-start(f32[2,128,256]{2,1,0:T(8,128)S(1)} %get-tuple-element.46), channel_id=1, source_target_pairs={{0,224},{32,0},{64,32},{96,64},{128,96},{160,128},{192,160},{224,1... | collective-permute-start | bytes 786440 | tf_op jit(solution)/shard_map/ppermute | solution.py:410
  9.2 3.2 %collective-permute-start.15 = (f32[2,128,256]{2,1,0:T(8,128)S(1)}, f32[2,128,256]{2,1,0:T(8,128)S(1)}, u32[]{:S(2)}, u32[]{:S(2)}) collective-permute-start(f32[2,128,256]{2,1,0:T(8,128)S(1)} %get-tuple-element.63), channel_id=1, source_target_pairs={{0,224},{32,0},{64,32},{96,64},{128,96},{160,128},{192,160},{224,1... | collective-permute-start | bytes 786440 | tf_op jit(solution)/shard_map/ppermute | solution.py:410
  12.5 3.8 %collective-permute-done.lower = f32[2,128,256]{2,1,0:T(8,128)S(1)} collective-permute-done((f32[2,128,256]{2,1,0:T(8,128)S(1)}, f32[2,128,256]{2,1,0:T(8,128)S(1)}, u32[]{:S(2)}, u32[]{:S(2)}) %collective-permute-start) | collective-permute-done | bytes 262176 | tf_op jit(solution)/shard_map/ppermute | solution.py:410
  16.3 2.0 %collective-permute-start.8 = (f32[2,128,256]{2,1,0:T(8,128)S(1)}, f32[2,128,256]{2,1,0:T(8,128)S(1)}, u32[]{:S(2)}, u32[]{:S(2)}) collective-permute-start(f32[2,128,256]{2,1,0:T(8,128)S(1)} %get-tuple-element.55), channel_id=1, source_target_pairs={{0,224},{32,0},{64,32},{96,64},{128,96},{160,128},{192,160},{224,1... | collective-permute-start | bytes 786440 | tf_op jit(solution)/shard_map/ppermute | solution.py:410
  18.3 0.5 collective-permute-start.19
  18.8 3.1 %collective-permute-done.14.lower = f32[2,128,256]{2,1,0:T(8,128)S(1)} collective-permute-done((f32[2,128,256]{2,1,0:T(8,128)S(1)}, f32[2,128,256]{2,1,0:T(8,128)S(1)}, u32[]{:S(2)}, u32[]{:S(2)}) %collective-permute-start.14) | collective-permute-done | bytes 262176 | tf_op jit(solution)/shard_map/ppermute | solution.py:410
  21.9 1.4 %collective-permute-start.20 = (f32[2,128,256]{2,1,0:T(8,128)S(1)}, f32[2,128,256]{2,1,0:T(8,128)S(1)}, u32[]{:S(2)}, u32[]{:S(2)}) collective-permute-start(f32[2,128,256]{2,1,0:T(8,128)S(1)} %get-tuple-element.70), channel_id=1, source_target_pairs={{0,16},{8,24},{16,0},{24,8},{1,17},{9,25},{17,1},{25,9},{2,18},{10... | collective-permute-start | bytes 786440 | tf_op jit(solution)/shard_map/ppermute | solution.py:410
  23.3 0.2 shard_map.45
  23.6 3.1 %collective-permute-done.7.lower = f32[2,128,256]{2,1,0:T(8,128)S(1)} collective-permute-done((f32[2,128,256]{2,1,0:T(8,128)S(1)}, f32[2,128,256]{2,1,0:T(8,128)S(1)}, u32[]{:S(2)}, u32[]{:S(2)}) %collective-permute-start.7) | collective-permute-done | bytes 262176 | tf_op jit(solution)/shard_map/ppermute | solution.py:410
  26.7 0.5 collective-permute-start.16
  27.3 2.9 %collective-permute-start.3 = (f32[8,8,256]{2,1,0:T(8,128)S(1)}, f32[8,8,256]{2,1,0:T(8,128)S(1)}, u32[]{:S(2)}, u32[]{:S(2)}) collective-permute-start(f32[8,8,256]{2,1,0:T(8,128)S(1)} %get-tuple-element.49), channel_id=1, source_target_pairs={{0,7},{1,0},{2,1},{3,2},{4,3},{5,4},{6,5},{7,6},{8,15},{9,8},{10,9... | collective-permute-start | bytes 196616 | tf_op jit(solution)/shard_map/ppermute | solution.py:410
  30.5 2.2 %collective-permute-done.20.refs_2_.refs_5_ = f32[2,128,256]{2,1,0:T(8,128)S(1)} collective-permute-done((f32[2,128,256]{2,1,0:T(8,128)S(1)}, f32[2,128,256]{2,1,0:T(8,128)S(1)}, u32[]{:S(2)}, u32[]{:S(2)}) %collective-permute-start.20) | collective-permute-done | bytes 262176 | tf_op jit(solution)/shard_map/ppermute | solution.py:410
  32.6 1.4 %collective-permute-start.17 = (f32[2,128,256]{2,1,0:T(8,128)S(1)}, f32[2,128,256]{2,1,0:T(8,128)S(1)}, u32[]{:S(2)}, u32[]{:S(2)}) collective-permute-start(f32[2,128,256]{2,1,0:T(8,128)S(1)} %get-tuple-element.66), channel_id=1, source_target_pairs={{0,16},{8,24},{16,0},{24,8},{1,17},{9,25},{17,1},{25,9},{2,18},{10... | collective-permute-start | bytes 786440 | tf_op jit(solution)/shard_map/ppermute | solution.py:410
  34.0 3.9 %collective-permute-done.21.refs_3_.refs_6_ = f32[2,128,256]{2,1,0:T(8,128)S(1)} collective-permute-done((f32[2,128,256]{2,1,0:T(8,128)S(1)}, f32[2,128,256]{2,1,0:T(8,128)S(1)}, u32[]{:S(2)}, u32[]{:S(2)}) %collective-permute-start.21) | collective-permute-done | bytes 262176 | tf_op jit(solution)/shard_map/ppermute | solution.py:410
  37.9 3.2 %collective-permute-start.9 = (f32[2,128,256]{2,1,0:T(8,128)S(1)}, f32[2,128,256]{2,1,0:T(8,128)S(1)}, u32[]{:S(2)}, u32[]{:S(2)}) collective-permute-start(f32[2,128,256]{2,1,0:T(8,128)S(1)} %get-tuple-element.57), channel_id=1, source_target_pairs={{0,8},{8,16},{16,24},{24,0},{1,9},{9,17},{17,25},{25,1},{2,10},{10... | collective-permute-start | bytes 786440 | tf_op jit(solution)/shard_map/ppermute | solution.py:410
  41.2 0.9 %collective-permute-start.11 = (f32[2,128,256]{2,1,0:T(8,128)S(1)}, f32[2,128,256]{2,1,0:T(8,128)S(1)}, u32[]{:S(2)}, u32[]{:S(2)}) collective-permute-start(f32[2,128,256]{2,1,0:T(8,128)S(1)} %get-tuple-element.59), channel_id=1, source_target_pairs={{0,24},{8,0},{16,8},{24,16},{1,25},{9,1},{17,9},{25,17},{2,26},{10... | collective-permute-start | bytes 786440 | tf_op jit(solution)/shard_map/ppermute | solution.py:410
  42.1 0.5 shard_map.42
  42.6 1.0 %collective-permute-done.17.refs_6_.refs_5_ = f32[2,128,256]{2,1,0:T(8,128)S(1)} collective-permute-done((f32[2,128,256]{2,1,0:T(8,128)S(1)}, f32[2,128,256]{2,1,0:T(8,128)S(1)}, u32[]{:S(2)}, u32[]{:S(2)}) %collective-permute-start.17) | collective-permute-done | bytes 262176 | tf_op jit(solution)/shard_map/ppermute | solution.py:410
  43.5 2.2 %collective-permute-start.4 = (f32[2,128,256]{2,1,0:T(8,128)S(1)}, f32[2,128,256]{2,1,0:T(8,128)S(1)}, u32[]{:S(2)}, u32[]{:S(2)}) collective-permute-start(f32[2,128,256]{2,1,0:T(8,128)S(1)} %get-tuple-element.51), channel_id=1, source_target_pairs={{0,8},{8,16},{16,24},{24,0},{1,9},{9,17},{17,25},{25,1},{2,10},{10... | collective-permute-start | bytes 786440 | tf_op jit(solution)/shard_map/ppermute | solution.py:410
  45.8 8.1 %collective-permute-done.18.refs_7_.refs_6_ = f32[2,128,256]{2,1,0:T(8,128)S(1)} collective-permute-done((f32[2,128,256]{2,1,0:T(8,128)S(1)}, f32[2,128,256]{2,1,0:T(8,128)S(1)}, u32[]{:S(2)}, u32[]{:S(2)}) %collective-permute-start.18) | collective-permute-done | bytes 262176 | tf_op jit(solution)/shard_map/ppermute | solution.py:410
  53.9 0.9 %collective-permute-done.10.refs_2_.refs_5_ = f32[2,128,256]{2,1,0:T(8,128)S(1)} collective-permute-done((f32[2,128,256]{2,1,0:T(8,128)S(1)}, f32[2,128,256]{2,1,0:T(8,128)S(1)}, u32[]{:S(2)}, u32[]{:S(2)}) %collective-permute-start.10) | collective-permute-done | bytes 262176 | tf_op jit(solution)/shard_map/ppermute | solution.py:410
  54.8 10.2 %collective-permute-done.11.refs_3_.refs_6_ = f32[2,128,256]{2,1,0:T(8,128)S(1)} collective-permute-done((f32[2,128,256]{2,1,0:T(8,128)S(1)}, f32[2,128,256]{2,1,0:T(8,128)S(1)}, u32[]{:S(2)}, u32[]{:S(2)}) %collective-permute-start.11) | collective-permute-done | bytes 262176 | tf_op jit(solution)/shard_map/ppermute | solution.py:410
  65.1 0.5 collective-permute-start.12
  65.6 2.0 %collective-permute-done.23.refs_8_ = f32[16,8,256]{2,1,0:T(8,128)S(1)} collective-permute-done((f32[16,8,256]{2,1,0:T(8,128)S(1)}, f32[16,8,256]{2,1,0:T(8,128)S(1)}, u32[]{:S(2)}, u32[]{:S(2)}) %collective-permute-start.23) | collective-permute-done | bytes 131104 | tf_op jit(solution)/shard_map/ppermute | solution.py:410
  67.6 3.4 %collective-permute-start.13 = (f32[8,8,256]{2,1,0:T(8,128)S(1)}, f32[8,8,256]{2,1,0:T(8,128)S(1)}, u32[]{:S(2)}, u32[]{:S(2)}) collective-permute-start(f32[8,8,256]{2,1,0:T(8,128)S(1)} %get-tuple-element.61), channel_id=1, source_target_pairs={{0,7},{1,0},{2,1},{3,2},{4,3},{5,4},{6,5},{7,6},{8,15},{9,8},{10,9... | collective-permute-start | bytes 196616 | tf_op jit(solution)/shard_map/ppermute | solution.py:410
  71.0 0.2 scales.1
  71.2 2.0 %shard_map.47 = (f32[8,128,1024]{2,1,0:T(8,128)}, f32[8,128,1024]{2,1,0:T(8,128)}) custom-call(f32[128,1024]{1,0:T(8,128)S(1)} %get-tuple-element.41.refs_0_, f32[8,256]{1,0:T(8,128)S(1)} %get-tuple-element.42.refs_1_, bf16[768,256]{1,0:T(8,128)(2,1)S(1)} %get-tuple-element.43.refs_2_, f32[2,128,256]{2,1,0:T(8,128)S(1)} %get-tuple-element.68.refs_0_.refs_3_, ...), custom_call_target="tpu_custom_call" | custom-call | flops 40000000 | bytes 8388608 | tf_op jit(solution)/shard_map/pallas_call | solution.py:339
  73.2 2.0 %shard_map.48 = (f32[8,128,1024]{2,1,0:T(8,128)}, f32[8,128,1024]{2,1,0:T(8,128)}) custom-call(f32[128,1024]{1,0:T(8,128)S(1)} %get-tuple-element.41.refs_0_, f32[8,256]{1,0:T(8,128)S(1)} %get-tuple-element.42.refs_1_, bf16[768,256]{1,0:T(8,128)(2,1)S(1)} %get-tuple-element.43.refs_2_, ...), custom_call_target="tpu_custom_call", output_to_operand_aliasing={{0}: (9, {}), {1}: (10, {})} | custom-call | flops 40000000 | bytes 8388608 | tf_op jit(solution)/shard_map/pallas_call | solution.py:339
  75.3 2.0 %shard_map.49 = (f32[8,128,1024]{2,1,0:T(8,128)}, f32[8,128,1024]{2,1,0:T(8,128)}) custom-call(f32[128,1024]{1,0:T(8,128)S(1)} %get-tuple-element.41.refs_0_, f32[8,256]{1,0:T(8,128)S(1)} %get-tuple-element.42.refs_1_, bf16[768,256]{1,0:T(8,128)(2,1)S(1)} %get-tuple-element.43.refs_2_, ...), custom_call_target="tpu_custom_call", output_to_operand_aliasing={{0}: (9, {}), {1}: (10, {})} | custom-call | flops 40000000 | bytes 8388608 | tf_op jit(solution)/shard_map/pallas_call | solution.py:339
  77.3 1.8 %shard_map.50 = (f32[8,128,1024]{2,1,0:T(8,128)}, f32[8,128,1024]{2,1,0:T(8,128)}) custom-call(f32[128,1024]{1,0:T(8,128)S(1)} %get-tuple-element.41.refs_0_, f32[8,256]{1,0:T(8,128)S(1)} %get-tuple-element.42.refs_1_, bf16[768,256]{1,0:T(8,128)(2,1)S(1)} %get-tuple-element.43.refs_2_, ...), custom_call_target="tpu_custom_call", output_to_operand_aliasing={{0}: (7, {}), {1}: (8, {})} | custom-call | flops 40000000 | bytes 8388608 | tf_op jit(solution)/shard_map/pallas_call | solution.py:339
  (28 shorter events, 0.4 us)
Async XLA Ops:
  3.2 13.1 %collective-permute-start = (f32[2,128,256]{2,1,0:T(8,128)S(1)}, f32[2,128,256]{2,1,0:T(8,128)S(1)}, u32[]{:S(2)}, u32[]{:S(2)}) collective-permute-start(f32[2,128,256]{2,1,0:T(8,128)S(1)} %get-tuple-element.45), channel_id=1, source_target_pairs={{0,32},{32,64},{64,96},{96,128},{128,160},{160,192},{192,224},{224... | collective-permute-start | bytes 786440 | tf_op jit(solution)/shard_map/ppermute | solution.py:410
  5.2 13.1 %collective-permute-start.1 = (f32[2,128,256]{2,1,0:T(8,128)S(1)}, f32[2,128,256]{2,1,0:T(8,128)S(1)}, u32[]{:S(2)}, u32[]{:S(2)}) collective-permute-start(f32[2,128,256]{2,1,0:T(8,128)S(1)} %get-tuple-element.46), channel_id=1, source_target_pairs={{0,224},{32,0},{64,32},{96,64},{128,96},{160,128},{192,160},{224,1... | collective-permute-start | bytes 786440 | tf_op jit(solution)/shard_map/ppermute | solution.py:410
  9.2 12.7 %collective-permute-start.14 = (f32[2,128,256]{2,1,0:T(8,128)S(1)}, f32[2,128,256]{2,1,0:T(8,128)S(1)}, u32[]{:S(2)}, u32[]{:S(2)}) collective-permute-start(f32[2,128,256]{2,1,0:T(8,128)S(1)} %get-tuple-element.62), channel_id=1, source_target_pairs={{0,32},{32,64},{64,96},{96,128},{128,160},{160,192},{192,224},{224... | collective-permute-start | bytes 786440 | tf_op jit(solution)/shard_map/ppermute | solution.py:410
  9.2 14.1 %collective-permute-start.15 = (f32[2,128,256]{2,1,0:T(8,128)S(1)}, f32[2,128,256]{2,1,0:T(8,128)S(1)}, u32[]{:S(2)}, u32[]{:S(2)}) collective-permute-start(f32[2,128,256]{2,1,0:T(8,128)S(1)} %get-tuple-element.63), channel_id=1, source_target_pairs={{0,224},{32,0},{64,32},{96,64},{128,96},{160,128},{192,160},{224,1... | collective-permute-start | bytes 786440 | tf_op jit(solution)/shard_map/ppermute | solution.py:410
  12.5 14.2 %collective-permute-start.7 = (f32[2,128,256]{2,1,0:T(8,128)S(1)}, f32[2,128,256]{2,1,0:T(8,128)S(1)}, u32[]{:S(2)}, u32[]{:S(2)}) collective-permute-start(f32[2,128,256]{2,1,0:T(8,128)S(1)} %get-tuple-element.54), channel_id=1, source_target_pairs={{0,32},{32,64},{64,96},{96,128},{128,160},{160,192},{192,224},{224... | collective-permute-start | bytes 786440 | tf_op jit(solution)/shard_map/ppermute | solution.py:410
  16.3 11.0 %collective-permute-start.8 = (f32[2,128,256]{2,1,0:T(8,128)S(1)}, f32[2,128,256]{2,1,0:T(8,128)S(1)}, u32[]{:S(2)}, u32[]{:S(2)}) collective-permute-start(f32[2,128,256]{2,1,0:T(8,128)S(1)} %get-tuple-element.55), channel_id=1, source_target_pairs={{0,224},{32,0},{64,32},{96,64},{128,96},{160,128},{192,160},{224,1... | collective-permute-start | bytes 786440 | tf_op jit(solution)/shard_map/ppermute | solution.py:410
  18.3 9.0 %collective-permute-start.19 = (f32[2,128,256]{2,1,0:T(8,128)S(1)}, f32[2,128,256]{2,1,0:T(8,128)S(1)}, u32[]{:S(2)}, u32[]{:S(2)}) collective-permute-start(f32[2,128,256]{2,1,0:T(8,128)S(1)} %get-tuple-element.69), channel_id=1, source_target_pairs={{0,8},{8,16},{16,24},{24,0},{1,9},{9,17},{17,25},{25,1},{2,10},{10... | collective-permute-start | bytes 786440 | tf_op jit(solution)/shard_map/ppermute | solution.py:410
  21.9 10.7 %collective-permute-start.20 = (f32[2,128,256]{2,1,0:T(8,128)S(1)}, f32[2,128,256]{2,1,0:T(8,128)S(1)}, u32[]{:S(2)}, u32[]{:S(2)}) collective-permute-start(f32[2,128,256]{2,1,0:T(8,128)S(1)} %get-tuple-element.70), channel_id=1, source_target_pairs={{0,16},{8,24},{16,0},{24,8},{1,17},{9,25},{17,1},{25,9},{2,18},{10... | collective-permute-start | bytes 786440 | tf_op jit(solution)/shard_map/ppermute | solution.py:410
  23.3 14.6 %collective-permute-start.21 = (f32[2,128,256]{2,1,0:T(8,128)S(1)}, f32[2,128,256]{2,1,0:T(8,128)S(1)}, u32[]{:S(2)}, u32[]{:S(2)}) collective-permute-start(f32[2,128,256]{2,1,0:T(8,128)S(1)} %get-tuple-element.71), channel_id=1, source_target_pairs={{0,24},{8,0},{16,8},{24,16},{1,25},{9,1},{17,9},{25,17},{2,26},{10... | collective-permute-start | bytes 786440 | tf_op jit(solution)/shard_map/ppermute | solution.py:410
  26.7 14.5 %collective-permute-start.16 = (f32[2,128,256]{2,1,0:T(8,128)S(1)}, f32[2,128,256]{2,1,0:T(8,128)S(1)}, u32[]{:S(2)}, u32[]{:S(2)}) collective-permute-start(f32[2,128,256]{2,1,0:T(8,128)S(1)} %get-tuple-element.65), channel_id=1, source_target_pairs={{0,8},{8,16},{16,24},{24,0},{1,9},{9,17},{17,25},{25,1},{2,10},{10... | collective-permute-start | bytes 786440 | tf_op jit(solution)/shard_map/ppermute | solution.py:410
  27.3 10.6 %collective-permute-start.2 = (f32[8,8,256]{2,1,0:T(8,128)S(1)}, f32[8,8,256]{2,1,0:T(8,128)S(1)}, u32[]{:S(2)}, u32[]{:S(2)}) collective-permute-start(f32[8,8,256]{2,1,0:T(8,128)S(1)} %get-tuple-element.48), channel_id=1, source_target_pairs={{0,1},{1,2},{2,3},{3,4},{4,5},{5,6},{6,7},{7,0},{8,9},{9,10},{10,1... | collective-permute-start | bytes 196616 | tf_op jit(solution)/shard_map/ppermute | solution.py:410
  27.3 13.8 %collective-permute-start.3 = (f32[8,8,256]{2,1,0:T(8,128)S(1)}, f32[8,8,256]{2,1,0:T(8,128)S(1)}, u32[]{:S(2)}, u32[]{:S(2)}) collective-permute-start(f32[8,8,256]{2,1,0:T(8,128)S(1)} %get-tuple-element.49), channel_id=1, source_target_pairs={{0,7},{1,0},{2,1},{3,2},{4,3},{5,4},{6,5},{7,6},{8,15},{9,8},{10,9... | collective-permute-start | bytes 196616 | tf_op jit(solution)/shard_map/ppermute | solution.py:410
  32.6 10.9 %collective-permute-start.17 = (f32[2,128,256]{2,1,0:T(8,128)S(1)}, f32[2,128,256]{2,1,0:T(8,128)S(1)}, u32[]{:S(2)}, u32[]{:S(2)}) collective-permute-start(f32[2,128,256]{2,1,0:T(8,128)S(1)} %get-tuple-element.66), channel_id=1, source_target_pairs={{0,16},{8,24},{16,0},{24,8},{1,17},{9,25},{17,1},{25,9},{2,18},{10... | collective-permute-start | bytes 786440 | tf_op jit(solution)/shard_map/ppermute | solution.py:410
  37.9 16.0 %collective-permute-start.18 = (f32[2,128,256]{2,1,0:T(8,128)S(1)}, f32[2,128,256]{2,1,0:T(8,128)S(1)}, u32[]{:S(2)}, u32[]{:S(2)}) collective-permute-start(f32[2,128,256]{2,1,0:T(8,128)S(1)} %get-tuple-element.67), channel_id=1, source_target_pairs={{0,24},{8,0},{16,8},{24,16},{1,25},{9,1},{17,9},{25,17},{2,26},{10... | collective-permute-start | bytes 786440 | tf_op jit(solution)/shard_map/ppermute | solution.py:410
  37.9 16.0 %collective-permute-start.9 = (f32[2,128,256]{2,1,0:T(8,128)S(1)}, f32[2,128,256]{2,1,0:T(8,128)S(1)}, u32[]{:S(2)}, u32[]{:S(2)}) collective-permute-start(f32[2,128,256]{2,1,0:T(8,128)S(1)} %get-tuple-element.57), channel_id=1, source_target_pairs={{0,8},{8,16},{16,24},{24,0},{1,9},{9,17},{17,25},{25,1},{2,10},{10... | collective-permute-start | bytes 786440 | tf_op jit(solution)/shard_map/ppermute | solution.py:410
  41.1 13.7 %collective-permute-start.10 = (f32[2,128,256]{2,1,0:T(8,128)S(1)}, f32[2,128,256]{2,1,0:T(8,128)S(1)}, u32[]{:S(2)}, u32[]{:S(2)}) collective-permute-start(f32[2,128,256]{2,1,0:T(8,128)S(1)} %get-tuple-element.58), channel_id=1, source_target_pairs={{0,16},{8,24},{16,0},{24,8},{1,17},{9,25},{17,1},{25,9},{2,18},{10... | collective-permute-start | bytes 786440 | tf_op jit(solution)/shard_map/ppermute | solution.py:410
  41.2 23.9 %collective-permute-start.11 = (f32[2,128,256]{2,1,0:T(8,128)S(1)}, f32[2,128,256]{2,1,0:T(8,128)S(1)}, u32[]{:S(2)}, u32[]{:S(2)}) collective-permute-start(f32[2,128,256]{2,1,0:T(8,128)S(1)} %get-tuple-element.59), channel_id=1, source_target_pairs={{0,24},{8,0},{16,8},{24,16},{1,25},{9,1},{17,9},{25,17},{2,26},{10... | collective-permute-start | bytes 786440 | tf_op jit(solution)/shard_map/ppermute | solution.py:410
  43.5 33.8 %collective-permute-start.4 = (f32[2,128,256]{2,1,0:T(8,128)S(1)}, f32[2,128,256]{2,1,0:T(8,128)S(1)}, u32[]{:S(2)}, u32[]{:S(2)}) collective-permute-start(f32[2,128,256]{2,1,0:T(8,128)S(1)} %get-tuple-element.51), channel_id=1, source_target_pairs={{0,8},{8,16},{16,24},{24,0},{1,9},{9,17},{17,25},{25,1},{2,10},{10... | collective-permute-start | bytes 786440 | tf_op jit(solution)/shard_map/ppermute | solution.py:410
  53.9 23.5 %collective-permute-start.5 = (f32[2,128,256]{2,1,0:T(8,128)S(1)}, f32[2,128,256]{2,1,0:T(8,128)S(1)}, u32[]{:S(2)}, u32[]{:S(2)}) collective-permute-start(f32[2,128,256]{2,1,0:T(8,128)S(1)} %get-tuple-element.52), channel_id=1, source_target_pairs={{0,16},{8,24},{16,0},{24,8},{1,17},{9,25},{17,1},{25,9},{2,18},{10... | collective-permute-start | bytes 786440 | tf_op jit(solution)/shard_map/ppermute | solution.py:410
  53.9 23.5 %collective-permute-start.6 = (f32[2,128,256]{2,1,0:T(8,128)S(1)}, f32[2,128,256]{2,1,0:T(8,128)S(1)}, u32[]{:S(2)}, u32[]{:S(2)}) collective-permute-start(f32[2,128,256]{2,1,0:T(8,128)S(1)} %get-tuple-element.53), channel_id=1, source_target_pairs={{0,24},{8,0},{16,8},{24,16},{1,25},{9,1},{17,9},{25,17},{2,26},{10... | collective-permute-start | bytes 786440 | tf_op jit(solution)/shard_map/ppermute | solution.py:410
  54.8 10.2 %collective-permute-start.22 = (f32[16,8,256]{2,1,0:T(8,128)S(1)}, f32[16,8,256]{2,1,0:T(8,128)S(1)}, u32[]{:S(2)}, u32[]{:S(2)}) collective-permute-start(f32[16,8,256]{2,1,0:T(8,128)S(1)} %get-tuple-element.72), channel_id=1, source_target_pairs={{0,1},{1,2},{2,3},{3,4},{4,5},{5,6},{6,7},{7,0},{8,9},{9,10},{10,1... | collective-permute-start | bytes 393224 | tf_op jit(solution)/shard_map/ppermute | solution.py:410
  65.0 2.5 %collective-permute-start.23 = (f32[16,8,256]{2,1,0:T(8,128)S(1)}, f32[16,8,256]{2,1,0:T(8,128)S(1)}, u32[]{:S(2)}, u32[]{:S(2)}) collective-permute-start(f32[16,8,256]{2,1,0:T(8,128)S(1)} %get-tuple-element.73), channel_id=1, source_target_pairs={{0,7},{1,0},{2,1},{3,2},{4,3},{5,4},{6,5},{7,6},{8,15},{9,8},{10,9... | collective-permute-start | bytes 393224 | tf_op jit(solution)/shard_map/ppermute | solution.py:410
  65.1 10.2 %collective-permute-start.12 = (f32[8,8,256]{2,1,0:T(8,128)S(1)}, f32[8,8,256]{2,1,0:T(8,128)S(1)}, u32[]{:S(2)}, u32[]{:S(2)}) collective-permute-start(f32[8,8,256]{2,1,0:T(8,128)S(1)} %get-tuple-element.60), channel_id=1, source_target_pairs={{0,1},{1,2},{2,3},{3,4},{4,5},{5,6},{6,7},{7,0},{8,9},{9,10},{10,1... | collective-permute-start | bytes 196616 | tf_op jit(solution)/shard_map/ppermute | solution.py:410
  67.6 7.7 %collective-permute-start.13 = (f32[8,8,256]{2,1,0:T(8,128)S(1)}, f32[8,8,256]{2,1,0:T(8,128)S(1)}, u32[]{:S(2)}, u32[]{:S(2)}) collective-permute-start(f32[8,8,256]{2,1,0:T(8,128)S(1)} %get-tuple-element.61), channel_id=1, source_target_pairs={{0,7},{1,0},{2,1},{3,2},{4,3},{5,4},{6,5},{7,6},{8,15},{9,8},{10,9... | collective-permute-start | bytes 196616 | tf_op jit(solution)/shard_map/ppermute | solution.py:410

commit v5 on v4

--- a/solution.py
+++ b/solution.py
@@ -19,7 +19,7 @@
 
 STAGES = (2, 2, 2, 2)
 GROUPS = ((0, 1), (2,))
-CHUNKS = 4
+CHUNKS = 8
 
 
 def first_of(stage):
@@ -320,12 +320,12 @@
             sharp[put, lanes] = (
                 top + jnp.tanh(sharpness * (smoothed - threshold))
             ) * inverse
-        for source, target in ((smooth, filtered), (sharp, projected)):
-            copy = pltpu.make_async_copy(
-                source.at[put, :], target.at[offset + j], sem.at[len(copies)]
-            )
-            copy.start()
-            copies.append(copy)
+            for source, target in ((smooth, filtered), (sharp, projected)):
+                copy = pltpu.make_async_copy(
+                    source.at[put, lanes], target.at[offset + j, :, lanes], sem.at[len(copies)]
+                )
+                copy.start()
+                copies.append(copy)
     for copy in copies:
         copy.wait()
 
@@ -344,7 +344,7 @@
         scratch_shapes=[
             pltpu.VMEM((count * rows, width), jnp.float32),
             pltpu.VMEM((count * rows, width), jnp.float32),
-            pltpu.SemaphoreType.DMA((2 * count,)),
+            pltpu.SemaphoreType.DMA((8 * count,)),
         ],
         input_output_aliases={len(args): 0, len(args) + 1: 1} if results else {},
         compiler_params=params(20),
@@ -425,9 +425,7 @@
     outer = rest[4:]
     halos = []
     for k in range(last):
-        halos.append(
-            (shifted(outer[2 * k], "gz", 1), shifted(outer[2 * k + 1], "gz", -1))
-        )
+        halos.append((shifted(outer[2 * k], "gz", 1), shifted(outer[2 * k + 1], "gz", -1)))
     tables = scales(row_count, width, columns, layers)
     for stage in range(1, last):
         sends = stage_sends(stage, conv, *halos[stage - 1])

time: 79.4 us -> 79.3 us (level)
  no operation moved by 1% of the time
where the time goes in v5:
time: 79.3 us; the launch traced here: 79.2 us
  waiting for transfers between devices  38.3 us (48%)
  starting transfers between devices  28.3 us (36%)
  Pallas kernels  11.6 us (15%)
  between operations  0.95 us (1%)
    ppermute x24, waiting for transfers between devices, shifted(): return lax.ppermute(block, axis, route)  38.3 us
    ppermute x24, starting transfers between devices, shifted(): return lax.ppermute(block, axis, route)  28.3 us
    pallas_call x4, Pallas kernels, finish(): pl.pallas_call(functools.partial(finish_kernel, stage, start), out_shape=...  7.87 us
    pallas_call x1, Pallas kernels, section(): pl.pallas_call(section_kernel, out_shape=shapes, in_specs=[pl.BlockSpec(m...  2.46 us
  transfers between devices with their start and end apart: 24, of which 10 were waited for; matrix products, arithmetic and copies ran while one was open for 0% of the time, Pallas kernels for 9%

profile of v5, /device:TPU:6, one launch (start us, length us, event | category | flops | bytes accessed | tf_op | source)
XLA Modules:
  0.0 79.2 jit_solution(3023740568706655487)
XLA Ops:
  0.6 2.5 %section.1 = (f32[32,128,256]{2,1,0:T(8,128)S(1)}, f32[2,128,256]{2,1,0:T(8,128)S(1)}, f32[2,128,256]{2,1,0:T(8,128)S(1)}, f32[2,128,256]{2,1,0:T(8,128)S(1)}, f...) custom-call(f32[32,128,256]{2,1,0:T(8,128)} %density.1, ...), custom_call_target="tpu_custom_call" | custom-call | flops 40000000 | bytes 8388608 | tf_op jit(solution)/shard_map/section/pallas_call | solution.py:158
  3.1 2.0 %collective-permute-start = (f32[2,128,256]{2,1,0:T(8,128)S(1)}, f32[2,128,256]{2,1,0:T(8,128)S(1)}, u32[]{:S(2)}, u32[]{:S(2)}) collective-permute-start(f32[2,128,256]{2,1,0:T(8,128)S(1)} %get-tuple-element.45), channel_id=1, source_target_pairs={{0,32},{32,64},{64,96},{96,128},{128,160},{160,192},{192,224},{224... | collective-permute-start | bytes 786440 | tf_op jit(solution)/shard_map/ppermute | solution.py:410
  5.1 4.0 %collective-permute-start.1 = (f32[2,128,256]{2,1,0:T(8,128)S(1)}, f32[2,128,256]{2,1,0:T(8,128)S(1)}, u32[]{:S(2)}, u32[]{:S(2)}) collective-permute-start(f32[2,128,256]{2,1,0:T(8,128)S(1)} %get-tuple-element.46), channel_id=1, source_target_pairs={{0,224},{32,0},{64,32},{96,64},{128,96},{160,128},{192,160},{224,1... | collective-permute-start | bytes 786440 | tf_op jit(solution)/shard_map/ppermute | solution.py:410
  9.1 3.2 %collective-permute-start.15 = (f32[2,128,256]{2,1,0:T(8,128)S(1)}, f32[2,128,256]{2,1,0:T(8,128)S(1)}, u32[]{:S(2)}, u32[]{:S(2)}) collective-permute-start(f32[2,128,256]{2,1,0:T(8,128)S(1)} %get-tuple-element.63), channel_id=1, source_target_pairs={{0,224},{32,0},{64,32},{96,64},{128,96},{160,128},{192,160},{224,1... | collective-permute-start | bytes 786440 | tf_op jit(solution)/shard_map/ppermute | solution.py:410
  12.4 3.8 %collective-permute-done.lower = f32[2,128,256]{2,1,0:T(8,128)S(1)} collective-permute-done((f32[2,128,256]{2,1,0:T(8,128)S(1)}, f32[2,128,256]{2,1,0:T(8,128)S(1)}, u32[]{:S(2)}, u32[]{:S(2)}) %collective-permute-start) | collective-permute-done | bytes 262176 | tf_op jit(solution)/shard_map/ppermute | solution.py:410
  16.2 2.0 %collective-permute-start.8 = (f32[2,128,256]{2,1,0:T(8,128)S(1)}, f32[2,128,256]{2,1,0:T(8,128)S(1)}, u32[]{:S(2)}, u32[]{:S(2)}) collective-permute-start(f32[2,128,256]{2,1,0:T(8,128)S(1)} %get-tuple-element.55), channel_id=1, source_target_pairs={{0,224},{32,0},{64,32},{96,64},{128,96},{160,128},{192,160},{224,1... | collective-permute-start | bytes 786440 | tf_op jit(solution)/shard_map/ppermute | solution.py:410
  18.2 0.5 collective-permute-start.19
  18.7 3.1 %collective-permute-done.14.lower = f32[2,128,256]{2,1,0:T(8,128)S(1)} collective-permute-done((f32[2,128,256]{2,1,0:T(8,128)S(1)}, f32[2,128,256]{2,1,0:T(8,128)S(1)}, u32[]{:S(2)}, u32[]{:S(2)}) %collective-permute-start.14) | collective-permute-done | bytes 262176 | tf_op jit(solution)/shard_map/ppermute | solution.py:410
  21.8 1.4 %collective-permute-start.20 = (f32[2,128,256]{2,1,0:T(8,128)S(1)}, f32[2,128,256]{2,1,0:T(8,128)S(1)}, u32[]{:S(2)}, u32[]{:S(2)}) collective-permute-start(f32[2,128,256]{2,1,0:T(8,128)S(1)} %get-tuple-element.70), channel_id=1, source_target_pairs={{0,16},{8,24},{16,0},{24,8},{1,17},{9,25},{17,1},{25,9},{2,18},{10... | collective-permute-start | bytes 786440 | tf_op jit(solution)/shard_map/ppermute | solution.py:410
  23.2 0.2 shard_map.45
  23.5 3.1 %collective-permute-done.7.lower = f32[2,128,256]{2,1,0:T(8,128)S(1)} collective-permute-done((f32[2,128,256]{2,1,0:T(8,128)S(1)}, f32[2,128,256]{2,1,0:T(8,128)S(1)}, u32[]{:S(2)}, u32[]{:S(2)}) %collective-permute-start.7) | collective-permute-done | bytes 262176 | tf_op jit(solution)/shard_map/ppermute | solution.py:410
  26.6 0.5 collective-permute-start.16
  27.2 2.9 %collective-permute-start.3 = (f32[8,8,256]{2,1,0:T(8,128)S(1)}, f32[8,8,256]{2,1,0:T(8,128)S(1)}, u32[]{:S(2)}, u32[]{:S(2)}) collective-permute-start(f32[8,8,256]{2,1,0:T(8,128)S(1)} %get-tuple-element.49), channel_id=1, source_target_pairs={{0,7},{1,0},{2,1},{3,2},{4,3},{5,4},{6,5},{7,6},{8,15},{9,8},{10,9... | collective-permute-start | bytes 196616 | tf_op jit(solution)/shard_map/ppermute | solution.py:410
  30.3 2.2 %collective-permute-done.20.refs_2_.refs_5_ = f32[2,128,256]{2,1,0:T(8,128)S(1)} collective-permute-done((f32[2,128,256]{2,1,0:T(8,128)S(1)}, f32[2,128,256]{2,1,0:T(8,128)S(1)}, u32[]{:S(2)}, u32[]{:S(2)}) %collective-permute-start.20) | collective-permute-done | bytes 262176 | tf_op jit(solution)/shard_map/ppermute | solution.py:410
  32.5 1.4 %collective-permute-start.17 = (f32[2,128,256]{2,1,0:T(8,128)S(1)}, f32[2,128,256]{2,1,0:T(8,128)S(1)}, u32[]{:S(2)}, u32[]{:S(2)}) collective-permute-start(f32[2,128,256]{2,1,0:T(8,128)S(1)} %get-tuple-element.66), channel_id=1, source_target_pairs={{0,16},{8,24},{16,0},{24,8},{1,17},{9,25},{17,1},{25,9},{2,18},{10... | collective-permute-start | bytes 786440 | tf_op jit(solution)/shard_map/ppermute | solution.py:410
  33.9 3.9 %collective-permute-done.21.refs_3_.refs_6_ = f32[2,128,256]{2,1,0:T(8,128)S(1)} collective-permute-done((f32[2,128,256]{2,1,0:T(8,128)S(1)}, f32[2,128,256]{2,1,0:T(8,128)S(1)}, u32[]{:S(2)}, u32[]{:S(2)}) %collective-permute-start.21) | collective-permute-done | bytes 262176 | tf_op jit(solution)/shard_map/ppermute | solution.py:410
  37.8 3.2 %collective-permute-start.9 = (f32[2,128,256]{2,1,0:T(8,128)S(1)}, f32[2,128,256]{2,1,0:T(8,128)S(1)}, u32[]{:S(2)}, u32[]{:S(2)}) collective-permute-start(f32[2,128,256]{2,1,0:T(8,128)S(1)} %get-tuple-element.57), channel_id=1, source_target_pairs={{0,8},{8,16},{16,24},{24,0},{1,9},{9,17},{17,25},{25,1},{2,10},{10... | collective-permute-start | bytes 786440 | tf_op jit(solution)/shard_map/ppermute | solution.py:410
  41.1 0.9 %collective-permute-start.11 = (f32[2,128,256]{2,1,0:T(8,128)S(1)}, f32[2,128,256]{2,1,0:T(8,128)S(1)}, u32[]{:S(2)}, u32[]{:S(2)}) collective-permute-start(f32[2,128,256]{2,1,0:T(8,128)S(1)} %get-tuple-element.59), channel_id=1, source_target_pairs={{0,24},{8,0},{16,8},{24,16},{1,25},{9,1},{17,9},{25,17},{2,26},{10... | collective-permute-start | bytes 786440 | tf_op jit(solution)/shard_map/ppermute | solution.py:410
  42.0 0.5 shard_map.42
  42.5 1.0 %collective-permute-done.17.refs_6_.refs_5_ = f32[2,128,256]{2,1,0:T(8,128)S(1)} collective-permute-done((f32[2,128,256]{2,1,0:T(8,128)S(1)}, f32[2,128,256]{2,1,0:T(8,128)S(1)}, u32[]{:S(2)}, u32[]{:S(2)}) %collective-permute-start.17) | collective-permute-done | bytes 262176 | tf_op jit(solution)/shard_map/ppermute | solution.py:410
  43.4 2.2 %collective-permute-start.4 = (f32[2,128,256]{2,1,0:T(8,128)S(1)}, f32[2,128,256]{2,1,0:T(8,128)S(1)}, u32[]{:S(2)}, u32[]{:S(2)}) collective-permute-start(f32[2,128,256]{2,1,0:T(8,128)S(1)} %get-tuple-element.51), channel_id=1, source_target_pairs={{0,8},{8,16},{16,24},{24,0},{1,9},{9,17},{17,25},{25,1},{2,10},{10... | collective-permute-start | bytes 786440 | tf_op jit(solution)/shard_map/ppermute | solution.py:410
  45.7 8.1 %collective-permute-done.18.refs_7_.refs_6_ = f32[2,128,256]{2,1,0:T(8,128)S(1)} collective-permute-done((f32[2,128,256]{2,1,0:T(8,128)S(1)}, f32[2,128,256]{2,1,0:T(8,128)S(1)}, u32[]{:S(2)}, u32[]{:S(2)}) %collective-permute-start.18) | collective-permute-done | bytes 262176 | tf_op jit(solution)/shard_map/ppermute | solution.py:410
  53.8 0.9 %collective-permute-done.10.refs_2_.refs_5_ = f32[2,128,256]{2,1,0:T(8,128)S(1)} collective-permute-done((f32[2,128,256]{2,1,0:T(8,128)S(1)}, f32[2,128,256]{2,1,0:T(8,128)S(1)}, u32[]{:S(2)}, u32[]{:S(2)}) %collective-permute-start.10) | collective-permute-done | bytes 262176 | tf_op jit(solution)/shard_map/ppermute | solution.py:410
  54.7 10.2 %collective-permute-done.11.refs_3_.refs_6_ = f32[2,128,256]{2,1,0:T(8,128)S(1)} collective-permute-done((f32[2,128,256]{2,1,0:T(8,128)S(1)}, f32[2,128,256]{2,1,0:T(8,128)S(1)}, u32[]{:S(2)}, u32[]{:S(2)}) %collective-permute-start.11) | collective-permute-done | bytes 262176 | tf_op jit(solution)/shard_map/ppermute | solution.py:410
  65.0 0.5 collective-permute-start.12
  65.5 2.0 %collective-permute-done.23.refs_8_ = f32[16,8,256]{2,1,0:T(8,128)S(1)} collective-permute-done((f32[16,8,256]{2,1,0:T(8,128)S(1)}, f32[16,8,256]{2,1,0:T(8,128)S(1)}, u32[]{:S(2)}, u32[]{:S(2)}) %collective-permute-start.23) | collective-permute-done | bytes 131104 | tf_op jit(solution)/shard_map/ppermute | solution.py:410
  67.5 3.4 %collective-permute-start.13 = (f32[8,8,256]{2,1,0:T(8,128)S(1)}, f32[8,8,256]{2,1,0:T(8,128)S(1)}, u32[]{:S(2)}, u32[]{:S(2)}) collective-permute-start(f32[8,8,256]{2,1,0:T(8,128)S(1)} %get-tuple-element.61), channel_id=1, source_target_pairs={{0,7},{1,0},{2,1},{3,2},{4,3},{5,4},{6,5},{7,6},{8,15},{9,8},{10,9... | collective-permute-start | bytes 196616 | tf_op jit(solution)/shard_map/ppermute | solution.py:410
  70.8 0.2 scales.1
  71.1 2.0 %shard_map.47 = (f32[8,128,1024]{2,1,0:T(8,128)}, f32[8,128,1024]{2,1,0:T(8,128)}) custom-call(f32[128,1024]{1,0:T(8,128)S(1)} %get-tuple-element.41.refs_0_, f32[8,256]{1,0:T(8,128)S(1)} %get-tuple-element.42.refs_1_, bf16[768,256]{1,0:T(8,128)(2,1)S(1)} %get-tuple-element.43.refs_2_, f32[2,128,256]{2,1,0:T(8,128)S(1)} %get-tuple-element.68.refs_0_.refs_3_, ...), custom_call_target="tpu_custom_call" | custom-call | flops 40000000 | bytes 8388608 | tf_op jit(solution)/shard_map/pallas_call | solution.py:339
  73.1 2.0 %shard_map.48 = (f32[8,128,1024]{2,1,0:T(8,128)}, f32[8,128,1024]{2,1,0:T(8,128)}) custom-call(f32[128,1024]{1,0:T(8,128)S(1)} %get-tuple-element.41.refs_0_, f32[8,256]{1,0:T(8,128)S(1)} %get-tuple-element.42.refs_1_, bf16[768,256]{1,0:T(8,128)(2,1)S(1)} %get-tuple-element.43.refs_2_, ...), custom_call_target="tpu_custom_call", output_to_operand_aliasing={{0}: (9, {}), {1}: (10, {})} | custom-call | flops 40000000 | bytes 8388608 | tf_op jit(solution)/shard_map/pallas_call | solution.py:339
  75.2 2.0 %shard_map.49 = (f32[8,128,1024]{2,1,0:T(8,128)}, f32[8,128,1024]{2,1,0:T(8,128)}) custom-call(f32[128,1024]{1,0:T(8,128)S(1)} %get-tuple-element.41.refs_0_, f32[8,256]{1,0:T(8,128)S(1)} %get-tuple-element.42.refs_1_, bf16[768,256]{1,0:T(8,128)(2,1)S(1)} %get-tuple-element.43.refs_2_, ...), custom_call_target="tpu_custom_call", output_to_operand_aliasing={{0}: (9, {}), {1}: (10, {})} | custom-call | flops 40000000 | bytes 8388608 | tf_op jit(solution)/shard_map/pallas_call | solution.py:339
  77.2 1.8 %shard_map.50 = (f32[8,128,1024]{2,1,0:T(8,128)}, f32[8,128,1024]{2,1,0:T(8,128)}) custom-call(f32[128,1024]{1,0:T(8,128)S(1)} %get-tuple-element.41.refs_0_, f32[8,256]{1,0:T(8,128)S(1)} %get-tuple-element.42.refs_1_, bf16[768,256]{1,0:T(8,128)(2,1)S(1)} %get-tuple-element.43.refs_2_, ...), custom_call_target="tpu_custom_call", output_to_operand_aliasing={{0}: (7, {}), {1}: (8, {})} | custom-call | flops 40000000 | bytes 8388608 | tf_op jit(solution)/shard_map/pallas_call | solution.py:339
  (28 shorter events, 0.4 us)
Async XLA Ops:
  3.1 13.1 %collective-permute-start = (f32[2,128,256]{2,1,0:T(8,128)S(1)}, f32[2,128,256]{2,1,0:T(8,128)S(1)}, u32[]{:S(2)}, u32[]{:S(2)}) collective-permute-start(f32[2,128,256]{2,1,0:T(8,128)S(1)} %get-tuple-element.45), channel_id=1, source_target_pairs={{0,32},{32,64},{64,96},{96,128},{128,160},{160,192},{192,224},{224... | collective-permute-start | bytes 786440 | tf_op jit(solution)/shard_map/ppermute | solution.py:410
  5.1 13.1 %collective-permute-start.1 = (f32[2,128,256]{2,1,0:T(8,128)S(1)}, f32[2,128,256]{2,1,0:T(8,128)S(1)}, u32[]{:S(2)}, u32[]{:S(2)}) collective-permute-start(f32[2,128,256]{2,1,0:T(8,128)S(1)} %get-tuple-element.46), channel_id=1, source_target_pairs={{0,224},{32,0},{64,32},{96,64},{128,96},{160,128},{192,160},{224,1... | collective-permute-start | bytes 786440 | tf_op jit(solution)/shard_map/ppermute | solution.py:410
  9.1 12.7 %collective-permute-start.14 = (f32[2,128,256]{2,1,0:T(8,128)S(1)}, f32[2,128,256]{2,1,0:T(8,128)S(1)}, u32[]{:S(2)}, u32[]{:S(2)}) collective-permute-start(f32[2,128,256]{2,1,0:T(8,128)S(1)} %get-tuple-element.62), channel_id=1, source_target_pairs={{0,32},{32,64},{64,96},{96,128},{128,160},{160,192},{192,224},{224... | collective-permute-start | bytes 786440 | tf_op jit(solution)/shard_map/ppermute | solution.py:410
  9.1 14.1 %collective-permute-start.15 = (f32[2,128,256]{2,1,0:T(8,128)S(1)}, f32[2,128,256]{2,1,0:T(8,128)S(1)}, u32[]{:S(2)}, u32[]{:S(2)}) collective-permute-start(f32[2,128,256]{2,1,0:T(8,128)S(1)} %get-tuple-element.63), channel_id=1, source_target_pairs={{0,224},{32,0},{64,32},{96,64},{128,96},{160,128},{192,160},{224,1... | collective-permute-start | bytes 786440 | tf_op jit(solution)/shard_map/ppermute | solution.py:410
  12.4 14.2 %collective-permute-start.7 = (f32[2,128,256]{2,1,0:T(8,128)S(1)}, f32[2,128,256]{2,1,0:T(8,128)S(1)}, u32[]{:S(2)}, u32[]{:S(2)}) collective-permute-start(f32[2,128,256]{2,1,0:T(8,128)S(1)} %get-tuple-element.54), channel_id=1, source_target_pairs={{0,32},{32,64},{64,96},{96,128},{128,160},{160,192},{192,224},{224... | collective-permute-start | bytes 786440 | tf_op jit(solution)/shard_map/ppermute | solution.py:410
  16.2 11.0 %collective-permute-start.8 = (f32[2,128,256]{2,1,0:T(8,128)S(1)}, f32[2,128,256]{2,1,0:T(8,128)S(1)}, u32[]{:S(2)}, u32[]{:S(2)}) collective-permute-start(f32[2,128,256]{2,1,0:T(8,128)S(1)} %get-tuple-element.55), channel_id=1, source_target_pairs={{0,224},{32,0},{64,32},{96,64},{128,96},{160,128},{192,160},{224,1... | collective-permute-start | bytes 786440 | tf_op jit(solution)/shard_map/ppermute | solution.py:410
  18.2 9.0 %collective-permute-start.19 = (f32[2,128,256]{2,1,0:T(8,128)S(1)}, f32[2,128,256]{2,1,0:T(8,128)S(1)}, u32[]{:S(2)}, u32[]{:S(2)}) collective-permute-start(f32[2,128,256]{2,1,0:T(8,128)S(1)} %get-tuple-element.69), channel_id=1, source_target_pairs={{0,8},{8,16},{16,24},{24,0},{1,9},{9,17},{17,25},{25,1},{2,10},{10... | collective-permute-start | bytes 786440 | tf_op jit(solution)/shard_map/ppermute | solution.py:410
  21.8 10.7 %collective-permute-start.20 = (f32[2,128,256]{2,1,0:T(8,128)S(1)}, f32[2,128,256]{2,1,0:T(8,128)S(1)}, u32[]{:S(2)}, u32[]{:S(2)}) collective-permute-start(f32[2,128,256]{2,1,0:T(8,128)S(1)} %get-tuple-element.70), channel_id=1, source_target_pairs={{0,16},{8,24},{16,0},{24,8},{1,17},{9,25},{17,1},{25,9},{2,18},{10... | collective-permute-start | bytes 786440 | tf_op jit(solution)/shard_map/ppermute | solution.py:410
  23.2 14.6 %collective-permute-start.21 = (f32[2,128,256]{2,1,0:T(8,128)S(1)}, f32[2,128,256]{2,1,0:T(8,128)S(1)}, u32[]{:S(2)}, u32[]{:S(2)}) collective-permute-start(f32[2,128,256]{2,1,0:T(8,128)S(1)} %get-tuple-element.71), channel_id=1, source_target_pairs={{0,24},{8,0},{16,8},{24,16},{1,25},{9,1},{17,9},{25,17},{2,26},{10... | collective-permute-start | bytes 786440 | tf_op jit(solution)/shard_map/ppermute | solution.py:410
  26.6 14.5 %collective-permute-start.16 = (f32[2,128,256]{2,1,0:T(8,128)S(1)}, f32[2,128,256]{2,1,0:T(8,128)S(1)}, u32[]{:S(2)}, u32[]{:S(2)}) collective-permute-start(f32[2,128,256]{2,1,0:T(8,128)S(1)} %get-tuple-element.65), channel_id=1, source_target_pairs={{0,8},{8,16},{16,24},{24,0},{1,9},{9,17},{17,25},{25,1},{2,10},{10... | collective-permute-start | bytes 786440 | tf_op jit(solution)/shard_map/ppermute | solution.py:410
  27.2 10.6 %collective-permute-start.2 = (f32[8,8,256]{2,1,0:T(8,128)S(1)}, f32[8,8,256]{2,1,0:T(8,128)S(1)}, u32[]{:S(2)}, u32[]{:S(2)}) collective-permute-start(f32[8,8,256]{2,1,0:T(8,128)S(1)} %get-tuple-element.48), channel_id=1, source_target_pairs={{0,1},{1,2},{2,3},{3,4},{4,5},{5,6},{6,7},{7,0},{8,9},{9,10},{10,1... | collective-permute-start | bytes 196616 | tf_op jit(solution)/shard_map/ppermute | solution.py:410
  27.2 13.8 %collective-permute-start.3 = (f32[8,8,256]{2,1,0:T(8,128)S(1)}, f32[8,8,256]{2,1,0:T(8,128)S(1)}, u32[]{:S(2)}, u32[]{:S(2)}) collective-permute-start(f32[8,8,256]{2,1,0:T(8,128)S(1)} %get-tuple-element.49), channel_id=1, source_target_pairs={{0,7},{1,0},{2,1},{3,2},{4,3},{5,4},{6,5},{7,6},{8,15},{9,8},{10,9... | collective-permute-start | bytes 196616 | tf_op jit(solution)/shard_map/ppermute | solution.py:410
  32.5 10.9 %collective-permute-start.17 = (f32[2,128,256]{2,1,0:T(8,128)S(1)}, f32[2,128,256]{2,1,0:T(8,128)S(1)}, u32[]{:S(2)}, u32[]{:S(2)}) collective-permute-start(f32[2,128,256]{2,1,0:T(8,128)S(1)} %get-tuple-element.66), channel_id=1, source_target_pairs={{0,16},{8,24},{16,0},{24,8},{1,17},{9,25},{17,1},{25,9},{2,18},{10... | collective-permute-start | bytes 786440 | tf_op jit(solution)/shard_map/ppermute | solution.py:410
  37.8 16.0 %collective-permute-start.18 = (f32[2,128,256]{2,1,0:T(8,128)S(1)}, f32[2,128,256]{2,1,0:T(8,128)S(1)}, u32[]{:S(2)}, u32[]{:S(2)}) collective-permute-start(f32[2,128,256]{2,1,0:T(8,128)S(1)} %get-tuple-element.67), channel_id=1, source_target_pairs={{0,24},{8,0},{16,8},{24,16},{1,25},{9,1},{17,9},{25,17},{2,26},{10... | collective-permute-start | bytes 786440 | tf_op jit(solution)/shard_map/ppermute | solution.py:410
  37.8 16.0 %collective-permute-start.9 = (f32[2,128,256]{2,1,0:T(8,128)S(1)}, f32[2,128,256]{2,1,0:T(8,128)S(1)}, u32[]{:S(2)}, u32[]{:S(2)}) collective-permute-start(f32[2,128,256]{2,1,0:T(8,128)S(1)} %get-tuple-element.57), channel_id=1, source_target_pairs={{0,8},{8,16},{16,24},{24,0},{1,9},{9,17},{17,25},{25,1},{2,10},{10... | collective-permute-start | bytes 786440 | tf_op jit(solution)/shard_map/ppermute | solution.py:410
  41.0 13.7 %collective-permute-start.10 = (f32[2,128,256]{2,1,0:T(8,128)S(1)}, f32[2,128,256]{2,1,0:T(8,128)S(1)}, u32[]{:S(2)}, u32[]{:S(2)}) collective-permute-start(f32[2,128,256]{2,1,0:T(8,128)S(1)} %get-tuple-element.58), channel_id=1, source_target_pairs={{0,16},{8,24},{16,0},{24,8},{1,17},{9,25},{17,1},{25,9},{2,18},{10... | collective-permute-start | bytes 786440 | tf_op jit(solution)/shard_map/ppermute | solution.py:410
  41.1 23.9 %collective-permute-start.11 = (f32[2,128,256]{2,1,0:T(8,128)S(1)}, f32[2,128,256]{2,1,0:T(8,128)S(1)}, u32[]{:S(2)}, u32[]{:S(2)}) collective-permute-start(f32[2,128,256]{2,1,0:T(8,128)S(1)} %get-tuple-element.59), channel_id=1, source_target_pairs={{0,24},{8,0},{16,8},{24,16},{1,25},{9,1},{17,9},{25,17},{2,26},{10... | collective-permute-start | bytes 786440 | tf_op jit(solution)/shard_map/ppermute | solution.py:410
  43.4 33.8 %collective-permute-start.4 = (f32[2,128,256]{2,1,0:T(8,128)S(1)}, f32[2,128,256]{2,1,0:T(8,128)S(1)}, u32[]{:S(2)}, u32[]{:S(2)}) collective-permute-start(f32[2,128,256]{2,1,0:T(8,128)S(1)} %get-tuple-element.51), channel_id=1, source_target_pairs={{0,8},{8,16},{16,24},{24,0},{1,9},{9,17},{17,25},{25,1},{2,10},{10... | collective-permute-start | bytes 786440 | tf_op jit(solution)/shard_map/ppermute | solution.py:410
  53.8 23.5 %collective-permute-start.5 = (f32[2,128,256]{2,1,0:T(8,128)S(1)}, f32[2,128,256]{2,1,0:T(8,128)S(1)}, u32[]{:S(2)}, u32[]{:S(2)}) collective-permute-start(f32[2,128,256]{2,1,0:T(8,128)S(1)} %get-tuple-element.52), channel_id=1, source_target_pairs={{0,16},{8,24},{16,0},{24,8},{1,17},{9,25},{17,1},{25,9},{2,18},{10... | collective-permute-start | bytes 786440 | tf_op jit(solution)/shard_map/ppermute | solution.py:410
  53.8 23.5 %collective-permute-start.6 = (f32[2,128,256]{2,1,0:T(8,128)S(1)}, f32[2,128,256]{2,1,0:T(8,128)S(1)}, u32[]{:S(2)}, u32[]{:S(2)}) collective-permute-start(f32[2,128,256]{2,1,0:T(8,128)S(1)} %get-tuple-element.53), channel_id=1, source_target_pairs={{0,24},{8,0},{16,8},{24,16},{1,25},{9,1},{17,9},{25,17},{2,26},{10... | collective-permute-start | bytes 786440 | tf_op jit(solution)/shard_map/ppermute | solution.py:410
  54.7 10.2 %collective-permute-start.22 = (f32[16,8,256]{2,1,0:T(8,128)S(1)}, f32[16,8,256]{2,1,0:T(8,128)S(1)}, u32[]{:S(2)}, u32[]{:S(2)}) collective-permute-start(f32[16,8,256]{2,1,0:T(8,128)S(1)} %get-tuple-element.72), channel_id=1, source_target_pairs={{0,1},{1,2},{2,3},{3,4},{4,5},{5,6},{6,7},{7,0},{8,9},{9,10},{10,1... | collective-permute-start | bytes 393224 | tf_op jit(solution)/shard_map/ppermute | solution.py:410
  64.9 2.5 %collective-permute-start.23 = (f32[16,8,256]{2,1,0:T(8,128)S(1)}, f32[16,8,256]{2,1,0:T(8,128)S(1)}, u32[]{:S(2)}, u32[]{:S(2)}) collective-permute-start(f32[16,8,256]{2,1,0:T(8,128)S(1)} %get-tuple-element.73), channel_id=1, source_target_pairs={{0,7},{1,0},{2,1},{3,2},{4,3},{5,4},{6,5},{7,6},{8,15},{9,8},{10,9... | collective-permute-start | bytes 393224 | tf_op jit(solution)/shard_map/ppermute | solution.py:410
  65.0 10.2 %collective-permute-start.12 = (f32[8,8,256]{2,1,0:T(8,128)S(1)}, f32[8,8,256]{2,1,0:T(8,128)S(1)}, u32[]{:S(2)}, u32[]{:S(2)}) collective-permute-start(f32[8,8,256]{2,1,0:T(8,128)S(1)} %get-tuple-element.60), channel_id=1, source_target_pairs={{0,1},{1,2},{2,3},{3,4},{4,5},{5,6},{6,7},{7,0},{8,9},{9,10},{10,1... | collective-permute-start | bytes 196616 | tf_op jit(solution)/shard_map/ppermute | solution.py:410
  67.5 7.7 %collective-permute-start.13 = (f32[8,8,256]{2,1,0:T(8,128)S(1)}, f32[8,8,256]{2,1,0:T(8,128)S(1)}, u32[]{:S(2)}, u32[]{:S(2)}) collective-permute-start(f32[8,8,256]{2,1,0:T(8,128)S(1)} %get-tuple-element.61), channel_id=1, source_target_pairs={{0,7},{1,0},{2,1},{3,2},{4,3},{5,4},{6,5},{7,6},{8,15},{9,8},{10,9... | collective-permute-start | bytes 196616 | tf_op jit(solution)/shard_map/ppermute | solution.py:410
